TPU v7x, 32 devices: a whole 2x2x4 slice. The times are simulated.
32 devices in a mesh: task: 16 (over z, x, core), tensor: 2 (over y).
Axes of the slice: x: 2, y: 2, z: 4, core: 2. Of those that a mesh axis runs over, the one named last changes fastest.
Arguments:
- inputs: bfloat16 [2048, 4096], P('task', 'tensor'), may hold values from -6 to 6
- targets: bfloat16 [2048, 4096], P('task', 'tensor'), may hold values from -6 to 6
- queries: bfloat16 [2048, 2048], P('task', 'tensor'), may hold values from -120 to 120
- key_rows: bfloat16 [2048, 2048], P('task', 'tensor'), may hold values from -4 to 4
- value_weight: bfloat16 [4096, 2048], P(None, 'tensor'), may hold values from -0.09375 to 0.09375
- output_weight: bfloat16 [2048, 4096], P('tensor'), may hold values from -0.125 to 0.125
- splits: int32 [16], P('task'), may hold values from 32 to 96
Outputs:
- meta_value: float32 [4096, 2048], P('task', 'tensor')
- meta_output: float32 [2048, 4096], P('tensor', 'task')
Inputs may be any that keep to these rules, and one draw needn't show every extreme that they name: `splits`: support and query parts of every task are both nonempty.
All inputs are finite; a program needn't handle non-finite values.
Results may differ from a plain program's by a relative error of at most 0.025.
Values may be sent and summed in bfloat16 or wider, within the bound.
No kernel may reach another device: no remote copies, remote signals or barrier semaphores. Data moves between devices by JAX's collectives and lax.ppermute only.
A program may use at most 128 MiB of HBM per device.

v0:
```python
import jax
import jax.numpy as jnp
from jax import lax
from jax.sharding import PartitionSpec as P

HD = 128
TASK_LEN = 128


step_rate = 0.25


def normed_rows(inputs):
    values = inputs.astype(jnp.float32)
    scale = lax.rsqrt(jnp.mean(values * values, axis=-1, keepdims=True) + 1e-05)
    return (values * scale).astype(jnp.bfloat16)


def attention_probs(queries, key_rows, heads):
    length = queries.shape[0]
    query_f = queries.astype(jnp.float32).reshape(length, heads, -1)
    key_f = key_rows.astype(jnp.float32).reshape(length, heads, -1)
    scores = jnp.einsum("ihd,jhd->hij", query_f, key_f) / jnp.sqrt(jnp.float32(query_f.shape[2]))
    position = jnp.arange(length)
    causal = position[:, None] >= position[None, :]
    scores = jnp.where(causal[None], scores, jnp.float32(-1e30))
    scores = scores - jnp.max(scores, axis=-1, keepdims=True)
    expo = jnp.exp(scores)
    return (expo / jnp.sum(expo, axis=-1, keepdims=True)).astype(jnp.bfloat16)


def local_out(value_mat, output_mat, normed, probs):
    heads = probs.shape[0]
    length = normed.shape[0]
    upper = jnp.dot(
        normed, value_mat.astype(jnp.bfloat16), preferred_element_type=jnp.float32
    ).astype(jnp.bfloat16)
    mixed = jnp.einsum(
        "hij,jhd->ihd",
        probs.astype(jnp.float32),
        upper.astype(jnp.float32).reshape(length, heads, -1),
    )
    mixed = mixed.reshape(length, -1).astype(jnp.bfloat16)
    return jnp.dot(
        mixed, output_mat.astype(jnp.bfloat16), preferred_element_type=jnp.float32
    ).astype(jnp.bfloat16)


def grads_of(value_mat, output_mat, error_term, normed, probs):

    def forward(value_arg, output_arg):
        return local_out(value_arg, output_arg, normed, probs)

    unused, pullback = jax.vjp(forward, value_mat, output_mat)
    return pullback(error_term.astype(jnp.bfloat16))


def combine(term, offset, weight):
    share = lax.psum_scatter(
        term.astype(jnp.bfloat16), "tensor", scatter_dimension=1, tiled=True
    ).astype(jnp.float32)
    return lax.all_gather(
        (weight * (share + offset)).astype(jnp.bfloat16), "tensor", axis=1, tiled=True
    )


def per_device(inputs, targets, queries, key_rows, value_weight, output_weight, splits):
    value_start = value_weight.astype(jnp.float32)
    output_start = output_weight.astype(jnp.float32)
    heads_here = queries.shape[1] // HD
    full_inputs = lax.all_gather(inputs, "tensor", axis=1, tiled=True)
    offset_all = inputs.astype(jnp.float32) - targets.astype(jnp.float32)
    normed_all = normed_rows(full_inputs)
    position = jnp.arange(TASK_LEN)
    total_value = None
    total_output = None
    probs = attention_probs(queries, key_rows, heads_here)
    split = splits[0]
    count_s = split.astype(jnp.float32)
    support = (position < split).astype(jnp.float32)[:, None]
    support_weight = support / count_s
    query_weight = (1.0 - support) / (jnp.float32(TASK_LEN) - count_s)
    part = local_out(value_start, output_start, normed_all, probs)
    error_term = combine(part.astype(jnp.float32), offset_all, support_weight)
    grad_value, grad_output = grads_of(value_start, output_start, error_term, normed_all, probs)
    value_next = value_start - step_rate * grad_value
    output_next = output_start - step_rate * grad_output
    saved_states = [(value_start, output_start, error_term)]
    part_final = local_out(value_next, output_next, normed_all, probs)
    query_term = combine(part_final.astype(jnp.float32), offset_all, query_weight)
    direct_value, direct_output = grads_of(value_next, output_next, query_term, normed_all, probs)
    extra_value = jnp.zeros_like(direct_value)
    extra_output = jnp.zeros_like(direct_output)
    for saved in reversed(saved_states):

        def gradient_map(value_arg, output_arg, error_arg):
            return grads_of(value_arg, output_arg, error_arg, normed_all, probs)

        unused, pull_grads = jax.vjp(gradient_map, saved[0], saved[1], saved[2].astype(jnp.float32))
        second_value, second_output, error_back = pull_grads(
            (-step_rate * direct_value, -step_rate * direct_output)
        )
        out_back = combine(error_back, 0.0, support_weight)

        def forward_map(value_arg, output_arg):
            return local_out(value_arg, output_arg, normed_all, probs)

        unused_out, pull_out = jax.vjp(forward_map, saved[0], saved[1])
        first_value, first_output = pull_out(out_back)
        extra_value = second_value + first_value
        extra_output = second_output + first_output
    total_value = direct_value + extra_value
    total_output = direct_output + extra_output
    total_value, total_output = (
        lax.psum_scatter(
            total_value.astype(jnp.bfloat16), "task", scatter_dimension=0, tiled=True
        ).astype(jnp.float32),
        lax.psum_scatter(
            total_output.astype(jnp.bfloat16), "task", scatter_dimension=1, tiled=True
        ).astype(jnp.float32),
    )
    return (total_value, total_output)


def solution(mesh):
    return jax.shard_map(
        per_device,
        mesh=mesh,
        in_specs=(
            P("task", "tensor"),
            P("task", "tensor"),
            P("task", "tensor"),
            P("task", "tensor"),
            P(None, "tensor"),
            P("tensor", None),
            P("task"),
        ),
        out_specs=(P("task", "tensor"), P("tensor", "task")),
        check_vma=False,
    )
```

profile of v0, /device:TPU:0, one launch (start us, length us, event | category | flops | bytes accessed | tf_op | source)
XLA Modules:
  0.0 465.0 jit_solution(15424022318885126670)
XLA Ops:
  9.5 24.1 %all-gather.5.cloned.1.call-done = bf16[128,4096]{1,0:T(8,128)(2,1)} async-done(((bf16[128,2048]{1,0:T(8,128)(2,1)}), bf16[128,4096]{1,0:T(8,128)(2,1)}) %all-gather.5.cloned.1.call-update) | async-done | bytes 1048592 | tf_op jit(solution)/shard_map/all_gather | solution.py:71
  35.1 5.0 %convolution_convert_fusion.14 = bf16[128,1024]{1,0:T(8,128)(2,1)S(1)} fusion(bf16[4096,1024]{1,0:T(8,128)(2,1)} %param.11, bf16[128,4096]{1,0:T(8,128)(2,1)} %all-gather.5.cloned.1.call-done, f32[128]{0:T(128)S(1)} %add_rsqrt_fusion), kind=kOutput, calls=%fused_computation.46 | convolution fusion | flops 1075445760 | bytes 9699840 | tf_op jit(solution)/shard_map/dot_general | solution.py:35
  40.6 5.6 %convolution_convert_fusion.3 = bf16[128,4096]{1,0:T(8,128)(2,1)} fusion(bf16[128,1024]{0,1:T(8,128)(2,1)S(1)} %bitcast.105, bf16[1024,4096]{1,0:T(8,128)(2,1)} %param.12), kind=kOutput, calls=%fused_computation.24 | convolution fusion | flops 1074266112 | bytes 9699328 | tf_op jit(solution)/shard_map/dot_general | solution.py:44
  47.1 19.7 %reduce-scatter.6.cloned.1.call-done = bf16[128,2048]{1,0:T(8,128)(2,1)} async-done(((bf16[128,4096]{1,0:T(8,128)(2,1)}), bf16[128,2048]{1,0:T(8,128)(2,1)}) %reduce-scatter.6.cloned.1.call-update) | async-done | bytes 524304 | tf_op jit(solution)/shard_map/reduce_scatter | solution.py:59
  69.1 21.2 %all-gather.7.cloned.1.call-done = bf16[128,4096]{1,0:T(8,128)(2,1)} async-done(((bf16[128,2048]{1,0:T(8,128)(2,1)}), bf16[128,4096]{1,0:T(8,128)(2,1)}) %all-gather.7.cloned.1.call-update) | async-done | bytes 1048592 | tf_op jit(solution)/shard_map/all_gather | solution.py:62
  90.3 6.6 %convolution_convert_fusion.12 = bf16[128,1024]{1,0:T(8,128)(2,1)S(1)} fusion(bf16[128,4096]{1,0:T(8,128)(2,1)} %all-gather.7.cloned.1.call-done, bf16[1024,4096]{1,0:T(8,128)(2,1)} %param.12), kind=kOutput, calls=%fused_computation.44 | convolution fusion | flops 1073872896 | bytes 9699328 | tf_op jit(solution)/shard_map/transpose(jvp())/dot_general | solution.py:44
  97.4 8.0 %fusion.34 = bf16[128,1024]{1,0:T(8,128)(2,1)} fusion(bf16[4096,1024]{1,0:T(8,128)(2,1)} %param.11, bf16[128,1024]{0,1:T(8,128)(2,1)S(1)} %bitcast.123, bf16[128,4096]{1,0:T(8,128)(2,1)S(1)} %copy-done.5, f32[128]{0:T(128)S(1)} %add_rsqrt_fusion), kind=kOutput, calls=%fused_computation.35 | convolution fusion | flops 2175926272 | bytes 9961984 | tf_op jit(solution)/shard_map/dot_general | solution.py:35
  108.4 4.7 %subtract_convert_fusion = bf16[1024,4096]{1,0:T(8,128)(2,1)S(1)} fusion(bf16[1024,4096]{1,0:T(8,128)(2,1)} %param.12, bf16[128,1024]{0,1:T(8,128)(2,1)S(1)} %bitcast.106, bf16[128,4096]{1,0:T(8,128)(2,1)S(1)} %copy-done.6), kind=kOutput, calls=%fused_computation.9 | convolution fusion | flops 1098907648 | bytes 18087936 | tf_op jit(solution)/shard_map/transpose(jvp())/dot_general | solution.py:44
  113.2 3.2 copy-done.2
  118.8 20.5 %reduce-scatter.8.cloned.1.call-done = bf16[128,2048]{1,0:T(8,128)(2,1)} async-done(((bf16[128,4096]{1,0:T(8,128)(2,1)}), bf16[128,2048]{1,0:T(8,128)(2,1)}) %reduce-scatter.8.cloned.1.call-update) | async-done | bytes 524304 | tf_op jit(solution)/shard_map/reduce_scatter | solution.py:59
  141.8 21.2 %all-gather.9.cloned.1.call-done = bf16[128,4096]{1,0:T(8,128)(2,1)} async-done(((bf16[128,2048]{1,0:T(8,128)(2,1)}), bf16[128,4096]{1,0:T(8,128)(2,1)}) %all-gather.9.cloned.1.call-update) | async-done | bytes 1048592 | tf_op jit(solution)/shard_map/all_gather | solution.py:62
  163.0 6.6 %convolution_convert_fusion.9 = bf16[128,1024]{1,0:T(8,128)(2,1)S(1)} fusion(bf16[128,4096]{1,0:T(8,128)(2,1)} %all-gather.9.cloned.1.call-done, bf16[1024,4096]{1,0:T(8,128)(2,1)} %copy-done.2), kind=kOutput, calls=%fused_computation.41 | convolution fusion | flops 1073872896 | bytes 9699328 | tf_op jit(solution)/shard_map/transpose(jvp())/dot_general | solution.py:44
  172.5 3.2 copy-done.4
  178.0 4.7 %fusion.58 = f32[128,4096]{1,0:T(8,128)S(1)} fusion(bf16[128,1024]{0,1:T(8,128)(2,1)S(1)} %bitcast.111, bf16[1024,4096]{1,0:T(8,128)(2,1)} %param.12), kind=kOutput, calls=%fused_computation.68 | convolution fusion | flops 1073741824 | bytes 10747904 | tf_op jit(solution)/shard_map/transpose(jvp(transpose(jvp())))/dot_general | solution.py:44
  185.1 3.2 copy-done.3
  191.2 20.5 %reduce-scatter.10.cloned.1.call-done = bf16[128,2048]{1,0:T(8,128)(2,1)} async-done(((bf16[128,4096]{1,0:T(8,128)(2,1)}), bf16[128,2048]{1,0:T(8,128)(2,1)}) %reduce-scatter.10.cloned.1.call-update) | async-done | bytes 524304 | tf_op jit(solution)/shard_map/reduce_scatter | solution.py:59
  214.0 5.6 %fusion.59 = bf16[1024,4096]{1,0:T(8,128)(2,1)} fusion(bf16[128,1024]{0,1:T(8,128)(2,1)S(1)} %bitcast.112, bf16[128,4096]{1,0:T(8,128)(2,1)S(1)} %copy-done.6), kind=kOutput, calls=%fused_computation.69 | convolution fusion | flops 1073741824 | bytes 9699328 | tf_op jit(solution)/shard_map/transpose(jvp(transpose(jvp())))/dot_general | solution.py:44
  219.6 15.6 %all-gather.11.cloned.1.call-done = bf16[128,4096]{1,0:T(8,128)(2,1)} async-done(((bf16[128,2048]{1,0:T(8,128)(2,1)}), bf16[128,4096]{1,0:T(8,128)(2,1)}) %all-gather.11.cloned.1.call-update) | async-done | bytes 1048592 | tf_op jit(solution)/shard_map/all_gather | solution.py:62
  235.2 9.7 %fusion.4 = bf16[1024,4096]{1,0:T(8,128)(2,1)} fusion(bf16[1024,4096]{1,0:T(8,128)(2,1)} %copy-done.3, bf16[1024,4096]{1,0:T(8,128)(2,1)} %fusion.59, bf16[128,1024]{0,1:T(8,128)(2,1)S(1)} %bitcast.108, bf16[128,4096]{1,0:T(8,128)(2,1)} %all-gather.11.cloned.1.call-done), kind=kOutput, calls=%fused_computation.8 | convolution fusion | flops 1103101952 | bytes 26476544 | tf_op jit(solution)/shard_map/transpose(jvp())/dot_general | solution.py:44
  245.0 6.3 %fusion.28 = bf16[128,1024]{1,0:T(8,128)(2,1)S(1)} fusion(bf16[128,4096]{1,0:T(8,128)(2,1)S(1)} %copy-done.6, bf16[1024,4096]{1,0:T(8,128)(2,1)} %copy-done.3), kind=kOutput, calls=%fused_computation.33 | convolution fusion | flops 1086455808 | bytes 9699328 | tf_op jit(solution)/shard_map/transpose(jvp(transpose(jvp())))/dot_general | solution.py:44
  251.8 6.6 %fusion.46 = bf16[4096,1024]{1,0:T(8,128)(2,1)} fusion(bf16[128,1024]{0,1:T(8,128)(2,1)S(1)} %bitcast.115, bf16[128,4096]{1,0:T(8,128)(2,1)S(1)} %copy-done.5, f32[128]{0:T(128)S(1)} %add_rsqrt_fusion), kind=kOutput, calls=%fused_computation.66 | convolution fusion | flops 1075314688 | bytes 9699840 | tf_op jit(solution)/shard_map/transpose(jvp(jvp()))/dot_general | solution.py:35
  261.8 11.2 %fusion.2 = bf16[4096,1024]{1,0:T(8,128)(2,1)} fusion(bf16[4096,1024]{1,0:T(8,128)(2,1)} %copy-done.4, bf16[4096,1024]{1,0:T(8,128)(2,1)} %fusion.46, bf16[128,1024]{0,1:T(8,128)(2,1)S(1)} %bitcast.113, bf16[128,4096]{1,0:T(8,128)(2,1)S(1)} %copy-done.5, f32[128]{0:T(128)S(1)} %add_rsqrt_fusion), kind=kOutput, calls=%fused_computation.6 | convolution fusion | flops 1104674816 | bytes 26477056 | tf_op jit(solution)/shard_map/transpose(jvp())/dot_general | solution.py:35
  273.0 75.7 %reduce-scatter.14.cloned.1.call-done = bf16[1024,256]{1,0:T(8,128)(2,1)} async-done(((bf16[1024,4096]{1,0:T(8,128)(2,1)}), bf16[1024,256]{1,0:T(8,128)(2,1)}) %reduce-scatter.14.cloned.1.call-update) | async-done | bytes 524304 | tf_op jit(solution)/shard_map/reduce_scatter | solution.py:118
  350.8 105.1 %reduce-scatter.12.cloned.1.call-done = bf16[256,1024]{1,0:T(8,128)(2,1)} async-done(((bf16[4096,1024]{1,0:T(8,128)(2,1)}), bf16[256,1024]{1,0:T(8,128)(2,1)}) %reduce-scatter.12.cloned.1.call-update) | async-done | bytes 524304 | tf_op jit(solution)/shard_map/reduce_scatter | solution.py:115
  (74 shorter events, 35.7 us)
Async XLA Ops:
  7.2 1.0 copy-start
  7.2 26.4 %all-gather.5.cloned.1.call-start = ((), (), s32[]{:S(2)}) async-start(), calls=%async_computation.5 | async-start | bytes 1572864 | tf_op jit(solution)/shard_map/all_gather | solution.py:71
  7.9 58.8 %reduce-scatter.6.cloned.1.call-start = ((), (), s32[]{:S(2)}) async-start(), calls=%async_computation.6 | async-start | bytes 1572864 | tf_op jit(solution)/shard_map/reduce_scatter | solution.py:59
  40.1 26.6 %copy-start.7 = (bf16[128,2048]{1,0:T(8,128)(2,1)S(1)}, bf16[128,2048]{1,0:T(8,128)(2,1)}, u32[]{:S(2)}) copy-start(bf16[128,2048]{1,0:T(8,128)(2,1)} %param.7) | copy-start | bytes 1572868
  40.1 26.6 %copy-start.10 = (bf16[128,2048]{1,0:T(8,128)(2,1)S(1)}, bf16[128,2048]{1,0:T(8,128)(2,1)}, u32[]{:S(2)}) copy-start(bf16[128,2048]{1,0:T(8,128)(2,1)} %param.8) | copy-start | bytes 1572868
  46.2 51.2 %copy-start.5 = (bf16[128,4096]{1,0:T(8,128)(2,1)S(1)}, bf16[128,4096]{1,0:T(8,128)(2,1)}, u32[]{:S(2)}) copy-start(bf16[128,4096]{1,0:T(8,128)(2,1)} %all-gather.5.cloned.1.call-done) | copy-start | bytes 3145732
  46.2 44.1 %all-gather.7.cloned.1.call-start = ((), (), s32[]{:S(2)}) async-start(), calls=%async_computation.7 | async-start | bytes 1572864 | tf_op jit(solution)/shard_map/all_gather | solution.py:62
  68.9 70.4 %reduce-scatter.8.cloned.1.call-start = ((), (), s32[]{:S(2)}) async-start(), calls=%async_computation.8 | async-start | bytes 1572864 | tf_op jit(solution)/shard_map/reduce_scatter | solution.py:59
  97.4 11.0 %copy-start.6 = (bf16[128,4096]{1,0:T(8,128)(2,1)S(1)}, bf16[128,4096]{1,0:T(8,128)(2,1)}, u32[]{:S(2)}) copy-start(bf16[128,4096]{1,0:T(8,128)(2,1)} %all-gather.7.cloned.1.call-done) | copy-start | bytes 3145732
  113.2 3.2 copy-start.2
  118.7 44.2 %all-gather.9.cloned.1.call-start = ((), (), s32[]{:S(2)}) async-start(), calls=%async_computation.9 | async-start | bytes 1572864 | tf_op jit(solution)/shard_map/all_gather | solution.py:62
  141.5 70.2 %reduce-scatter.10.cloned.1.call-start = ((), (), s32[]{:S(2)}) async-start(), calls=%async_computation.10 | async-start | bytes 1572864 | tf_op jit(solution)/shard_map/reduce_scatter | solution.py:59
  172.5 3.2 copy-start.4
  177.8 5.0 %copy-start.9 = (bf16[128,4096]{1,0:T(8,128)(2,1)S(1)}, bf16[128,4096]{1,0:T(8,128)(2,1)}, u32[]{:S(2)}) copy-start(bf16[128,4096]{1,0:T(8,128)(2,1)} %all-gather.9.cloned.1.call-done) | copy-start | bytes 3145732
  185.1 3.2 copy-start.3
  191.2 44.0 %all-gather.11.cloned.1.call-start = ((), (), s32[]{:S(2)}) async-start(), calls=%async_computation.11 | async-start | bytes 1572864 | tf_op jit(solution)/shard_map/all_gather | solution.py:62
  213.7 134.9 %reduce-scatter.14.cloned.1.call-start = ((), (), s32[]{:S(2)}) async-start(), calls=%async_computation.13 | async-start | bytes 8912896 | tf_op jit(solution)/shard_map/reduce_scatter | solution.py:118
  244.9 210.9 %reduce-scatter.12.cloned.1.call-start = ((), (), s32[]{:S(2)}) async-start(), calls=%async_computation.12 | async-start | bytes 8912896 | tf_op jit(solution)/shard_map/reduce_scatter | solution.py:115
  251.3 7.1 %copy-start.8 = (bf16[128,4096]{1,0:T(8,128)(2,1)S(1)}, bf16[128,4096]{1,0:T(8,128)(2,1)}, u32[]{:S(2)}) copy-start(bf16[128,4096]{1,0:T(8,128)(2,1)} %all-gather.11.cloned.1.call-done) | copy-start | bytes 3145732
  251.5 6.9 %slice-start = ((s8[8388608]{0:T(1024)(128)(4,1)}), s8[4194304]{0:T(1024)(128)(4,1)S(1)}, s32[]{:S(2)}) async-start(s8[8388608]{0:T(1024)(128)(4,1)} %bitcast.103), calls=%async_computation.14 | async-start | bytes 8388608
  251.8 6.6 %slice-start.1 = ((s8[8388608]{0:T(1024)(128)(4,1)}), s8[4194304]{0:T(1024)(128)(4,1)S(1)}, s32[]{:S(2)}) async-start(s8[8388608]{0:T(1024)(128)(4,1)} %bitcast.103), calls=%async_computation.15 | async-start | bytes 8388608
  261.8 196.2 %copy-start.1 = (bf16[128,1024]{1,0:T(8,128)(2,1)S(1)}, bf16[128,1024]{1,0:T(8,128)(2,1)}, u32[]{:S(2)}) copy-start(bf16[128,1024]{1,0:T(8,128)(2,1)} %param.10) | copy-start | bytes 786436
Sparse Core Ops, SparseCore 0:
  9.5 23.9 all-gather.4
  46.3 20.3 reduce-scatter.5
  69.0 21.2 all-gather.6
  118.8 20.3 reduce-scatter.7
  141.6 21.2 all-gather.8
  191.3 20.3 reduce-scatter.9
  213.9 21.2 all-gather.10
  245.1 103.5 reduce-scatter.13
  352.7 103.0 reduce-scatter.11
where the time goes:
time: 469 us; the launch traced here: 465 us
  waiting for transfers between devices  324 us (69%)
  matrix products  99.5 us (21%)
  between operations  15.4 us (3%)
  local copies, waits for them, and re-layouts  12.7 us (3%)
  other arithmetic  12.2 us (3%)
    reduce_scatter x1, waiting for transfers between devices, per_device(): lax.psum_scatter(total_value.astype(jnp.bfloat16), 'task', scatter_dimens...  105 us
    reduce_scatter x1, waiting for transfers between devices, per_device(): lax.psum_scatter(total_output.astype(jnp.bfloat16), 'task', scatter_dimen...  75.7 us
    reduce_scatter x3, waiting for transfers between devices, combine(): lax.psum_scatter(term.astype(jnp.bfloat16), 'tensor', scatter_dimension=1...  60.7 us
    dot_general x12, matrix products, local_out(): jnp.dot(mixed, output_mat.astype(jnp.bfloat16), preferred_element_type=jn...  60.3 us
    all_gather x3, waiting for transfers between devices, combine(): lax.all_gather((weight * (share + offset)).astype(jnp.bfloat16), 'tensor'...  58 us
    dot_general x6, matrix products, local_out(): jnp.dot(normed, value_mat.astype(jnp.bfloat16), preferred_element_type=jn...  35.1 us
    all_gather x1, waiting for transfers between devices, per_device(): full_inputs = lax.all_gather(inputs, 'tensor', axis=1, tiled=True)  24.1 us
    unnamed x26, local copies, waits for them, and re-layouts  9.88 us
  transfers between devices with their start and end apart: 9, of which 9 were waited for; matrix products, arithmetic and copies ran while one was open for 8% of the time, Pallas kernels for 0%

commit v1 on v0

v1 whole, which is shorter than its diff:
```python
import functools

import jax
import jax.numpy as jnp
from jax import lax
from jax.experimental import pallas as pl
from jax.experimental.pallas import tpu as pltpu
from jax.sharding import PartitionSpec as P


HD = 128
RATE = 0.25
CORES = 2
PAIRS = 2
CHUNKS = 4
VMEM_LIMIT = 16 * 1024 * 1024


f32 = jnp.float32
bf16 = jnp.bfloat16
Shape = jax.ShapeDtypeStruct


def dot_nn(a, b):
    return lax.dot_general(a, b, (((1,), (0,)), ((), ())), preferred_element_type=f32)


def dot_nt(a, b):
    return lax.dot_general(a, b, (((1,), (1,)), ((), ())), preferred_element_type=f32)


def dot_tn(a, b):
    return lax.dot_general(a, b, (((0,), (0,)), ((), ())), preferred_element_type=f32)


def split_dot(dot, small, big):
    upper = small.astype(bf16)
    lower = (small - upper.astype(f32)).astype(bf16)
    return dot(upper, big) + dot(lower, big)


def by_head(dot, probs_ref, value):
    return jnp.concatenate(
        [dot(probs_ref[h], value[:, h * HD : (h + 1) * HD]) for h in range(probs_ref.shape[0])],
        axis=1,
    )


def call(kernel, out_shape, **kwargs):
    return pl.pallas_call(
        kernel,
        out_shape=out_shape,
        compiler_params=pltpu.CompilerParams(vmem_limit_bytes=VMEM_LIMIT),
        **kwargs,
    )


def whole(array):
    return pl.BlockSpec(array.shape, lambda *unused: (0,) * len(array.shape))


def probs_kernel(split_ref, query_ref, key_ref, out_ref, support_ref, asked_ref):
    heads, length, _ = out_ref.shape
    inside = lax.broadcasted_iota(jnp.int32, (length, 1), 0) < split_ref[0]
    count = split_ref[0].astype(f32)
    support_ref[...] = jnp.where(inside, 1.0, 0.0) / count
    asked_ref[...] = jnp.where(inside, 0.0, 1.0) / (f32(length) - count)
    row = lax.broadcasted_iota(jnp.int32, (length, length), 0)
    col = lax.broadcasted_iota(jnp.int32, (length, length), 1)
    for h in range(heads):
        cols = slice(h * HD, (h + 1) * HD)
        scores = dot_nt(query_ref[:, cols], key_ref[:, cols]) / jnp.sqrt(f32(HD))
        scores = jnp.where(row >= col, scores, f32(-1e30))
        expo = jnp.exp(scores - jnp.max(scores, axis=-1, keepdims=True))
        out_ref[h] = (expo / jnp.sum(expo, axis=-1, keepdims=True)).astype(bf16)


def piece_kernel(place_ref, x_ref, weight_ref, acc_ref, old_ref, out_ref, square_ref):
    @pl.when(pl.program_id(0) == 0)
    def _():
        square_ref[...] = old_ref[...] + row_squares(x_ref[...])

    out_ref[...] = acc_ref[...] + dot_nn(x_ref[...], weight_ref[...])


def row_squares(value):
    value = value.astype(f32)
    return jnp.sum(value * value, axis=-1, keepdims=True)


def first_piece_kernel(place_ref, x_ref, weight_ref, out_ref, square_ref):
    @pl.when(pl.program_id(0) == 0)
    def _():
        square_ref[...] = row_squares(x_ref[...])

    out_ref[...] = dot_nn(x_ref[...], weight_ref[...])


def upper_kernel(wide, place_ref, x_ref, weight_ref, acc_ref, square_ref, probs_ref, upper_ref, mixed_ref, scale_ref, keep_ref):
    @pl.when(pl.program_id(0) == 0)
    def _():
        square = square_ref[...] + row_squares(x_ref[...])
        scale = lax.rsqrt(square / wide + 1e-05)
        keep_ref[...] = scale
        scale_ref[...] = scale

    upper = keep_ref[...] * (acc_ref[...] + dot_nn(x_ref[...], weight_ref[...]))
    upper = upper.astype(bf16)
    upper_ref[...] = upper
    mixed_ref[...] = by_head(dot_nn, probs_ref, upper).astype(bf16)


def gram_kernel(pieces, group_ref, scale_ref, *refs):
    x_refs, (normed_ref, gram_ref) = refs[:pieces], refs[pieces:]
    count, _, step = normed_ref.shape
    span = count // pieces
    scale = scale_ref[...]
    group = group_ref[0]
    gram = None
    for shift in range(pieces):
        normed = (x_refs[shift][...].astype(f32) * scale).astype(bf16)
        term = dot_nt(normed, normed)
        gram = term if gram is None else gram + term
        start = lax.rem(group + pieces - shift, pieces) * span
        for m in range(span):
            normed_ref[start + m] = normed[:, m * step : (m + 1) * step]
    gram_ref[...] = gram


def part_kernel(cross, offset, *refs):
    refs = list(refs)
    take = lambda n: [refs.pop(0) for _ in range(n)]
    left_ref, weight_ref = take(2)
    part = dot_nn(left_ref[...], weight_ref[...])
    if cross is not None:
        cross_ref, error_ref = take(2)
        part = part + cross(cross_ref[...], error_ref[0])
    if offset is not None:
        rows, piece = offset
        group_ref, x_ref, t_ref = take(3)
        gap = x_ref[rows].astype(f32) - t_ref[rows].astype(f32)
        part = part + jnp.where(group_ref[0] == piece, gap, 0.0)
    refs[0][...] = part.astype(bf16)


def finish_kernel(rows, others, matched, merged, chained, filled, tail, n_tail, *refs):
    refs = list(refs)
    take = lambda n: [refs.pop(0) for _ in range(n)]
    part_ref, weight_ref, scale_ref = take(3)
    other_refs = take(others)
    match_in = take(1) if matched else []
    merge_in = take(1) if merged else []
    chain_in = take(2 if matched else 1) if chained else []
    take(1 if filled else 0)
    tail_in = take(n_tail)
    error_ref = take(1)[0]
    if tail is None:
        acc_ref = take(1)[0]
        match_ref = take(1)[0] if matched else None
        tail_out = []
    else:
        n_scratch = 2 if matched else 1
        tail_out = take(len(refs) - n_scratch)
        acc_ref = take(1)[0]
        match_ref = take(1)[0] if matched else None

    total = part_ref[...].astype(f32)
    for other in other_refs:
        total = total + other[...].astype(f32)
    scale = scale_ref[...]
    scaled = scale[rows] * total
    error = scaled.astype(bf16)
    if merged:
        query = merge_in[0][0].astype(f32)
        length, cols = scale.shape[0], query.shape[1]
        gap = jnp.zeros((length - query.shape[0], cols), f32)
        error_ref[0] = jnp.where(
            scale > 0.0, jnp.concatenate([scaled, gap], axis=0), jnp.concatenate([gap, query], axis=0)
        ).astype(bf16)
    else:
        error_ref[0] = error
    acc = dot_nt(error, weight_ref[...])
    match = dot_nt(error, match_in[0][0]) if matched else None
    first = pl.program_id(0) == 0

    @pl.when(first)
    def _():
        acc_ref[...] = acc + chain_in[0][...] if chained else acc
        if matched:
            match_ref[...] = match + chain_in[1][...] if chained else match

    @pl.when(jnp.logical_not(first))
    def _():
        acc_ref[...] += acc
        if matched:
            match_ref[...] += match

    if tail is not None:
        @pl.when(pl.program_id(0) == pl.num_programs(0) - 1)
        def _():
            if matched:
                tail(acc_ref[...], match_ref[...], *tail_in, *tail_out)
            else:
                tail(acc_ref[...], *tail_in, *tail_out)


def step_tail(low, high, acc, probs_ref, gram_ref, upper_ref, mixed_ref, support_ref, next_ref, query_ref, left_ref, cross_ref):
    length, width = upper_ref.shape
    grad_mixed = jnp.concatenate([acc.astype(bf16), jnp.zeros((length - high, width), bf16)], axis=0)
    grad_upper = by_head(dot_tn, probs_ref, grad_mixed).astype(bf16)
    upper = upper_ref[...].astype(f32) - RATE * split_dot(dot_nn, gram_ref[...], grad_upper)
    mixed_next = by_head(dot_nn, probs_ref, upper.astype(bf16)).astype(bf16)
    next_ref[...] = mixed_next
    query_ref[...] = mixed_next[low:]
    mixed = mixed_ref[...]
    inside = support_ref[...] > 0.0
    left_ref[...] = jnp.where(inside, mixed.astype(f32), mixed_next.astype(f32)).astype(bf16)
    cross_ref[...] = (-RATE * dot_nt(mixed_next[low:], mixed[:high])).astype(bf16)


def second_tail(low, high, acc, match, probs_ref, gram_ref, mixed_ref, next_ref, tangent_ref, grad_ref):
    length, width = mixed_ref.shape
    match = -RATE * match
    grad_next = acc + split_dot(dot_nn, match, mixed_ref[:high])
    grad_next = jnp.concatenate([jnp.zeros((low, width), f32), grad_next], axis=0)
    grad_upper = by_head(dot_tn, probs_ref, grad_next.astype(bf16)).astype(bf16)
    upper_dot = -RATE * split_dot(dot_nn, gram_ref[...], grad_upper)
    tangent = by_head(dot_nn, probs_ref, upper_dot.astype(bf16)).astype(bf16)
    tangent_ref[...] = tangent[:high]
    back = split_dot(dot_tn, match, next_ref[low:])
    back = jnp.concatenate([back, jnp.zeros((length - high, width), f32)], axis=0)
    grad_ref[...] = grad_next + back


def third_tail(high, acc, grad_ref, probs_ref, out_ref):
    length, width = grad_ref.shape
    extra = jnp.concatenate([acc, jnp.zeros((length - high, width), f32)], axis=0)
    out_ref[...] = by_head(dot_tn, probs_ref, (grad_ref[...] + extra).astype(bf16)).astype(bf16)


def sources(task, members):
    pairs, cores = PAIRS, CORES
    planes = members // pairs
    plane, pair, core = task // (cores * pairs), lax.rem(task // cores, pairs), lax.rem(task, cores)
    found = [
        lax.rem(plane + planes - turn, planes) * pairs + lax.rem(pair + flip, pairs)
        for flip in range(pairs)
        for turn in range(planes)
    ]
    return found, core


def value_kernel(count, task_ref, cols_ref, *refs):
    blocks, (own_ref, sent_ref) = refs[:count], refs[count:]
    rows = blocks[0].shape[0]
    found, core = sources(task_ref[0], count)
    total = None
    for slot in range(count):
        start = pl.multiple_of(found[slot] * rows, rows)
        term = dot_tn(cols_ref[pl.ds(start, rows), :], blocks[slot][...])
        total = term if total is None else total + term
    half = total.shape[0] // CORES
    top, bottom = total[:half], total[half:]
    own_ref[...] = jnp.where(core == 0, top, bottom)
    sent_ref[...] = jnp.where(core == 0, bottom, top).astype(bf16)


def output_kernel(count, task_ref, merged_ref, error_ref, *refs):
    left, tangent, (own_ref, sent_ref) = refs[:count], refs[count : 2 * count], refs[2 * count :]
    rows, short = left[0].shape[0], tangent[0].shape[0]
    found, core = sources(task_ref[0], count)
    total = None
    for slot in range(count):
        start = pl.multiple_of(found[slot] * rows, rows)
        short_start = pl.multiple_of(found[slot] * short, short)
        term = dot_tn(left[slot][...], merged_ref[pl.ds(start, rows), :])
        term = term + dot_tn(tangent[slot][...], error_ref[pl.ds(short_start, short), :])
        total = term if total is None else total + term
    half = total.shape[1] // CORES
    first, second = total[:, :half], total[:, half:]
    own_ref[...] = jnp.where(core == 0, first, second)
    sent_ref[...] = jnp.where(core == 0, second, first).astype(bf16)


def program(n_task, n_tensor, inputs, targets, queries, key_rows, value_weight, output_weight, splits):
    length, part_width = inputs.shape
    wide = part_width * n_tensor
    heads = queries.shape[1] // HD
    width = heads * HD
    low, high = length // 4, length - length // 4
    lane = wide // CHUNKS
    group = lax.axis_index("tensor").astype(jnp.int32)
    here = group.reshape(1)
    task = lax.axis_index("task").astype(jnp.int32).reshape(1)
    cores, pairs = CORES, PAIRS
    smem = pl.BlockSpec(memory_space=pltpu.SMEM)
    vmem = pl.BlockSpec(memory_space=pltpu.VMEM)
    planes = n_task // (cores * pairs)
    members = planes * pairs

    def over_tensor(value, shift):
        return lax.ppermute(value, "tensor", [(i, (i + shift) % n_tensor) for i in range(n_tensor)])

    def from_others(value):
        return [over_tensor(value, shift) for shift in range(1, n_tensor)]

    def over_task(value, target):
        return lax.ppermute(value, "task", [(i, target(i)) for i in range(n_task)])

    def gathered(value):
        blocks = [value]
        for turn in range(1, planes):
            blocks.append(
                over_task(value, lambda i, turn=turn: (i + turn * cores * pairs) % n_task)
            )
        crossed = [over_task(value, lambda i: i ^ cores)]
        crossed += [over_task(b, lambda i: i ^ cores) for b in blocks[1:]]
        return blocks + crossed

    def spread(value):
        groups = [[m * cores + c for m in range(members)] for c in range(cores)]
        moved = lax.all_to_all(value, "task", split_axis=0, concat_axis=0, axis_index_groups=groups, tiled=True)
        return moved.reshape(members * value.shape[1], value.shape[2])

    x_pieces = [inputs] + from_others(inputs)
    places = [((group - s) % n_tensor).astype(jnp.int32).reshape(1) for s in range(n_tensor)]
    probs, support_weight, query_weight = call(
        probs_kernel,
        [Shape((heads, length, length), bf16), Shape((length, 1), f32), Shape((length, 1), f32)],
        in_specs=[smem, vmem, vmem],
    )(splits, queries, key_rows)

    block = 2 * HD if heads % 2 == 0 else HD
    x_spec = pl.BlockSpec((length, part_width), lambda i, place: (0, 0))
    w_spec = pl.BlockSpec((part_width, block), lambda i, place: (place[0], i))
    cols_spec = pl.BlockSpec((length, block), lambda i, place: (0, i))
    one_spec = pl.BlockSpec((length, 1), lambda i, place: (0, 0))

    def spec(ins, outs, scratch=()):
        return pltpu.PrefetchScalarGridSpec(
            num_scalar_prefetch=1, grid=(width // block,), in_specs=ins, out_specs=outs, scratch_shapes=scratch
        )

    sums = [Shape((length, width), f32), Shape((length, 1), f32)]
    acc, square = call(first_piece_kernel, sums, grid_spec=spec([x_spec, w_spec], [cols_spec, one_spec]))(
        places[0], inputs, value_weight
    )
    for s in range(1, n_tensor - 1):
        acc, square = call(
            piece_kernel, sums, grid_spec=spec([x_spec, w_spec, cols_spec, one_spec], [cols_spec, one_spec])
        )(places[s], x_pieces[s], value_weight, acc, square)
    probs_spec = pl.BlockSpec((block // HD, length, length), lambda i, place: (i, 0, 0))
    upper, mixed, scale = call(
        functools.partial(upper_kernel, wide),
        [Shape((length, width), bf16), Shape((length, width), bf16), Shape((length, 1), f32)],
        grid_spec=spec(
            [x_spec, w_spec, cols_spec, one_spec, probs_spec],
            [cols_spec, cols_spec, one_spec],
            [pltpu.VMEM((length, 1), f32)],
        ),
    )(places[-1], x_pieces[-1], value_weight, acc, square, probs)

    step = wide // members
    steps = lane // step
    normed, gram = call(
        functools.partial(gram_kernel, n_tensor),
        [Shape((members, length, step), bf16), Shape((length, length), f32)],
        in_specs=[smem] + [vmem] * (1 + n_tensor),
    )(here, scale, *x_pieces)
    normed_cols = spread(normed)

    def part_of(c, left, rows, cross=None, pair_of=None, error=None, offset=None):
        ins = [pl.BlockSpec((rows, width), lambda i: (0, 0)), pl.BlockSpec((width, step), lambda i: (0, c * steps + i))]
        args = [left, output_weight]
        if cross is not None:
            ins += [whole(pair_of), pl.BlockSpec((1, error.shape[1], step), lambda i: (c * steps + i, 0, 0))]
            args += [pair_of, error]
        if offset is not None:
            piece, start = c * lane // part_width, c * lane % part_width // step
            offset = (offset, piece)
            ins += [smem] + [pl.BlockSpec((length, step), lambda i: (0, start + i))] * 2
            args += [here, inputs, targets]
        part = call(
            functools.partial(part_kernel, cross, offset),
            Shape((rows, lane), bf16),
            grid=(steps,),
            in_specs=ins,
            out_specs=pl.BlockSpec((rows, step), lambda i: (0, i)),
        )(*args)
        return part, from_others(part)

    def combine(parts, row_slice, weight, matches, merged, tail, tail_args, tail_shapes):
        rows = row_slice.stop - row_slice.start
        errors = None
        chain = []
        for c, (part, others) in enumerate(parts):
            last = c == CHUNKS - 1
            cols = pl.BlockSpec((rows, step), lambda i: (0, i))
            stack = lambda r, c=c: pl.BlockSpec((1, r, step), lambda i: (c * steps + i, 0, 0))
            ins = [cols, pl.BlockSpec((width, step), lambda i, c=c: (0, c * steps + i)), whole(weight)]
            args = [part, output_weight, weight]
            ins += [cols] * len(others)
            args += others
            for extra in (matches, merged):
                if extra is not None:
                    ins.append(stack(extra.shape[1]))
                    args.append(extra)
            ins += [whole(a) for a in chain]
            args += chain
            aliases = {}
            if errors is not None:
                aliases = {len(args): 0}
                ins.append(pl.BlockSpec(memory_space=pl.ANY))
                args.append(errors)
            sums = [Shape((rows, width), f32)] + ([Shape((rows, matches.shape[1]), f32)] if matches is not None else [])
            out_rows = rows if merged is None else length
            outs = [Shape((members, out_rows, step), bf16)]
            out_specs = [stack(out_rows)]
            scratch = []
            n_tail = 0
            if last:
                ins += [whole(a) for a in tail_args]
                args += tail_args
                n_tail = len(tail_args)
                outs += tail_shapes
                out_specs += [whole(s) for s in tail_shapes]
                scratch = [pltpu.VMEM(s.shape, s.dtype) for s in sums]
            else:
                outs += sums
                out_specs += [whole(s) for s in sums]
            results = call(
                functools.partial(
                    finish_kernel, row_slice, len(others), matches is not None, merged is not None,
                    bool(chain), errors is not None, tail if last else None, n_tail,
                ),
                outs,
                grid=(steps,),
                in_specs=ins,
                out_specs=out_specs,
                scratch_shapes=scratch,
                input_output_aliases=aliases,
            )(*args)
            errors = results[0]
            chain = list(results[1:])
        return errors, chain

    parts = [part_of(c, mixed, high, offset=slice(0, high)) for c in range(CHUNKS)]
    error_0, (mixed_next, next_q, left, cross) = combine(
        parts, slice(0, high), support_weight, None, None,
        functools.partial(step_tail, low, high),
        [probs, gram, upper, mixed, support_weight],
        [
            Shape((length, width), bf16),
            Shape((length - low, width), bf16),
            Shape((length, width), bf16),
            Shape((length - low, high), bf16),
        ],
    )
    error_0_cols = spread(error_0)

    parts = [part_of(c, next_q, length - low, dot_nn, cross, error_0, slice(low, length)) for c in range(CHUNKS)]
    left_all = gathered(left)
    error_q, (tangent, grad_rest) = combine(
        parts, slice(low, length), query_weight, error_0, None,
        functools.partial(second_tail, low, high),
        [probs, gram, mixed, mixed_next],
        [Shape((high, width), bf16), Shape((length, width), f32)],
    )
    parts = [part_of(c, tangent, high, dot_tn, cross, error_q) for c in range(CHUNKS)]
    tangent_all = gathered(tangent)
    merged, (right,) = combine(
        parts, slice(0, high), support_weight, None, error_q,
        functools.partial(third_tail, high),
        [grad_rest, probs],
        [Shape((length, width), bf16)],
    )
    right_all = gathered(right)
    merged_cols = spread(merged)

    wide_block = wide // n_task
    own_v, sent_v = call(
        functools.partial(value_kernel, members),
        [Shape((wide_block, width), f32), Shape((wide_block, width), bf16)],
        in_specs=[smem] + [vmem] * (1 + members),
        out_specs=[vmem, vmem],
    )(task, normed_cols, *right_all)
    own_o, sent_o = call(
        functools.partial(output_kernel, members),
        [Shape((width, wide_block), f32), Shape((width, wide_block), bf16)],
        in_specs=[smem] + [vmem] * (2 + 2 * members),
        out_specs=[vmem, vmem],
    )(task, merged_cols, error_0_cols, *left_all, *tangent_all)
    total_value = own_v + over_task(sent_v, lambda i: i ^ 1).astype(f32)
    total_output = own_o + over_task(sent_o, lambda i: i ^ 1).astype(f32)
    return (total_value, total_output)


def solution(mesh):
    body = functools.partial(program, mesh.shape["task"], mesh.shape["tensor"])
    return jax.shard_map(
        body,
        mesh=mesh,
        in_specs=(
            P("task", "tensor"),
            P("task", "tensor"),
            P("task", "tensor"),
            P("task", "tensor"),
            P(None, "tensor"),
            P("tensor", None),
            P("task"),
        ),
        out_specs=(P("task", "tensor"), P("tensor", "task")),
        check_vma=False,
    )
```

time: 469 us -> 256 us (0.55)
  waiting for transfers between devices: 324 us -> 99.7 us
  matrix products: 99.5 us -> 0 us
  starting transfers between devices: 1.01 us -> 48.6 us
  Pallas kernels: 0 us -> 45.9 us
  blocking collectives: 0 us -> 24.1 us
  local copies, waits for them, and re-layouts: 12.7 us -> 32 us
  between operations: 15.4 us -> 1.75 us
  other arithmetic: 12.2 us -> 3.6 us
    reduce_scatter x5 -> x0, waiting for transfers between devices: 241 us -> none  [the longest x1 105 us: per_device(): lax.psum_scatter(total_value.astype(jnp.bfloat16), 'task', scatter_dimens...]
    ppermute x0 -> x36, waiting for transfers between devices: none -> 99.7 us  [the longest x23 76.1 us: over_task(): return lax.ppermute(value, 'task', [(i, target(i)) for i in range(n_task)])]
    dot_general x25 -> x0, matrix products: 98.2 us -> none  [the longest x12 60.3 us: local_out(): jnp.dot(mixed, output_mat.astype(jnp.bfloat16), preferred_element_type=jn...]
    all_gather x4 -> x0, waiting for transfers between devices: 82 us -> none  [the longest x3 58 us: combine(): lax.all_gather((weight * (share + offset)).astype(jnp.bfloat16), 'tensor'...]
    pallas_call x0 -> x30, Pallas kernels: none -> 45.9 us  [the longest x12 19.7 us: combine(): call(functools.partial(finish_kernel, row_slice, len(others), matches is...]
    ppermute x0 -> x36, starting transfers between devices: none -> 39.2 us  [the longest x23 23.3 us: over_task(): return lax.ppermute(value, 'task', [(i, target(i)) for i in range(n_task)])]
    all_to_all x0 -> x1, blocking collectives: none -> 24.1 us  [spread(): lax.all_to_all(value, 'task', split_axis=0, concat_axis=0, axis_index_gro...]
    unnamed x26 -> x90, local copies, waits for them, and re-layouts: 9.88 us -> 32 us
  transfers between devices with their start and end apart: 9 -> 38, of which waited for: 9 -> 21; matrix products, arithmetic and copies ran while one was open for 8% -> 1% of each run, Pallas kernels for 0% -> 16%
where the time goes in v1:
time: 256 us
  waiting for transfers between devices  99.7 us (39%)
  starting transfers between devices  48.6 us (19%)
  Pallas kernels  45.9 us (18%)
  local copies, waits for them, and re-layouts  32 us (12%)
  blocking collectives  24.1 us (9%)
  other arithmetic  3.6 us (1%)
    ppermute x23, waiting for transfers between devices, over_task(): return lax.ppermute(value, 'task', [(i, target(i)) for i in range(n_task)])  76.1 us
    unnamed x90, local copies, waits for them, and re-layouts  32 us
    all_to_all x1, blocking collectives, spread(): lax.all_to_all(value, 'task', split_axis=0, concat_axis=0, axis_index_gro...  24.1 us
    ppermute x13, waiting for transfers between devices, over_tensor(): lax.ppermute(value, 'tensor', [(i, (i + shift) % n_tensor) for i in range...  23.6 us
    ppermute x23, starting transfers between devices, over_task(): return lax.ppermute(value, 'task', [(i, target(i)) for i in range(n_task)])  23.3 us
    pallas_call x12, Pallas kernels, combine(): call(functools.partial(finish_kernel, row_slice, len(others), matches is...  19.7 us
    ppermute x13, starting transfers between devices, over_tensor(): lax.ppermute(value, 'tensor', [(i, (i + shift) % n_tensor) for i in range...  16 us
    pallas_call x12, Pallas kernels, part_of(): call(functools.partial(part_kernel, cross, offset), Shape((rows, lane), b...  11.1 us
  transfers between devices with their start and end apart: 38, of which 21 were waited for; matrix products, arithmetic and copies ran while one was open for 1% of the time, Pallas kernels for 16%

profile of v1, /device:TPU:0, one launch (start us, length us, event | category | flops | bytes accessed | tf_op | source)
XLA Modules:
  0.0 255.6 jit_solution(17145081921423568728)
XLA Ops:
  0.6 3.1 %collective-permute-start = (bf16[128,2048]{1,0:T(8,128)(2,1)}, bf16[128,2048]{1,0:T(8,128)(2,1)S(1)}, u32[]{:S(2)}, u32[]{:S(2)}) collective-permute-start(bf16[128,2048]{1,0:T(8,128)(2,1)} %refs_5_.7), channel_id=1, source_target_pairs={{0,1},{1,0},{2,3},{3,2},{4,5},{5,4},{6,7},{7,6},{8,9},{9,8},{10,11... | collective-permute-start | bytes 1572872 | tf_op jit(solution)/shard_map/ppermute | solution.py:302
  5.4 3.4 %copy-done.4 = bf16[4096,1024]{1,0:T(8,128)(2,1)S(1)} copy-done((bf16[4096,1024]{1,0:T(8,128)(2,1)S(1)}, bf16[4096,1024]{1,0:T(8,128)(2,1)}, u32[]{:S(2)}) %copy-start.4) | copy-done | bytes 8388632
  11.5 4.3 %collective-permute-done.x_ref.refs_1_ = bf16[128,2048]{1,0:T(8,128)(2,1)S(1)} collective-permute-done((bf16[128,2048]{1,0:T(8,128)(2,1)}, bf16[128,2048]{1,0:T(8,128)(2,1)S(1)}, u32[]{:S(2)}, u32[]{:S(2)}) %collective-permute-start) | collective-permute-done | bytes 524320 | tf_op jit(solution)/shard_map/ppermute | solution.py:302
  15.8 3.4 %copy-done.5 = bf16[4096,1024]{1,0:T(8,128)(2,1)S(1)} copy-done((bf16[4096,1024]{1,0:T(8,128)(2,1)S(1)}, bf16[4096,1024]{1,0:T(8,128)(2,1)}, u32[]{:S(2)}) %copy-start.5) | copy-done | bytes 8388632
  19.2 2.9 %shard_map.88 = (bf16[128,1024]{1,0:T(8,128)(2,1)S(1)}, bf16[128,1024]{1,0:T(8,128)(2,1)S(1)}, f32[128,1]{1,0:T(8,128)S(1)}) custom-call(s32[1]{0:T(128)} %bitcast.2.place_ref, bf16[128,2048]{1,0:T(8,128)(2,1)S(1)} %collective-permute-done.x_ref.refs_1_, bf16[4096,1024]{1,0:T(8,128)(2,1)S(1)} %copy-done.5, f32[128,1024]{1,0:T(8,128)S(1)} %get-tuple-element.47.acc_ref, ...), custom_call_target="tpu_custom_call" | custom-call | tf_op jit(solution)/shard_map/pallas_call | solution.py:353
  32.1 3.0 %collective-permute-done.3.refs_3_ = bf16[96,1024]{1,0:T(8,128)(2,1)S(1)} collective-permute-done((bf16[96,1024]{1,0:T(8,128)(2,1)S(1)}, bf16[96,1024]{1,0:T(8,128)(2,1)S(1)}, u32[]{:S(2)}, u32[]{:S(2)}) %collective-permute-start.3) | collective-permute-done | bytes 196640 | tf_op jit(solution)/shard_map/ppermute | solution.py:302
  36.3 3.0 %collective-permute-done.2.refs_3_ = bf16[96,1024]{1,0:T(8,128)(2,1)S(1)} collective-permute-done((bf16[96,1024]{1,0:T(8,128)(2,1)S(1)}, bf16[96,1024]{1,0:T(8,128)(2,1)S(1)}, u32[]{:S(2)}, u32[]{:S(2)}) %collective-permute-start.2) | collective-permute-done | bytes 196640 | tf_op jit(solution)/shard_map/ppermute | solution.py:302
  46.0 24.1 %all_to_all.15 = bf16[8,96,512]{2,1,0:T(8,128)(2,1)} all-to-all(bf16[8,96,512]{2,1,0:T(8,128)(2,1)S(1)} %get-tuple-element.64.refs_3_.refs_4_), channel_id=1, replica_groups={{0,4,8,12,16,20,24,28},{2,6,10,14,18,22,26,30},{1,5,9,13,17,21,25,29},{..., dimensions={0} | all-to-all | bytes 1572864 | tf_op jit(solution)/shard_map/all_to_all | solution.py:322
  70.1 3.7 %all-to-all-start = ((bf16[8,128,512]{2,1,0:T(8,128)(2,1)}), bf16[8,128,512]{2,1,0:T(8,128)(2,1)S(1)}, u32[]{:S(2)}, u32[]{:S(2)}) async-start(bf16[8,128,512]{2,1,0:T(8,128)(2,1)} %copy-done.11), calls=%async_computation | async-start | bytes 2097152 | tf_op jit(solution)/shard_map/all_to_all | solution.py:322
  73.8 3.4 %copy-done = bf16[1024,4096]{1,0:T(8,128)(2,1)S(1)} copy-done((bf16[1024,4096]{1,0:T(8,128)(2,1)S(1)}, bf16[1024,4096]{1,0:T(8,128)(2,1)}, u32[]{:S(2)}) %copy-start) | copy-done | bytes 8388632
  88.2 2.9 %collective-permute-done.7.refs_3_ = bf16[96,1024]{1,0:T(8,128)(2,1)S(1)} collective-permute-done((bf16[96,1024]{1,0:T(8,128)(2,1)S(1)}, bf16[96,1024]{1,0:T(8,128)(2,1)S(1)}, u32[]{:S(2)}, u32[]{:S(2)}) %collective-permute-start.7) | collective-permute-done | bytes 196640 | tf_op jit(solution)/shard_map/ppermute | solution.py:302
  92.4 2.8 %collective-permute-done.6.refs_3_ = bf16[96,1024]{1,0:T(8,128)(2,1)S(1)} collective-permute-done((bf16[96,1024]{1,0:T(8,128)(2,1)S(1)}, bf16[96,1024]{1,0:T(8,128)(2,1)S(1)}, u32[]{:S(2)}, u32[]{:S(2)}) %collective-permute-start.6) | collective-permute-done | bytes 196640 | tf_op jit(solution)/shard_map/ppermute | solution.py:302
  120.9 5.6 %all-to-all-start.1 = ((bf16[8,128,512]{2,1,0:T(8,128)(2,1)}), bf16[8,128,512]{2,1,0:T(8,128)(2,1)S(1)}, u32[]{:S(2)}, u32[]{:S(2)}) async-start(bf16[8,128,512]{2,1,0:T(8,128)(2,1)} %get-tuple-element.88), calls=%async_computation.1 | async-start | bytes 2097152 | tf_op jit(solution)/shard_map/all_to_all | solution.py:322
  133.5 21.1 %collective-permute-done.21.refs_1_ = bf16[128,1024]{1,0:T(8,128)(2,1)S(1)} collective-permute-done((bf16[128,1024]{1,0:T(8,128)(2,1)}, bf16[128,1024]{1,0:T(8,128)(2,1)S(1)}, u32[]{:S(2)}, u32[]{:S(2)}) %collective-permute-start.21) | collective-permute-done | bytes 262176 | tf_op jit(solution)/shard_map/ppermute | solution.py:308
  156.0 24.4 %collective-permute-done.22.refs_2_ = bf16[128,1024]{1,0:T(8,128)(2,1)} collective-permute-done((bf16[128,1024]{1,0:T(8,128)(2,1)}, bf16[128,1024]{1,0:T(8,128)(2,1)}, u32[]{:S(2)}, u32[]{:S(2)}) %collective-permute-start.22) | collective-permute-done | bytes 262176 | tf_op jit(solution)/shard_map/ppermute | solution.py:308
  183.5 8.1 %collective-permute-done.14.refs_2_ = bf16[128,1024]{1,0:T(8,128)(2,1)S(1)} collective-permute-done((bf16[128,1024]{1,0:T(8,128)(2,1)}, bf16[128,1024]{1,0:T(8,128)(2,1)S(1)}, u32[]{:S(2)}, u32[]{:S(2)}) %collective-permute-start.14) | collective-permute-done | bytes 262176 | tf_op jit(solution)/shard_map/ppermute | solution.py:308
  197.3 5.0 %collective-permute-done.28.refs_9_ = bf16[96,1024]{1,0:T(8,128)(2,1)S(1)} collective-permute-done((bf16[96,1024]{1,0:T(8,128)(2,1)S(1)}, bf16[96,1024]{1,0:T(8,128)(2,1)S(1)}, u32[]{:S(2)}, u32[]{:S(2)}) %collective-permute-start.28) | collective-permute-done | bytes 196640 | tf_op jit(solution)/shard_map/ppermute | solution.py:308
  217.5 3.2 %shard_map.114 = (f32[256,1024]{1,0:T(8,128)S(1)}, bf16[256,1024]{1,0:T(8,128)(2,1)}) custom-call(s32[1]{0:T(128)} %bitcast.task_ref, bf16[1024,512]{1,0:T(8,128)(2,1)S(1)} %bitcast.11, bf16[128,1024]{1,0:T(8,128)(2,1)S(1)} %copy-done.24, bf16[128,1024]{1,0:T(8,128)(2,1)S(1)} %copy-done.26, bf16[128,1024]{1,0:T(8,128)(2,1)S(1)} %copy-done.28, ...), custom_call_target="tpu_custom_call" | custom-call | tf_op jit(solution)/shard_map/pallas_call | solution.py:481
  225.8 5.3 %collective-permute-done.27.refs_7_ = bf16[128,1024]{1,0:T(8,128)(2,1)S(1)} collective-permute-done((bf16[128,1024]{1,0:T(8,128)(2,1)}, bf16[128,1024]{1,0:T(8,128)(2,1)S(1)}, u32[]{:S(2)}, u32[]{:S(2)}) %collective-permute-start.27) | collective-permute-done | bytes 262176 | tf_op jit(solution)/shard_map/ppermute | solution.py:308
  231.1 4.2 %collective-permute-done.32.refs_13_ = bf16[96,1024]{1,0:T(8,128)(2,1)S(1)} collective-permute-done((bf16[96,1024]{1,0:T(8,128)(2,1)}, bf16[96,1024]{1,0:T(8,128)(2,1)S(1)}, u32[]{:S(2)}, u32[]{:S(2)}) %collective-permute-start.32) | collective-permute-done | bytes 196640 | tf_op jit(solution)/shard_map/ppermute | solution.py:308
  235.3 4.2 %collective-permute-done.33.refs_14_ = bf16[96,1024]{1,0:T(8,128)(2,1)S(1)} collective-permute-done((bf16[96,1024]{1,0:T(8,128)(2,1)}, bf16[96,1024]{1,0:T(8,128)(2,1)S(1)}, u32[]{:S(2)}, u32[]{:S(2)}) %collective-permute-start.33) | collective-permute-done | bytes 196640 | tf_op jit(solution)/shard_map/ppermute | solution.py:308
  239.5 3.7 %collective-permute-done.34.refs_15_ = bf16[96,1024]{1,0:T(8,128)(2,1)S(1)} collective-permute-done((bf16[96,1024]{1,0:T(8,128)(2,1)}, bf16[96,1024]{1,0:T(8,128)(2,1)S(1)}, u32[]{:S(2)}, u32[]{:S(2)}) %collective-permute-start.34) | collective-permute-done | bytes 196640 | tf_op jit(solution)/shard_map/ppermute | solution.py:308
  246.1 5.9 %shard_map.115 = (f32[1024,256]{1,0:T(8,128)S(1)}, bf16[1024,256]{1,0:T(8,128)(2,1)S(1)}) custom-call(s32[1]{0:T(128)} %bitcast.task_ref, bf16[1024,512]{1,0:T(8,128)(2,1)S(1)} %bitcast.12, bf16[768,512]{1,0:T(8,128)(2,1)S(1)} %bitcast.13, bf16[128,1024]{1,0:T(8,128)(2,1)S(1)} %copy-done.16, bf16[128,1024]{1,0:T(8,128)(2,1)S(1)} %collective-permute-done.21.refs_1_, ...), custom_call_target="tpu_custom_call" | custom-call | tf_op jit(solution)/shard_map/pallas_call | solution.py:487
  252.0 2.5 convert_add_fusion.1
  (177 shorter events, 100.8 us)
Async XLA Ops:
  0.6 15.2 %collective-permute-start = (bf16[128,2048]{1,0:T(8,128)(2,1)}, bf16[128,2048]{1,0:T(8,128)(2,1)S(1)}, u32[]{:S(2)}, u32[]{:S(2)}) collective-permute-start(bf16[128,2048]{1,0:T(8,128)(2,1)} %refs_5_.7), channel_id=1, source_target_pairs={{0,1},{1,0},{2,3},{3,2},{4,5},{5,4},{6,7},{7,6},{8,9},{9,8},{10,11... | collective-permute-start | bytes 1572872 | tf_op jit(solution)/shard_map/ppermute | solution.py:302
  26.9 12.3 %collective-permute-start.2 = (bf16[96,1024]{1,0:T(8,128)(2,1)S(1)}, bf16[96,1024]{1,0:T(8,128)(2,1)S(1)}, u32[]{:S(2)}, u32[]{:S(2)}) collective-permute-start(bf16[96,1024]{1,0:T(8,128)(2,1)S(1)} %shard_map.91.refs_0_), channel_id=1, source_target_pairs={{0,1},{1,0},{2,3},{3,2},{4,5},{5,4},{6,7},{7,6},{8,9},{9,8},{10,11... | collective-permute-start | bytes 589832 | tf_op jit(solution)/shard_map/ppermute | solution.py:302
  70.1 50.9 %all-to-all-start = ((bf16[8,128,512]{2,1,0:T(8,128)(2,1)}), bf16[8,128,512]{2,1,0:T(8,128)(2,1)S(1)}, u32[]{:S(2)}, u32[]{:S(2)}) async-start(bf16[8,128,512]{2,1,0:T(8,128)(2,1)} %copy-done.11), calls=%async_computation | async-start | bytes 2097152 | tf_op jit(solution)/shard_map/all_to_all | solution.py:322
  120.9 122.3 %all-to-all-start.1 = ((bf16[8,128,512]{2,1,0:T(8,128)(2,1)}), bf16[8,128,512]{2,1,0:T(8,128)(2,1)S(1)}, u32[]{:S(2)}, u32[]{:S(2)}) async-start(bf16[8,128,512]{2,1,0:T(8,128)(2,1)} %get-tuple-element.88), calls=%async_computation.1 | async-start | bytes 2097152 | tf_op jit(solution)/shard_map/all_to_all | solution.py:322
  126.5 28.1 %collective-permute-start.21 = (bf16[128,1024]{1,0:T(8,128)(2,1)}, bf16[128,1024]{1,0:T(8,128)(2,1)S(1)}, u32[]{:S(2)}, u32[]{:S(2)}) collective-permute-start(bf16[128,1024]{1,0:T(8,128)(2,1)} %copy-done.15), channel_id=1, source_target_pairs={{0,8},{2,10},{4,12},{6,14},{8,16},{10,18},{12,20},{14,22},{16,24},... | collective-permute-start | bytes 786440 | tf_op jit(solution)/shard_map/ppermute | solution.py:308
  128.5 51.9 %collective-permute-start.22 = (bf16[128,1024]{1,0:T(8,128)(2,1)}, bf16[128,1024]{1,0:T(8,128)(2,1)}, u32[]{:S(2)}, u32[]{:S(2)}) collective-permute-start(bf16[128,1024]{1,0:T(8,128)(2,1)} %copy-done.15), channel_id=1, source_target_pairs={{0,16},{2,18},{4,20},{6,22},{8,24},{10,26},{12,28},{14,30},{16,0},... | collective-permute-start | bytes 786440 | tf_op jit(solution)/shard_map/ppermute | solution.py:308
  130.9 49.8 %collective-permute-start.23 = (bf16[128,1024]{1,0:T(8,128)(2,1)}, bf16[128,1024]{1,0:T(8,128)(2,1)}, u32[]{:S(2)}, u32[]{:S(2)}) collective-permute-start(bf16[128,1024]{1,0:T(8,128)(2,1)} %copy-done.15), channel_id=1, source_target_pairs={{0,24},{2,26},{4,28},{6,30},{8,0},{10,2},{12,4},{14,6},{16,8},{18,... | collective-permute-start | bytes 786440 | tf_op jit(solution)/shard_map/ppermute | solution.py:308
  132.3 49.6 %collective-permute-start.13 = (bf16[128,1024]{1,0:T(8,128)(2,1)}, bf16[128,1024]{1,0:T(8,128)(2,1)S(1)}, u32[]{:S(2)}, u32[]{:S(2)}) collective-permute-start(bf16[128,1024]{1,0:T(8,128)(2,1)} %copy-done.23), channel_id=1, source_target_pairs={{0,8},{2,10},{4,12},{6,14},{8,16},{10,18},{12,20},{14,22},{16,24},... | collective-permute-start | bytes 786440 | tf_op jit(solution)/shard_map/ppermute | solution.py:308
  132.9 58.6 %collective-permute-start.14 = (bf16[128,1024]{1,0:T(8,128)(2,1)}, bf16[128,1024]{1,0:T(8,128)(2,1)S(1)}, u32[]{:S(2)}, u32[]{:S(2)}) collective-permute-start(bf16[128,1024]{1,0:T(8,128)(2,1)} %copy-done.23), channel_id=1, source_target_pairs={{0,16},{2,18},{4,20},{6,22},{8,24},{10,26},{12,28},{14,30},{16,0},... | collective-permute-start | bytes 786440 | tf_op jit(solution)/shard_map/ppermute | solution.py:308
  154.6 38.7 %collective-permute-start.24 = (bf16[128,1024]{1,0:T(8,128)(2,1)}, bf16[128,1024]{1,0:T(8,128)(2,1)S(1)}, u32[]{:S(2)}, u32[]{:S(2)}) collective-permute-start(bf16[128,1024]{1,0:T(8,128)(2,1)} %copy-done.15), channel_id=1, source_target_pairs={{0,4},{2,6},{4,0},{6,2},{8,12},{10,14},{12,8},{14,10},{16,20},{18,... | collective-permute-start | bytes 786440 | tf_op jit(solution)/shard_map/ppermute | solution.py:308
  180.4 15.5 %collective-permute-start.15 = (bf16[128,1024]{1,0:T(8,128)(2,1)}, bf16[128,1024]{1,0:T(8,128)(2,1)S(1)}, u32[]{:S(2)}, u32[]{:S(2)}) collective-permute-start(bf16[128,1024]{1,0:T(8,128)(2,1)} %copy-done.23), channel_id=1, source_target_pairs={{0,24},{2,26},{4,28},{6,30},{8,0},{10,2},{12,4},{14,6},{16,8},{18,... | collective-permute-start | bytes 786440 | tf_op jit(solution)/shard_map/ppermute | solution.py:308
  180.7 21.7 %collective-permute-start.16 = (bf16[128,1024]{1,0:T(8,128)(2,1)}, bf16[128,1024]{1,0:T(8,128)(2,1)S(1)}, u32[]{:S(2)}, u32[]{:S(2)}) collective-permute-start(bf16[128,1024]{1,0:T(8,128)(2,1)} %copy-done.23), channel_id=1, source_target_pairs={{0,4},{2,6},{4,0},{6,2},{8,12},{10,14},{12,8},{14,10},{16,20},{18,... | collective-permute-start | bytes 786440 | tf_op jit(solution)/shard_map/ppermute | solution.py:308
  181.9 23.1 %collective-permute-start.17 = (bf16[128,1024]{1,0:T(8,128)(2,1)S(1)}, bf16[128,1024]{1,0:T(8,128)(2,1)S(1)}, u32[]{:S(2)}, u32[]{:S(2)}) collective-permute-start(bf16[128,1024]{1,0:T(8,128)(2,1)S(1)} %collective-permute-done.13.refs_1_), channel_id=1, source_target_pairs={{0,4},{2,6},{4,0},{6,2},{8,12},{10,14},{12,8},{14,10},{16,20},{18,... | collective-permute-start | bytes 786440 | tf_op jit(solution)/shard_map/ppermute | solution.py:308
  191.6 14.9 %collective-permute-start.18 = (bf16[128,1024]{1,0:T(8,128)(2,1)S(1)}, bf16[128,1024]{1,0:T(8,128)(2,1)S(1)}, u32[]{:S(2)}, u32[]{:S(2)}) collective-permute-start(bf16[128,1024]{1,0:T(8,128)(2,1)S(1)} %collective-permute-done.14.refs_2_), channel_id=1, source_target_pairs={{0,4},{2,6},{4,0},{6,2},{8,12},{10,14},{12,8},{14,10},{16,20},{18,... | collective-permute-start | bytes 786440 | tf_op jit(solution)/shard_map/ppermute | solution.py:308
  195.9 12.6 %collective-permute-start.19 = (bf16[128,1024]{1,0:T(8,128)(2,1)S(1)}, bf16[128,1024]{1,0:T(8,128)(2,1)S(1)}, u32[]{:S(2)}, u32[]{:S(2)}) collective-permute-start(bf16[128,1024]{1,0:T(8,128)(2,1)S(1)} %collective-permute-done.15.refs_3_), channel_id=1, source_target_pairs={{0,4},{2,6},{4,0},{6,2},{8,12},{10,14},{12,8},{14,10},{16,20},{18,... | collective-permute-start | bytes 786440 | tf_op jit(solution)/shard_map/ppermute | solution.py:308
  202.3 19.3 %collective-permute-start.29 = (bf16[96,1024]{1,0:T(8,128)(2,1)S(1)}, bf16[96,1024]{1,0:T(8,128)(2,1)}, u32[]{:S(2)}, u32[]{:S(2)}) collective-permute-start(bf16[96,1024]{1,0:T(8,128)(2,1)S(1)} %get-tuple-element.76.refs_0_.refs_8_), channel_id=1, source_target_pairs={{0,16},{2,18},{4,20},{6,22},{8,24},{10,26},{12,28},{14,30},{16,0},... | collective-permute-start | bytes 589832 | tf_op jit(solution)/shard_map/ppermute | solution.py:308
  203.1 18.5 %collective-permute-start.30 = (bf16[96,1024]{1,0:T(8,128)(2,1)S(1)}, bf16[96,1024]{1,0:T(8,128)(2,1)}, u32[]{:S(2)}, u32[]{:S(2)}) collective-permute-start(bf16[96,1024]{1,0:T(8,128)(2,1)S(1)} %get-tuple-element.76.refs_0_.refs_8_), channel_id=1, source_target_pairs={{0,24},{2,26},{4,28},{6,30},{8,0},{10,2},{12,4},{14,6},{16,8},{18,... | collective-permute-start | bytes 589832 | tf_op jit(solution)/shard_map/ppermute | solution.py:308
  205.8 18.0 %collective-permute-start.25 = (bf16[128,1024]{1,0:T(8,128)(2,1)S(1)}, bf16[128,1024]{1,0:T(8,128)(2,1)}, u32[]{:S(2)}, u32[]{:S(2)}) collective-permute-start(bf16[128,1024]{1,0:T(8,128)(2,1)S(1)} %collective-permute-done.21.refs_1_), channel_id=1, source_target_pairs={{0,4},{2,6},{4,0},{6,2},{8,12},{10,14},{12,8},{14,10},{16,20},{18,... | collective-permute-start | bytes 786440 | tf_op jit(solution)/shard_map/ppermute | solution.py:308
  207.1 18.0 %collective-permute-start.26 = (bf16[128,1024]{1,0:T(8,128)(2,1)}, bf16[128,1024]{1,0:T(8,128)(2,1)}, u32[]{:S(2)}, u32[]{:S(2)}) collective-permute-start(bf16[128,1024]{1,0:T(8,128)(2,1)} %collective-permute-done.22.refs_2_), channel_id=1, source_target_pairs={{0,4},{2,6},{4,0},{6,2},{8,12},{10,14},{12,8},{14,10},{16,20},{18,... | collective-permute-start | bytes 786440 | tf_op jit(solution)/shard_map/ppermute | solution.py:308
  209.3 13.9 %collective-permute-start.31 = (bf16[96,1024]{1,0:T(8,128)(2,1)S(1)}, bf16[96,1024]{1,0:T(8,128)(2,1)}, u32[]{:S(2)}, u32[]{:S(2)}) collective-permute-start(bf16[96,1024]{1,0:T(8,128)(2,1)S(1)} %get-tuple-element.76.refs_0_.refs_8_), channel_id=1, source_target_pairs={{0,4},{2,6},{4,0},{6,2},{8,12},{10,14},{12,8},{14,10},{16,20},{18,... | collective-permute-start | bytes 589832 | tf_op jit(solution)/shard_map/ppermute | solution.py:308
  221.6 30.4 %collective-permute-start.20 = (bf16[256,1024]{1,0:T(8,128)(2,1)}, bf16[256,1024]{1,0:T(8,128)(2,1)}, u32[]{:S(2)}, u32[]{:S(2)}) collective-permute-start(bf16[256,1024]{1,0:T(8,128)(2,1)} %get-tuple-element.87), channel_id=1, source_target_pairs={{0,2},{2,0},{4,6},{6,4},{8,10},{10,8},{12,14},{14,12},{16,18},{18,... | collective-permute-start | bytes 1572872 | tf_op jit(solution)/shard_map/ppermute | solution.py:308
  223.1 12.2 %collective-permute-start.32 = (bf16[96,1024]{1,0:T(8,128)(2,1)}, bf16[96,1024]{1,0:T(8,128)(2,1)S(1)}, u32[]{:S(2)}, u32[]{:S(2)}) collective-permute-start(bf16[96,1024]{1,0:T(8,128)(2,1)} %copy-done.39), channel_id=1, source_target_pairs={{0,4},{2,6},{4,0},{6,2},{8,12},{10,14},{12,8},{14,10},{16,20},{18,... | collective-permute-start | bytes 589832 | tf_op jit(solution)/shard_map/ppermute | solution.py:308
  223.8 15.8 %collective-permute-start.33 = (bf16[96,1024]{1,0:T(8,128)(2,1)}, bf16[96,1024]{1,0:T(8,128)(2,1)S(1)}, u32[]{:S(2)}, u32[]{:S(2)}) collective-permute-start(bf16[96,1024]{1,0:T(8,128)(2,1)} %collective-permute-done.29.refs_10_), channel_id=1, source_target_pairs={{0,4},{2,6},{4,0},{6,2},{8,12},{10,14},{12,8},{14,10},{16,20},{18,... | collective-permute-start | bytes 589832 | tf_op jit(solution)/shard_map/ppermute | solution.py:308
  225.1 18.1 %collective-permute-start.34 = (bf16[96,1024]{1,0:T(8,128)(2,1)}, bf16[96,1024]{1,0:T(8,128)(2,1)S(1)}, u32[]{:S(2)}, u32[]{:S(2)}) collective-permute-start(bf16[96,1024]{1,0:T(8,128)(2,1)} %collective-permute-done.30.refs_11_), channel_id=1, source_target_pairs={{0,4},{2,6},{4,0},{6,2},{8,12},{10,14},{12,8},{14,10},{16,20},{18,... | collective-permute-start | bytes 589832 | tf_op jit(solution)/shard_map/ppermute | solution.py:308
  (59 other events, 402.1 us)

commit v2 on v1

--- a/solution.py
+++ b/solution.py
@@ -12,7 +12,8 @@
 RATE = 0.25
 CORES = 2
 PAIRS = 2
-CHUNKS = 4
+SHARES = (4, 4)
+CHUNKS = len(SHARES)
 VMEM_LIMIT = 16 * 1024 * 1024
 
 
@@ -83,6 +84,24 @@
     out_ref[...] = acc_ref[...] + dot_nn(x_ref[...], weight_ref[...])
 
 
+def copy_kernel(source_ref, out_ref):
+    out_ref[...] = source_ref[...]
+
+
+def place_copy_kernel(place_ref, source_ref, out_ref):
+    out_ref[...] = source_ref[...]
+
+
+def pack_kernel(count, *refs):
+    out_ref = refs[-1]
+    for turn in range(count):
+        first, second = refs[turn], refs[count + turn]
+        rows = first.shape[1]
+        for flip in range(PAIRS):
+            out_ref[turn * PAIRS + flip, :rows] = first[flip]
+            out_ref[turn * PAIRS + flip, rows:] = second[flip]
+
+
 def row_squares(value):
     value = value.astype(f32)
     return jnp.sum(value * value, axis=-1, keepdims=True)
@@ -110,21 +129,61 @@
     mixed_ref[...] = by_head(dot_nn, probs_ref, upper).astype(bf16)
 
 
-def gram_kernel(pieces, group_ref, scale_ref, *refs):
-    x_refs, (normed_ref, gram_ref) = refs[:pieces], refs[pieces:]
-    count, _, step = normed_ref.shape
+def own_rows(value, group, parts):
+    rows = value.shape[0] // parts
+    out = value[:rows]
+    for p in range(1, parts):
+        out = jnp.where(group == p, value[p * rows : (p + 1) * rows], out)
+    return out
+
+
+def all_rows(pieces, group):
+    parts = len(pieces)
+    if parts == 1:
+        return pieces[0]
+    out = []
+    for p in range(parts):
+        piece = pieces[0]
+        for shift in range(1, parts):
+            piece = jnp.where(lax.rem(group + parts - shift, parts) == p, pieces[shift], piece)
+        out.append(piece)
+    return jnp.concatenate(out, axis=0)
+
+
+def deal(ids_ref, parts, blocks_ref, keep_ref, give_ref):
+    planes = keep_ref.shape[0]
+    group, plane, pair = ids_ref[0], ids_ref[1], ids_ref[2]
+    for turn in range(planes):
+        base = lax.rem(plane + turn, planes) * PAIRS
+        keep_ref[turn] = own_rows(blocks_ref[base + pair], group, parts)
+        give_ref[turn] = own_rows(blocks_ref[base + PAIRS - 1 - pair], group, parts)
+
+
+def deal_kernel(parts, ids_ref, blocks_ref, keep_ref, give_ref):
+    deal(ids_ref, parts, blocks_ref, keep_ref, give_ref)
+
+
+def pair_kernel(keep_ref, take_ref, *out_refs):
+    for turn, out_ref in enumerate(out_refs):
+        out_ref[0] = keep_ref[turn]
+        out_ref[1] = take_ref[turn]
+
+
+def gram_kernel(pieces, ids_ref, scale_ref, *refs):
+    x_refs, (keep_ref, give_ref, gram_ref, blocks_ref) = refs[:pieces], refs[pieces:]
+    count, _, step = blocks_ref.shape
     span = count // pieces
     scale = scale_ref[...]
-    group = group_ref[0]
     gram = None
     for shift in range(pieces):
         normed = (x_refs[shift][...].astype(f32) * scale).astype(bf16)
         term = dot_nt(normed, normed)
         gram = term if gram is None else gram + term
-        start = lax.rem(group + pieces - shift, pieces) * span
+        start = lax.rem(ids_ref[0] + pieces - shift, pieces) * span
         for m in range(span):
-            normed_ref[start + m] = normed[:, m * step : (m + 1) * step]
+            blocks_ref[start + m] = normed[:, m * step : (m + 1) * step]
     gram_ref[...] = gram
+    deal(ids_ref, pieces, blocks_ref, keep_ref, give_ref)
 
 
 def part_kernel(cross, offset, *refs):
@@ -136,7 +195,8 @@
         cross_ref, error_ref = take(2)
         part = part + cross(cross_ref[...], error_ref[0])
     if offset is not None:
-        rows, piece = offset
+        rows, begin, span = offset
+        piece = (begin + pl.program_id(0)) // span
         group_ref, x_ref, t_ref = take(3)
         gap = x_ref[rows].astype(f32) - t_ref[rows].astype(f32)
         part = part + jnp.where(group_ref[0] == piece, gap, 0.0)
@@ -149,7 +209,7 @@
     part_ref, weight_ref, scale_ref = take(3)
     other_refs = take(others)
     match_in = take(1) if matched else []
-    merge_in = take(1) if merged else []
+    merge_in, (ids_ref,) = (take(1), take(1)) if merged else ([], [None])
     chain_in = take(2 if matched else 1) if chained else []
     take(1 if filled else 0)
     tail_in = take(n_tail)
@@ -174,9 +234,10 @@
         query = merge_in[0][0].astype(f32)
         length, cols = scale.shape[0], query.shape[1]
         gap = jnp.zeros((length - query.shape[0], cols), f32)
-        error_ref[0] = jnp.where(
+        both = jnp.where(
             scale > 0.0, jnp.concatenate([scaled, gap], axis=0), jnp.concatenate([gap, query], axis=0)
-        ).astype(bf16)
+        )
+        error_ref[0] = own_rows(both, ids_ref[0], length // error_ref.shape[1]).astype(bf16)
     else:
         error_ref[0] = error
     acc = dot_nt(error, weight_ref[...])
@@ -238,44 +299,42 @@
     out_ref[...] = by_head(dot_tn, probs_ref, (grad_ref[...] + extra).astype(bf16)).astype(bf16)
 
 
-def sources(task, members):
-    pairs, cores = PAIRS, CORES
-    planes = members // pairs
-    plane, pair, core = task // (cores * pairs), lax.rem(task // cores, pairs), lax.rem(task, cores)
-    found = [
-        lax.rem(plane + planes - turn, planes) * pairs + lax.rem(pair + flip, pairs)
-        for flip in range(pairs)
+def value_kernel(parts, planes, ids_ref, *refs):
+    cols, refs = refs[:parts], refs[parts:]
+    blocks, (own_ref, sent_ref) = refs[: planes * PAIRS], refs[planes * PAIRS :]
+    group, core = ids_ref[0], ids_ref[3]
+    rows = blocks[0].shape[0] // parts
+    left = [
+        all_rows([c[turn * PAIRS + flip, :rows] for c in cols], group)
+        for flip in range(PAIRS)
         for turn in range(planes)
     ]
-    return found, core
-
-
-def value_kernel(count, task_ref, cols_ref, *refs):
-    blocks, (own_ref, sent_ref) = refs[:count], refs[count:]
-    rows = blocks[0].shape[0]
-    found, core = sources(task_ref[0], count)
-    total = None
-    for slot in range(count):
-        start = pl.multiple_of(found[slot] * rows, rows)
-        term = dot_tn(cols_ref[pl.ds(start, rows), :], blocks[slot][...])
-        total = term if total is None else total + term
+    total = dot_tn(jnp.concatenate(left, axis=0), jnp.concatenate([b[...] for b in blocks], axis=0))
     half = total.shape[0] // CORES
     top, bottom = total[:half], total[half:]
     own_ref[...] = jnp.where(core == 0, top, bottom)
     sent_ref[...] = jnp.where(core == 0, bottom, top).astype(bf16)
 
 
-def output_kernel(count, task_ref, merged_ref, error_ref, *refs):
-    left, tangent, (own_ref, sent_ref) = refs[:count], refs[count : 2 * count], refs[2 * count :]
-    rows, short = left[0].shape[0], tangent[0].shape[0]
-    found, core = sources(task_ref[0], count)
-    total = None
-    for slot in range(count):
-        start = pl.multiple_of(found[slot] * rows, rows)
-        short_start = pl.multiple_of(found[slot] * short, short)
-        term = dot_tn(left[slot][...], merged_ref[pl.ds(start, rows), :])
-        term = term + dot_tn(tangent[slot][...], error_ref[pl.ds(short_start, short), :])
-        total = term if total is None else total + term
+def output_kernel(parts, planes, ids_ref, *refs):
+    refs = list(refs)
+    take = lambda n: [refs.pop(0) for _ in range(n)]
+    count = planes * PAIRS
+    merged, cols, left, tangent = take(parts), take(parts), take(count), take(count)
+    own_ref, sent_ref = refs
+    group, plane, pair, core = [ids_ref[i] for i in range(4)]
+    rows = left[0].shape[0] // parts
+    right = []
+    for flip in range(PAIRS):
+        for turn in range(planes):
+            source = lax.rem(plane + planes - turn, planes) * PAIRS + lax.rem(pair + flip, PAIRS)
+            right.append(all_rows([m[source] for m in merged], group))
+    for flip in range(PAIRS):
+        for turn in range(planes):
+            right.append(all_rows([c[turn * PAIRS + flip, rows:] for c in cols], group))
+    total = dot_tn(
+        jnp.concatenate([b[...] for b in left + tangent], axis=0), jnp.concatenate(right, axis=0)
+    )
     half = total.shape[1] // CORES
     first, second = total[:, :half], total[:, half:]
     own_ref[...] = jnp.where(core == 0, first, second)
@@ -288,15 +347,16 @@
     heads = queries.shape[1] // HD
     width = heads * HD
     low, high = length // 4, length - length // 4
-    lane = wide // CHUNKS
-    group = lax.axis_index("tensor").astype(jnp.int32)
-    here = group.reshape(1)
-    task = lax.axis_index("task").astype(jnp.int32).reshape(1)
     cores, pairs = CORES, PAIRS
+    planes = n_task // (cores * pairs)
+    members = planes * pairs
     smem = pl.BlockSpec(memory_space=pltpu.SMEM)
     vmem = pl.BlockSpec(memory_space=pltpu.VMEM)
-    planes = n_task // (cores * pairs)
-    members = planes * pairs
+    group = lax.axis_index("tensor").astype(jnp.int32)
+    task = lax.axis_index("task").astype(jnp.int32)
+    ids = jnp.stack([group, task // (cores * pairs), (task // cores) % pairs, task % cores])
+    places = [((group - s) % n_tensor).astype(jnp.int32).reshape(1) for s in range(n_tensor)]
+    inputs, splits, ids, places = lax.optimization_barrier((inputs, splits, ids, places))
 
     def over_tensor(value, shift):
         return lax.ppermute(value, "tensor", [(i, (i + shift) % n_tensor) for i in range(n_tensor)])
@@ -320,10 +380,18 @@
     def spread(value):
         groups = [[m * cores + c for m in range(members)] for c in range(cores)]
         moved = lax.all_to_all(value, "task", split_axis=0, concat_axis=0, axis_index_groups=groups, tiled=True)
-        return moved.reshape(members * value.shape[1], value.shape[2])
+        return [moved] + from_others(moved)
+
+    def staged(keep, give):
+        taken = over_task(give, lambda i: i ^ cores)
+        shape = (pairs,) + keep.shape[1:]
+        sent = call(pair_kernel, [Shape(shape, bf16)] * planes)(keep, taken)
+        got = [sent[0]]
+        for turn in range(1, planes):
+            got.append(over_task(sent[turn], lambda i, turn=turn: (i + turn * cores * pairs) % n_task))
+        return got
 
     x_pieces = [inputs] + from_others(inputs)
-    places = [((group - s) % n_tensor).astype(jnp.int32).reshape(1) for s in range(n_tensor)]
     probs, support_weight, query_weight = call(
         probs_kernel,
         [Shape((heads, length, length), bf16), Shape((length, 1), f32), Shape((length, 1), f32)],
@@ -342,6 +410,19 @@
         )
 
     sums = [Shape((length, width), f32), Shape((length, 1), f32)]
+    if n_tensor > 1:
+        last_weight = call(
+            place_copy_kernel, Shape((part_width, width), bf16),
+            grid_spec=spec([w_spec], pl.BlockSpec((part_width, block), lambda i, place: (0, i))),
+        )(places[-1], value_weight)
+    else:
+        last_weight = value_weight
+    out_block = 4 * HD
+    output_weight = call(
+        copy_kernel, Shape((width, wide), bf16), grid=(wide // out_block,),
+        in_specs=[pl.BlockSpec((width, out_block), lambda i: (0, i))],
+        out_specs=pl.BlockSpec((width, out_block), lambda i: (0, i)),
+    )(output_weight)
     acc, square = call(first_piece_kernel, sums, grid_spec=spec([x_spec, w_spec], [cols_spec, one_spec]))(
         places[0], inputs, value_weight
     )
@@ -354,36 +435,40 @@
         functools.partial(upper_kernel, wide),
         [Shape((length, width), bf16), Shape((length, width), bf16), Shape((length, 1), f32)],
         grid_spec=spec(
-            [x_spec, w_spec, cols_spec, one_spec, probs_spec],
+            [x_spec, pl.BlockSpec((part_width, block), lambda i, place: (0, i)), cols_spec, one_spec, probs_spec],
             [cols_spec, cols_spec, one_spec],
             [pltpu.VMEM((length, 1), f32)],
         ),
-    )(places[-1], x_pieces[-1], value_weight, acc, square, probs)
+    )(places[-1], x_pieces[-1], last_weight, acc, square, probs)
 
     step = wide // members
-    steps = lane // step
-    normed, gram = call(
+    shares = [share * members // sum(SHARES) for share in SHARES]
+    starts = [sum(shares[:c]) for c in range(CHUNKS)]
+    span = part_width // step
+    dealt = Shape((planes, length // n_tensor, step), bf16)
+    keep, give, gram = call(
         functools.partial(gram_kernel, n_tensor),
-        [Shape((members, length, step), bf16), Shape((length, length), f32)],
+        [dealt, dealt, Shape((length, length), f32)],
         in_specs=[smem] + [vmem] * (1 + n_tensor),
-    )(here, scale, *x_pieces)
-    normed_cols = spread(normed)
+        scratch_shapes=[pltpu.VMEM((members, length, step), bf16)],
+    )(ids, scale, *x_pieces)
+    normed_cols = staged(keep, give)
 
     def part_of(c, left, rows, cross=None, pair_of=None, error=None, offset=None):
-        ins = [pl.BlockSpec((rows, width), lambda i: (0, 0)), pl.BlockSpec((width, step), lambda i: (0, c * steps + i))]
+        begin = starts[c]
+        ins = [pl.BlockSpec((rows, width), lambda i: (0, 0)), pl.BlockSpec((width, step), lambda i: (0, begin + i))]
         args = [left, output_weight]
         if cross is not None:
-            ins += [whole(pair_of), pl.BlockSpec((1, error.shape[1], step), lambda i: (c * steps + i, 0, 0))]
+            ins += [whole(pair_of), pl.BlockSpec((1, error.shape[1], step), lambda i: (begin + i, 0, 0))]
             args += [pair_of, error]
         if offset is not None:
-            piece, start = c * lane // part_width, c * lane % part_width // step
-            offset = (offset, piece)
-            ins += [smem] + [pl.BlockSpec((length, step), lambda i: (0, start + i))] * 2
-            args += [here, inputs, targets]
+            offset = (offset, begin, span)
+            ins += [smem] + [pl.BlockSpec((length, step), lambda i: (0, (begin + i) % span))] * 2
+            args += [ids, inputs, targets]
         part = call(
             functools.partial(part_kernel, cross, offset),
-            Shape((rows, lane), bf16),
-            grid=(steps,),
+            Shape((rows, shares[c] * step), bf16),
+            grid=(shares[c],),
             in_specs=ins,
             out_specs=pl.BlockSpec((rows, step), lambda i: (0, i)),
         )(*args)
@@ -396,8 +481,8 @@
         for c, (part, others) in enumerate(parts):
             last = c == CHUNKS - 1
             cols = pl.BlockSpec((rows, step), lambda i: (0, i))
-            stack = lambda r, c=c: pl.BlockSpec((1, r, step), lambda i: (c * steps + i, 0, 0))
-            ins = [cols, pl.BlockSpec((width, step), lambda i, c=c: (0, c * steps + i)), whole(weight)]
+            stack = lambda r, c=c: pl.BlockSpec((1, r, step), lambda i: (starts[c] + i, 0, 0))
+            ins = [cols, pl.BlockSpec((width, step), lambda i, c=c: (0, starts[c] + i)), whole(weight)]
             args = [part, output_weight, weight]
             ins += [cols] * len(others)
             args += others
@@ -405,6 +490,9 @@
                 if extra is not None:
                     ins.append(stack(extra.shape[1]))
                     args.append(extra)
+            if merged is not None:
+                ins.append(smem)
+                args.append(ids)
             ins += [whole(a) for a in chain]
             args += chain
             aliases = {}
@@ -413,7 +501,7 @@
                 ins.append(pl.BlockSpec(memory_space=pl.ANY))
                 args.append(errors)
             sums = [Shape((rows, width), f32)] + ([Shape((rows, matches.shape[1]), f32)] if matches is not None else [])
-            out_rows = rows if merged is None else length
+            out_rows = rows if merged is None else length // n_tensor
             outs = [Shape((members, out_rows, step), bf16)]
             out_specs = [stack(out_rows)]
             scratch = []
@@ -434,7 +522,7 @@
                     bool(chain), errors is not None, tail if last else None, n_tail,
                 ),
                 outs,
-                grid=(steps,),
+                grid=(shares[c],),
                 in_specs=ins,
                 out_specs=out_specs,
                 scratch_shapes=scratch,
@@ -456,7 +544,11 @@
             Shape((length - low, high), bf16),
         ],
     )
-    error_0_cols = spread(error_0)
+    dealt = Shape((planes, high // n_tensor, step), bf16)
+    keep, give = call(
+        functools.partial(deal_kernel, n_tensor), [dealt, dealt], in_specs=[smem, vmem]
+    )(ids, error_0)
+    error_0_cols = staged(keep, give)
 
     parts = [part_of(c, next_q, length - low, dot_nn, cross, error_0, slice(low, length)) for c in range(CHUNKS)]
     left_all = gathered(left)
@@ -477,19 +569,24 @@
     right_all = gathered(right)
     merged_cols = spread(merged)
 
+    kept = call(
+        functools.partial(pack_kernel, planes), Shape((members, (length + high) // n_tensor, step), bf16)
+    )(*normed_cols, *error_0_cols)
+    packed = [kept] + from_others(kept)
+
     wide_block = wide // n_task
     own_v, sent_v = call(
-        functools.partial(value_kernel, members),
+        functools.partial(value_kernel, n_tensor, planes),
         [Shape((wide_block, width), f32), Shape((wide_block, width), bf16)],
-        in_specs=[smem] + [vmem] * (1 + members),
+        in_specs=[smem] + [vmem] * (n_tensor + members),
         out_specs=[vmem, vmem],
-    )(task, normed_cols, *right_all)
+    )(ids, *packed, *right_all)
     own_o, sent_o = call(
-        functools.partial(output_kernel, members),
+        functools.partial(output_kernel, n_tensor, planes),
         [Shape((width, wide_block), f32), Shape((width, wide_block), bf16)],
-        in_specs=[smem] + [vmem] * (2 + 2 * members),
+        in_specs=[smem] + [vmem] * (2 * n_tensor + 2 * members),
         out_specs=[vmem, vmem],
-    )(task, merged_cols, error_0_cols, *left_all, *tangent_all)
+    )(ids, *merged_cols, *packed, *left_all, *tangent_all)
     total_value = own_v + over_task(sent_v, lambda i: i ^ 1).astype(f32)
     total_output = own_o + over_task(sent_o, lambda i: i ^ 1).astype(f32)
     return (total_value, total_output)

time: 256 us -> 201 us (0.79)
  waiting for transfers between devices: 99.7 us -> 54.7 us
  starting transfers between devices: 48.6 us -> 74.2 us
  blocking collectives: 24.1 us -> 0 us
  local copies, waits for them, and re-layouts: 32 us -> 18.3 us
  Pallas kernels: 45.9 us -> 48.7 us
    ppermute x23 -> x31, waiting for transfers between devices: 76.1 us -> 34.1 us  [over_task(): return lax.ppermute(value, 'task', [(i, target(i)) for i in range(n_task)])]
    ppermute x23 -> x31, starting transfers between devices: 23.3 us -> 59.8 us  [over_task(): return lax.ppermute(value, 'task', [(i, target(i)) for i in range(n_task)])]
    all_to_all x1 -> x0, blocking collectives: 24.1 us -> none  [spread(): lax.all_to_all(value, 'task', split_axis=0, concat_axis=0, axis_index_gro...]
    unnamed x90 -> x46, local copies, waits for them, and re-layouts: 32 us -> 18.3 us
    ppermute x13 -> x9, starting transfers between devices: 16 us -> 10.2 us  [over_tensor(): lax.ppermute(value, 'tensor', [(i, (i + shift) % n_tensor) for i in range...]
    all_to_all x2 -> x1, starting transfers between devices: 9.34 us -> 4.19 us  [spread(): lax.all_to_all(value, 'task', split_axis=0, concat_axis=0, axis_index_gro...]
    pallas_call x15, Pallas kernels: 20.7 us -> 23.9 us  [the longest x6 12.9 us: part_of(): call(functools.partial(part_kernel, cross, offset), Shape((rows, shares[c...]
    ppermute x13 -> x9, waiting for transfers between devices: 23.6 us -> 20.6 us  [over_tensor(): lax.ppermute(value, 'tensor', [(i, (i + shift) % n_tensor) for i in range...]
  transfers between devices with their start and end apart: 38 -> 41, of which waited for: 21 -> 16; matrix products, arithmetic and copies ran while one was open for 1% -> 1% of each run, Pallas kernels for 16% -> 19%
where the time goes in v2:
time: 201 us; the launch traced here: 200 us
  starting transfers between devices  74.2 us (37%)
  waiting for transfers between devices  54.7 us (27%)
  Pallas kernels  48.7 us (24%)
  local copies, waits for them, and re-layouts  18.3 us (9%)
  other arithmetic  2.26 us (1%)
    ppermute x31, starting transfers between devices, over_task(): return lax.ppermute(value, 'task', [(i, target(i)) for i in range(n_task)])  59.8 us
    ppermute x31, waiting for transfers between devices, over_task(): return lax.ppermute(value, 'task', [(i, target(i)) for i in range(n_task)])  34.1 us
    ppermute x9, waiting for transfers between devices, over_tensor(): lax.ppermute(value, 'tensor', [(i, (i + shift) % n_tensor) for i in range...  20.6 us
    pallas_call x6, Pallas kernels, combine(): call(functools.partial(finish_kernel, row_slice, len(others), matches is...  19.3 us
    unnamed x46, local copies, waits for them, and re-layouts  18.3 us
    pallas_call x6, Pallas kernels, part_of(): call(functools.partial(part_kernel, cross, offset), Shape((rows, shares[c...  12.9 us
    ppermute x9, starting transfers between devices, over_tensor(): lax.ppermute(value, 'tensor', [(i, (i + shift) % n_tensor) for i in range...  10.2 us
    all_to_all x1, starting transfers between devices, spread(): lax.all_to_all(value, 'task', split_axis=0, concat_axis=0, axis_index_gro...  4.19 us
  transfers between devices with their start and end apart: 41, of which 16 were waited for; matrix products, arithmetic and copies ran while one was open for 1% of the time, Pallas kernels for 19%

profile of v2, /device:TPU:0, one launch (start us, length us, event | category | flops | bytes accessed | tf_op | source)
XLA Modules:
  0.0 199.7 jit_solution(13258471227657196513)
XLA Ops:
  0.8 3.0 %collective-permute-start = (bf16[128,2048]{1,0:T(8,128)(2,1)}, bf16[128,2048]{1,0:T(8,128)(2,1)S(1)}, u32[]{:S(2)}, u32[]{:S(2)}) collective-permute-start(bf16[128,2048]{1,0:T(8,128)(2,1)} %refs_5_.1), channel_id=1, source_target_pairs={{0,1},{1,0},{2,3},{3,2},{4,5},{5,4},{6,7},{7,6},{8,9},{9,8},{10,11... | collective-permute-start | bytes 1572872 | tf_op jit(solution)/shard_map/ppermute | solution.py:362
  4.4 3.4 %copy-done = bf16[4096,1024]{1,0:T(8,128)(2,1)S(1)} copy-done((bf16[4096,1024]{1,0:T(8,128)(2,1)S(1)}, bf16[4096,1024]{1,0:T(8,128)(2,1)}, u32[]{:S(2)}) %copy-start) | copy-done | bytes 8388632
  27.1 6.3 %collective-permute-done.6.refs_3_ = bf16[96,2048]{1,0:T(8,128)(2,1)S(1)} collective-permute-done((bf16[96,2048]{1,0:T(8,128)(2,1)S(1)}, bf16[96,2048]{1,0:T(8,128)(2,1)S(1)}, u32[]{:S(2)}, u32[]{:S(2)}) %collective-permute-start.6) | collective-permute-done | bytes 393248 | tf_op jit(solution)/shard_map/ppermute | solution.py:362
  35.8 4.6 %collective-permute-done.5.refs_3_ = bf16[96,2048]{1,0:T(8,128)(2,1)S(1)} collective-permute-done((bf16[96,2048]{1,0:T(8,128)(2,1)S(1)}, bf16[96,2048]{1,0:T(8,128)(2,1)S(1)}, u32[]{:S(2)}, u32[]{:S(2)}) %collective-permute-start.5) | collective-permute-done | bytes 393248 | tf_op jit(solution)/shard_map/ppermute | solution.py:362
  40.4 3.3 %shard_map.96 = (bf16[8,96,512]{2,1,0:T(8,128)(2,1)S(1)}, bf16[128,1024]{1,0:T(8,128)(2,1)S(1)}, bf16[96,1024]{1,0:T(8,128)(2,1)S(1)}, bf16[128,1024]{1,0:T(8,128)(2,1)S(1)}, bf16[96,96]{1,0:T(8,128)(2,1)S(1)}) custom-call(bf16[96,2048]{1,0:T(8,128)(2,1)S(1)} %shard_map.93.refs_0_, ...), custom_call_target="tpu_custom_call", output_to_operand_aliasing={{0}: (5, {})} | custom-call | tf_op jit(solution)/shard_map/pallas_call | solution.py:519
  52.1 6.1 %collective-permute-done.13.refs_3_ = bf16[96,2048]{1,0:T(8,128)(2,1)S(1)} collective-permute-done((bf16[96,2048]{1,0:T(8,128)(2,1)S(1)}, bf16[96,2048]{1,0:T(8,128)(2,1)S(1)}, u32[]{:S(2)}, u32[]{:S(2)}) %collective-permute-start.13) | collective-permute-done | bytes 393248 | tf_op jit(solution)/shard_map/ppermute | solution.py:362
  60.7 3.6 %collective-permute-done.12.refs_3_ = bf16[96,2048]{1,0:T(8,128)(2,1)S(1)} collective-permute-done((bf16[96,2048]{1,0:T(8,128)(2,1)S(1)}, bf16[96,2048]{1,0:T(8,128)(2,1)S(1)}, u32[]{:S(2)}, u32[]{:S(2)}) %collective-permute-start.12) | collective-permute-done | bytes 393248 | tf_op jit(solution)/shard_map/ppermute | solution.py:362
  64.3 3.5 %shard_map.103 = (bf16[8,96,512]{2,1,0:T(8,128)(2,1)S(1)}, bf16[96,1024]{1,0:T(8,128)(2,1)S(1)}, f32[128,1024]{1,0:T(8,128)S(1)}) custom-call(bf16[96,2048]{1,0:T(8,128)(2,1)S(1)} %shard_map.100.refs_0_, bf16[1024,4096]{1,0:T(8,128)(2,1)S(1)} %shard_map.92.refs_1_, f32[128,1]{1,0:T(8,128)S(1)} %get-tuple-element.79.refs_2_, ...), custom_call_target="tpu_custom_call", output_to_operand_aliasing={{0}: (7, {})} | custom-call | tf_op jit(solution)/shard_map/pallas_call | solution.py:519
  80.2 3.5 %collective-permute-start.4 = (bf16[2,64,512]{2,1,0:T(8,128)(2,1)S(1)}, bf16[2,64,512]{2,1,0:T(8,128)(2,1)S(1)}, u32[]{:S(2)}, u32[]{:S(2)}) collective-permute-start(bf16[2,64,512]{2,1,0:T(8,128)(2,1)S(1)} %get-tuple-element.63), channel_id=1, source_target_pairs={{0,24},{2,26},{4,28},{6,30},{8,0},{10,2},{12,4},{14,6},{16,8},{18,... | collective-permute-start | bytes 393224 | tf_op jit(solution)/shard_map/ppermute | solution.py:368
  88.2 4.0 %collective-permute-start.8 = (bf16[2,48,512]{2,1,0:T(8,128)(2,1)S(1)}, bf16[2,48,512]{2,1,0:T(8,128)(2,1)S(1)}, u32[]{:S(2)}, u32[]{:S(2)}) collective-permute-start(bf16[2,48,512]{2,1,0:T(8,128)(2,1)S(1)} %get-tuple-element.74), channel_id=1, source_target_pairs={{0,8},{2,10},{4,12},{6,14},{8,16},{10,18},{12,20},{14,22},{16,24},... | collective-permute-start | bytes 294920 | tf_op jit(solution)/shard_map/ppermute | solution.py:368
  92.2 3.4 %collective-permute-start.9 = (bf16[2,48,512]{2,1,0:T(8,128)(2,1)S(1)}, bf16[2,48,512]{2,1,0:T(8,128)(2,1)S(1)}, u32[]{:S(2)}, u32[]{:S(2)}) collective-permute-start(bf16[2,48,512]{2,1,0:T(8,128)(2,1)S(1)} %get-tuple-element.75), channel_id=1, source_target_pairs={{0,16},{2,18},{4,20},{6,22},{8,24},{10,26},{12,28},{14,30},{16,0},... | collective-permute-start | bytes 294920 | tf_op jit(solution)/shard_map/ppermute | solution.py:368
  95.6 3.6 %shard_map.106 = (bf16[8,64,512]{2,1,0:T(8,128)(2,1)}, f32[96,1024]{1,0:T(8,128)S(1)}) custom-call(bf16[96,2048]{1,0:T(8,128)(2,1)S(1)} %shard_map.105.refs_0_, bf16[1024,4096]{1,0:T(8,128)(2,1)S(1)} %shard_map.92.refs_1_, f32[128,1]{1,0:T(8,128)S(1)} %get-tuple-element.65.refs_2_.refs_10_, bf16[96,2048]{1,0:T(8,128)(2,1)S(1)} %collective-permute-done.15.refs_3_, ...), custom_call_target="tpu_custom_call" | custom-call | tf_op jit(solution)/shard_map/pallas_call | solution.py:519
  100.6 3.9 %shard_map.107 = (bf16[8,64,512]{2,1,0:T(8,128)(2,1)}, bf16[128,1024]{1,0:T(8,128)(2,1)S(1)}) custom-call(bf16[96,2048]{1,0:T(8,128)(2,1)S(1)} %shard_map.104.refs_0_, bf16[1024,4096]{1,0:T(8,128)(2,1)S(1)} %shard_map.92.refs_1_, f32[128,1]{1,0:T(8,128)S(1)} %get-tuple-element.65.refs_2_.refs_10_, ...), custom_call_target="tpu_custom_call", output_to_operand_aliasing={{0}: (7, {})} | custom-call | tf_op jit(solution)/shard_map/pallas_call | solution.py:519
  104.5 4.2 %all-to-all-start = ((bf16[8,64,512]{2,1,0:T(8,128)(2,1)}), bf16[8,64,512]{2,1,0:T(8,128)(2,1)S(1)}, u32[]{:S(2)}, u32[]{:S(2)}) async-start(bf16[8,64,512]{2,1,0:T(8,128)(2,1)} %get-tuple-element.92), calls=%async_computation | async-start | bytes 1048576 | tf_op jit(solution)/shard_map/all_to_all | solution.py:382
  115.7 5.6 %collective-permute-done.26.refs_6_ = bf16[128,1024]{1,0:T(8,128)(2,1)} collective-permute-done((bf16[128,1024]{1,0:T(8,128)(2,1)S(1)}, bf16[128,1024]{1,0:T(8,128)(2,1)}, u32[]{:S(2)}, u32[]{:S(2)}) %collective-permute-start.26) | collective-permute-done | bytes 262176 | tf_op jit(solution)/shard_map/ppermute | solution.py:368
  122.6 5.6 %collective-permute-start.31 = (bf16[128,1024]{1,0:T(8,128)(2,1)S(1)}, bf16[128,1024]{1,0:T(8,128)(2,1)S(1)}, u32[]{:S(2)}, u32[]{:S(2)}) collective-permute-start(bf16[128,1024]{1,0:T(8,128)(2,1)S(1)} %collective-permute-done.27.refs_7_), channel_id=1, source_target_pairs={{0,4},{2,6},{4,0},{6,2},{8,12},{10,14},{12,8},{14,10},{16,20},{18,... | collective-permute-start | bytes 786440 | tf_op jit(solution)/shard_map/ppermute | solution.py:368
  129.6 6.8 %collective-permute-start.16 = (bf16[128,1024]{1,0:T(8,128)(2,1)S(1)}, bf16[128,1024]{1,0:T(8,128)(2,1)S(1)}, u32[]{:S(2)}, u32[]{:S(2)}) collective-permute-start(bf16[128,1024]{1,0:T(8,128)(2,1)S(1)} %get-tuple-element.89.refs_2_), channel_id=1, source_target_pairs={{0,8},{2,10},{4,12},{6,14},{8,16},{10,18},{12,20},{14,22},{16,24},... | collective-permute-start | bytes 786440 | tf_op jit(solution)/shard_map/ppermute | solution.py:368
  143.1 6.6 %collective-permute-done.17.refs_4_ = bf16[128,1024]{1,0:T(8,128)(2,1)S(1)} collective-permute-done((bf16[128,1024]{1,0:T(8,128)(2,1)S(1)}, bf16[128,1024]{1,0:T(8,128)(2,1)S(1)}, u32[]{:S(2)}, u32[]{:S(2)}) %collective-permute-start.17) | collective-permute-done | bytes 262176 | tf_op jit(solution)/shard_map/ppermute | solution.py:368
  152.8 5.3 %collective-permute-start.32 = (bf16[96,1024]{1,0:T(8,128)(2,1)S(1)}, bf16[96,1024]{1,0:T(8,128)(2,1)S(1)}, u32[]{:S(2)}, u32[]{:S(2)}) collective-permute-start(bf16[96,1024]{1,0:T(8,128)(2,1)S(1)} %get-tuple-element.84.refs_0_.refs_12_), channel_id=1, source_target_pairs={{0,8},{2,10},{4,12},{6,14},{8,16},{10,18},{12,20},{14,22},{16,24},... | collective-permute-start | bytes 589832 | tf_op jit(solution)/shard_map/ppermute | solution.py:368
  158.1 4.0 %collective-permute-start.33 = (bf16[96,1024]{1,0:T(8,128)(2,1)S(1)}, bf16[96,1024]{1,0:T(8,128)(2,1)S(1)}, u32[]{:S(2)}, u32[]{:S(2)}) collective-permute-start(bf16[96,1024]{1,0:T(8,128)(2,1)S(1)} %get-tuple-element.84.refs_0_.refs_12_), channel_id=1, source_target_pairs={{0,16},{2,18},{4,20},{6,22},{8,24},{10,26},{12,28},{14,30},{16,0},... | collective-permute-start | bytes 589832 | tf_op jit(solution)/shard_map/ppermute | solution.py:368
  174.8 4.8 %collective-permute-done.36.refs_17_ = bf16[96,1024]{1,0:T(8,128)(2,1)S(1)} collective-permute-done((bf16[96,1024]{1,0:T(8,128)(2,1)S(1)}, bf16[96,1024]{1,0:T(8,128)(2,1)S(1)}, u32[]{:S(2)}, u32[]{:S(2)}) %collective-permute-start.36) | collective-permute-done | bytes 196640 | tf_op jit(solution)/shard_map/ppermute | solution.py:368
  179.6 4.2 %collective-permute-done.37.refs_18_ = bf16[96,1024]{1,0:T(8,128)(2,1)S(1)} collective-permute-done((bf16[96,1024]{1,0:T(8,128)(2,1)S(1)}, bf16[96,1024]{1,0:T(8,128)(2,1)S(1)}, u32[]{:S(2)}, u32[]{:S(2)}) %collective-permute-start.37) | collective-permute-done | bytes 196640 | tf_op jit(solution)/shard_map/ppermute | solution.py:368
  183.8 3.2 %collective-permute-done.38.refs_19_ = bf16[96,1024]{1,0:T(8,128)(2,1)S(1)} collective-permute-done((bf16[96,1024]{1,0:T(8,128)(2,1)S(1)}, bf16[96,1024]{1,0:T(8,128)(2,1)S(1)}, u32[]{:S(2)}, u32[]{:S(2)}) %collective-permute-start.38) | collective-permute-done | bytes 196640 | tf_op jit(solution)/shard_map/ppermute | solution.py:368
  193.6 3.1 %shard_map.109 = (f32[1024,256]{1,0:T(8,128)S(1)}, bf16[1024,256]{1,0:T(8,128)(2,1)S(1)}) custom-call(s32[4]{0:T(128)S(1)} %pad_add_fusion.ids_ref.refs_2_.refs_4_.refs_5_, bf16[8,64,512]{2,1,0:T(8,128)(2,1)S(1)} %all-to-all-done.refs_0_, bf16[8,64,512]{2,1,0:T(8,128)(2,1)S(1)} %collective-permute-done.24.refs_1_, ...), custom_call_target="tpu_custom_call" | custom-call | tf_op jit(solution)/shard_map/pallas_call | solution.py:584
  (131 shorter events, 92.6 us)
Async XLA Ops:
  0.8 15.5 %collective-permute-start = (bf16[128,2048]{1,0:T(8,128)(2,1)}, bf16[128,2048]{1,0:T(8,128)(2,1)S(1)}, u32[]{:S(2)}, u32[]{:S(2)}) collective-permute-start(bf16[128,2048]{1,0:T(8,128)(2,1)} %refs_5_.1), channel_id=1, source_target_pairs={{0,1},{1,0},{2,3},{3,2},{4,5},{5,4},{6,7},{7,6},{8,9},{9,8},{10,11... | collective-permute-start | bytes 1572872 | tf_op jit(solution)/shard_map/ppermute | solution.py:362
  25.0 15.4 %collective-permute-start.5 = (bf16[96,2048]{1,0:T(8,128)(2,1)S(1)}, bf16[96,2048]{1,0:T(8,128)(2,1)S(1)}, u32[]{:S(2)}, u32[]{:S(2)}) collective-permute-start(bf16[96,2048]{1,0:T(8,128)(2,1)S(1)} %shard_map.93.refs_0_), channel_id=1, source_target_pairs={{0,1},{1,0},{2,3},{3,2},{4,5},{5,4},{6,7},{7,6},{8,9},{9,8},{10,11... | collective-permute-start | bytes 1179656 | tf_op jit(solution)/shard_map/ppermute | solution.py:362
  49.3 15.0 %collective-permute-start.12 = (bf16[96,2048]{1,0:T(8,128)(2,1)S(1)}, bf16[96,2048]{1,0:T(8,128)(2,1)S(1)}, u32[]{:S(2)}, u32[]{:S(2)}) collective-permute-start(bf16[96,2048]{1,0:T(8,128)(2,1)S(1)} %shard_map.100.refs_0_), channel_id=1, source_target_pairs={{0,1},{1,0},{2,3},{3,2},{4,5},{5,4},{6,7},{7,6},{8,9},{9,8},{10,11... | collective-permute-start | bytes 1179656 | tf_op jit(solution)/shard_map/ppermute | solution.py:362
  50.6 25.4 %collective-permute-start.1 = (bf16[4,64,512]{2,1,0:T(8,128)(2,1)S(1)}, bf16[4,64,512]{2,1,0:T(8,128)(2,1)S(1)}, u32[]{:S(2)}, u32[]{:S(2)}) collective-permute-start(bf16[4,64,512]{2,1,0:T(8,128)(2,1)S(1)} %get-tuple-element.59), channel_id=1, source_target_pairs={{0,4},{2,6},{4,0},{6,2},{8,12},{10,14},{12,8},{14,10},{16,20},{18,... | collective-permute-start | bytes 786440 | tf_op jit(solution)/shard_map/ppermute | solution.py:368
  69.7 22.4 %collective-permute-start.15 = (bf16[96,2048]{1,0:T(8,128)(2,1)S(1)}, bf16[96,2048]{1,0:T(8,128)(2,1)S(1)}, u32[]{:S(2)}, u32[]{:S(2)}) collective-permute-start(bf16[96,2048]{1,0:T(8,128)(2,1)S(1)} %shard_map.105.refs_0_), channel_id=1, source_target_pairs={{0,1},{1,0},{2,3},{3,2},{4,5},{5,4},{6,7},{7,6},{8,9},{9,8},{10,11... | collective-permute-start | bytes 1179656 | tf_op jit(solution)/shard_map/ppermute | solution.py:362
  72.0 28.6 %collective-permute-start.14 = (bf16[96,2048]{1,0:T(8,128)(2,1)S(1)}, bf16[96,2048]{1,0:T(8,128)(2,1)S(1)}, u32[]{:S(2)}, u32[]{:S(2)}) collective-permute-start(bf16[96,2048]{1,0:T(8,128)(2,1)S(1)} %shard_map.104.refs_0_), channel_id=1, source_target_pairs={{0,1},{1,0},{2,3},{3,2},{4,5},{5,4},{6,7},{7,6},{8,9},{9,8},{10,11... | collective-permute-start | bytes 1179656 | tf_op jit(solution)/shard_map/ppermute | solution.py:362
  80.2 18.9 %collective-permute-start.4 = (bf16[2,64,512]{2,1,0:T(8,128)(2,1)S(1)}, bf16[2,64,512]{2,1,0:T(8,128)(2,1)S(1)}, u32[]{:S(2)}, u32[]{:S(2)}) collective-permute-start(bf16[2,64,512]{2,1,0:T(8,128)(2,1)S(1)} %get-tuple-element.63), channel_id=1, source_target_pairs={{0,24},{2,26},{4,28},{6,30},{8,0},{10,2},{12,4},{14,6},{16,8},{18,... | collective-permute-start | bytes 393224 | tf_op jit(solution)/shard_map/ppermute | solution.py:368
  84.2 24.4 %collective-permute-start.10 = (bf16[2,48,512]{2,1,0:T(8,128)(2,1)S(1)}, bf16[2,48,512]{2,1,0:T(8,128)(2,1)S(1)}, u32[]{:S(2)}, u32[]{:S(2)}) collective-permute-start(bf16[2,48,512]{2,1,0:T(8,128)(2,1)S(1)} %get-tuple-element.76), channel_id=1, source_target_pairs={{0,24},{2,26},{4,28},{6,30},{8,0},{10,2},{12,4},{14,6},{16,8},{18,... | collective-permute-start | bytes 294920 | tf_op jit(solution)/shard_map/ppermute | solution.py:368
  88.2 20.5 %collective-permute-start.8 = (bf16[2,48,512]{2,1,0:T(8,128)(2,1)S(1)}, bf16[2,48,512]{2,1,0:T(8,128)(2,1)S(1)}, u32[]{:S(2)}, u32[]{:S(2)}) collective-permute-start(bf16[2,48,512]{2,1,0:T(8,128)(2,1)S(1)} %get-tuple-element.74), channel_id=1, source_target_pairs={{0,8},{2,10},{4,12},{6,14},{8,16},{10,18},{12,20},{14,22},{16,24},... | collective-permute-start | bytes 294920 | tf_op jit(solution)/shard_map/ppermute | solution.py:368
  92.2 17.5 %collective-permute-start.9 = (bf16[2,48,512]{2,1,0:T(8,128)(2,1)S(1)}, bf16[2,48,512]{2,1,0:T(8,128)(2,1)S(1)}, u32[]{:S(2)}, u32[]{:S(2)}) collective-permute-start(bf16[2,48,512]{2,1,0:T(8,128)(2,1)S(1)} %get-tuple-element.75), channel_id=1, source_target_pairs={{0,16},{2,18},{4,20},{6,22},{8,24},{10,26},{12,28},{14,30},{16,0},... | collective-permute-start | bytes 294920 | tf_op jit(solution)/shard_map/ppermute | solution.py:368
  99.1 15.3 %collective-permute-start.25 = (bf16[128,1024]{1,0:T(8,128)(2,1)S(1)}, bf16[128,1024]{1,0:T(8,128)(2,1)S(1)}, u32[]{:S(2)}, u32[]{:S(2)}) collective-permute-start(bf16[128,1024]{1,0:T(8,128)(2,1)S(1)} %get-tuple-element.93.refs_4_), channel_id=1, source_target_pairs={{0,8},{2,10},{4,12},{6,14},{8,16},{10,18},{12,20},{14,22},{16,24},... | collective-permute-start | bytes 786440 | tf_op jit(solution)/shard_map/ppermute | solution.py:368
  100.6 20.8 %collective-permute-start.26 = (bf16[128,1024]{1,0:T(8,128)(2,1)S(1)}, bf16[128,1024]{1,0:T(8,128)(2,1)}, u32[]{:S(2)}, u32[]{:S(2)}) collective-permute-start(bf16[128,1024]{1,0:T(8,128)(2,1)S(1)} %get-tuple-element.93.refs_4_), channel_id=1, source_target_pairs={{0,16},{2,18},{4,20},{6,22},{8,24},{10,26},{12,28},{14,30},{16,0},... | collective-permute-start | bytes 786440 | tf_op jit(solution)/shard_map/ppermute | solution.py:368
  104.5 47.9 %all-to-all-start = ((bf16[8,64,512]{2,1,0:T(8,128)(2,1)}), bf16[8,64,512]{2,1,0:T(8,128)(2,1)S(1)}, u32[]{:S(2)}, u32[]{:S(2)}) async-start(bf16[8,64,512]{2,1,0:T(8,128)(2,1)} %get-tuple-element.92), calls=%async_computation | async-start | bytes 1048576 | tf_op jit(solution)/shard_map/all_to_all | solution.py:382
  109.7 43.1 %collective-permute-start.11 = (bf16[8,112,512]{2,1,0:T(8,128)(2,1)S(1)}, bf16[8,112,512]{2,1,0:T(8,128)(2,1)S(1)}, u32[]{:S(2)}, u32[]{:S(2)}) collective-permute-start(bf16[8,112,512]{2,1,0:T(8,128)(2,1)S(1)} %shard_map.99.refs_0_.refs_2_), channel_id=1, source_target_pairs={{0,1},{1,0},{2,3},{3,2},{4,5},{5,4},{6,7},{7,6},{8,9},{9,8},{10,11... | collective-permute-start | bytes 2752520 | tf_op jit(solution)/shard_map/ppermute | solution.py:362
  113.0 15.9 %collective-permute-start.28 = (bf16[128,1024]{1,0:T(8,128)(2,1)S(1)}, bf16[128,1024]{1,0:T(8,128)(2,1)S(1)}, u32[]{:S(2)}, u32[]{:S(2)}) collective-permute-start(bf16[128,1024]{1,0:T(8,128)(2,1)S(1)} %get-tuple-element.93.refs_4_), channel_id=1, source_target_pairs={{0,4},{2,6},{4,0},{6,2},{8,12},{10,14},{12,8},{14,10},{16,20},{18,... | collective-permute-start | bytes 786440 | tf_op jit(solution)/shard_map/ppermute | solution.py:368
  114.4 21.9 %collective-permute-start.29 = (bf16[128,1024]{1,0:T(8,128)(2,1)S(1)}, bf16[128,1024]{1,0:T(8,128)(2,1)S(1)}, u32[]{:S(2)}, u32[]{:S(2)}) collective-permute-start(bf16[128,1024]{1,0:T(8,128)(2,1)S(1)} %collective-permute-done.25.refs_5_), channel_id=1, source_target_pairs={{0,4},{2,6},{4,0},{6,2},{8,12},{10,14},{12,8},{14,10},{16,20},{18,... | collective-permute-start | bytes 786440 | tf_op jit(solution)/shard_map/ppermute | solution.py:368
  121.3 15.7 %collective-permute-start.30 = (bf16[128,1024]{1,0:T(8,128)(2,1)}, bf16[128,1024]{1,0:T(8,128)(2,1)S(1)}, u32[]{:S(2)}, u32[]{:S(2)}) collective-permute-start(bf16[128,1024]{1,0:T(8,128)(2,1)} %collective-permute-done.26.refs_6_), channel_id=1, source_target_pairs={{0,4},{2,6},{4,0},{6,2},{8,12},{10,14},{12,8},{14,10},{16,20},{18,... | collective-permute-start | bytes 786440 | tf_op jit(solution)/shard_map/ppermute | solution.py:368
  122.6 17.6 %collective-permute-start.31 = (bf16[128,1024]{1,0:T(8,128)(2,1)S(1)}, bf16[128,1024]{1,0:T(8,128)(2,1)S(1)}, u32[]{:S(2)}, u32[]{:S(2)}) collective-permute-start(bf16[128,1024]{1,0:T(8,128)(2,1)S(1)} %collective-permute-done.27.refs_7_), channel_id=1, source_target_pairs={{0,4},{2,6},{4,0},{6,2},{8,12},{10,14},{12,8},{14,10},{16,20},{18,... | collective-permute-start | bytes 786440 | tf_op jit(solution)/shard_map/ppermute | solution.py:368
  143.1 15.1 %collective-permute-start.20 = (bf16[128,1024]{1,0:T(8,128)(2,1)S(1)}, bf16[128,1024]{1,0:T(8,128)(2,1)}, u32[]{:S(2)}, u32[]{:S(2)}) collective-permute-start(bf16[128,1024]{1,0:T(8,128)(2,1)S(1)} %collective-permute-done.16.refs_3_), channel_id=1, source_target_pairs={{0,4},{2,6},{4,0},{6,2},{8,12},{10,14},{12,8},{14,10},{16,20},{18,... | collective-permute-start | bytes 786440 | tf_op jit(solution)/shard_map/ppermute | solution.py:368
  149.7 15.2 %collective-permute-start.22 = (bf16[128,1024]{1,0:T(8,128)(2,1)}, bf16[128,1024]{1,0:T(8,128)(2,1)}, u32[]{:S(2)}, u32[]{:S(2)}) collective-permute-start(bf16[128,1024]{1,0:T(8,128)(2,1)} %collective-permute-done.18.refs_5_), channel_id=1, source_target_pairs={{0,4},{2,6},{4,0},{6,2},{8,12},{10,14},{12,8},{14,10},{16,20},{18,... | collective-permute-start | bytes 786440 | tf_op jit(solution)/shard_map/ppermute | solution.py:368
  152.4 34.5 %collective-permute-start.24 = (bf16[8,64,512]{2,1,0:T(8,128)(2,1)S(1)}, bf16[8,64,512]{2,1,0:T(8,128)(2,1)S(1)}, u32[]{:S(2)}, u32[]{:S(2)}) collective-permute-start(bf16[8,64,512]{2,1,0:T(8,128)(2,1)S(1)} %all-to-all-done.refs_0_), channel_id=1, source_target_pairs={{0,1},{1,0},{2,3},{3,2},{4,5},{5,4},{6,7},{7,6},{8,9},{9,8},{10,11... | collective-permute-start | bytes 1572872 | tf_op jit(solution)/shard_map/ppermute | solution.py:362
  152.8 17.0 %collective-permute-start.32 = (bf16[96,1024]{1,0:T(8,128)(2,1)S(1)}, bf16[96,1024]{1,0:T(8,128)(2,1)S(1)}, u32[]{:S(2)}, u32[]{:S(2)}) collective-permute-start(bf16[96,1024]{1,0:T(8,128)(2,1)S(1)} %get-tuple-element.84.refs_0_.refs_12_), channel_id=1, source_target_pairs={{0,8},{2,10},{4,12},{6,14},{8,16},{10,18},{12,20},{14,22},{16,24},... | collective-permute-start | bytes 589832 | tf_op jit(solution)/shard_map/ppermute | solution.py:368
  158.1 13.7 %collective-permute-start.33 = (bf16[96,1024]{1,0:T(8,128)(2,1)S(1)}, bf16[96,1024]{1,0:T(8,128)(2,1)S(1)}, u32[]{:S(2)}, u32[]{:S(2)}) collective-permute-start(bf16[96,1024]{1,0:T(8,128)(2,1)S(1)} %get-tuple-element.84.refs_0_.refs_12_), channel_id=1, source_target_pairs={{0,16},{2,18},{4,20},{6,22},{8,24},{10,26},{12,28},{14,30},{16,0},... | collective-permute-start | bytes 589832 | tf_op jit(solution)/shard_map/ppermute | solution.py:368
  169.8 27.0 %collective-permute-start.23 = (bf16[256,1024]{1,0:T(8,128)(2,1)S(1)}, bf16[256,1024]{1,0:T(8,128)(2,1)S(1)}, u32[]{:S(2)}, u32[]{:S(2)}) collective-permute-start(bf16[256,1024]{1,0:T(8,128)(2,1)S(1)} %get-tuple-element.91), channel_id=1, source_target_pairs={{0,2},{2,0},{4,6},{6,4},{8,10},{10,8},{12,14},{14,12},{16,18},{18,... | collective-permute-start | bytes 1572872 | tf_op jit(solution)/shard_map/ppermute | solution.py:368
  (40 other events, 283.2 us)

commit v3 on v2

--- a/solution.py
+++ b/solution.py
@@ -11,8 +11,9 @@
 HD = 128
 RATE = 0.25
 CORES = 2
+TASK, TENSOR = "task", "tensor"
 PAIRS = 2
-SHARES = (4, 4)
+SHARES = (2, 3, 3)
 CHUNKS = len(SHARES)
 VMEM_LIMIT = 16 * 1024 * 1024
 
@@ -92,14 +93,30 @@
     out_ref[...] = source_ref[...]
 
 
-def pack_kernel(count, *refs):
+def flips_kernel(*refs):
+    out_refs = refs[-PAIRS:]
+    for turn, ref in enumerate(refs[:-PAIRS]):
+        for flip in range(PAIRS):
+            out_refs[flip][turn] = ref[flip]
+
+
+def sides_kernel(ids_ref, *refs):
+    keep_ref, give_ref = refs[-2:]
+    pair = ids_ref[2]
+    for turn, ref in enumerate(refs[:-2]):
+        keep_ref[turn] = ref[pair]
+        give_ref[turn] = ref[PAIRS - 1 - pair]
+
+
+def stack_kernel(count, *refs):
     out_ref = refs[-1]
-    for turn in range(count):
-        first, second = refs[turn], refs[count + turn]
-        rows = first.shape[1]
-        for flip in range(PAIRS):
-            out_ref[turn * PAIRS + flip, :rows] = first[flip]
-            out_ref[turn * PAIRS + flip, rows:] = second[flip]
+    for flip in range(PAIRS):
+        start = 0
+        for piece in refs[flip:-1:PAIRS]:
+            rows = piece.shape[1]
+            for turn in range(count):
+                out_ref[turn * PAIRS + flip, start : start + rows] = piece[turn]
+            start += rows
 
 
 def row_squares(value):
@@ -159,8 +176,13 @@
         give_ref[turn] = own_rows(blocks_ref[base + PAIRS - 1 - pair], group, parts)
 
 
-def deal_kernel(parts, ids_ref, blocks_ref, keep_ref, give_ref):
-    deal(ids_ref, parts, blocks_ref, keep_ref, give_ref)
+def deal_kernel(parts, ids_ref, blocks_ref, *out_refs):
+    planes = len(out_refs)
+    group, plane = ids_ref[0], ids_ref[1]
+    for turn, out_ref in enumerate(out_refs):
+        base = lax.rem(plane + turn, planes) * PAIRS
+        for flip in range(PAIRS):
+            out_ref[flip] = own_rows(blocks_ref[base + flip], group, parts)
 
 
 def pair_kernel(keep_ref, take_ref, *out_refs):
@@ -209,7 +231,7 @@
     part_ref, weight_ref, scale_ref = take(3)
     other_refs = take(others)
     match_in = take(1) if matched else []
-    merge_in, (ids_ref,) = (take(1), take(1)) if merged else ([], [None])
+    merge_in = take(1) if merged else []
     chain_in = take(2 if matched else 1) if chained else []
     take(1 if filled else 0)
     tail_in = take(n_tail)
@@ -237,7 +259,7 @@
         both = jnp.where(
             scale > 0.0, jnp.concatenate([scaled, gap], axis=0), jnp.concatenate([gap, query], axis=0)
         )
-        error_ref[0] = own_rows(both, ids_ref[0], length // error_ref.shape[1]).astype(bf16)
+        error_ref[0] = both.astype(bf16)
     else:
         error_ref[0] = error
     acc = dot_nt(error, weight_ref[...])
@@ -303,11 +325,8 @@
     cols, refs = refs[:parts], refs[parts:]
     blocks, (own_ref, sent_ref) = refs[: planes * PAIRS], refs[planes * PAIRS :]
     group, core = ids_ref[0], ids_ref[3]
-    rows = blocks[0].shape[0] // parts
     left = [
-        all_rows([c[turn * PAIRS + flip, :rows] for c in cols], group)
-        for flip in range(PAIRS)
-        for turn in range(planes)
+        all_rows([c[turn * PAIRS + flip] for c in cols], group) for flip in range(PAIRS) for turn in range(planes)
     ]
     total = dot_tn(jnp.concatenate(left, axis=0), jnp.concatenate([b[...] for b in blocks], axis=0))
     half = total.shape[0] // CORES
@@ -320,18 +339,12 @@
     refs = list(refs)
     take = lambda n: [refs.pop(0) for _ in range(n)]
     count = planes * PAIRS
-    merged, cols, left, tangent = take(parts), take(parts), take(count), take(count)
+    merged, error, left, tangent = take(PAIRS * parts), take(parts), take(count), take(count)
     own_ref, sent_ref = refs
-    group, plane, pair, core = [ids_ref[i] for i in range(4)]
-    rows = left[0].shape[0] // parts
-    right = []
-    for flip in range(PAIRS):
-        for turn in range(planes):
-            source = lax.rem(plane + planes - turn, planes) * PAIRS + lax.rem(pair + flip, PAIRS)
-            right.append(all_rows([m[source] for m in merged], group))
-    for flip in range(PAIRS):
-        for turn in range(planes):
-            right.append(all_rows([c[turn * PAIRS + flip, rows:] for c in cols], group))
+    group, core = ids_ref[0], ids_ref[3]
+    slots = [(turn, flip) for flip in range(PAIRS) for turn in range(planes)]
+    right = [all_rows([merged[flip * parts + p][turn] for p in range(parts)], group) for turn, flip in slots]
+    right += [all_rows([e[turn * PAIRS + flip] for e in error], group) for turn, flip in slots]
     total = dot_tn(
         jnp.concatenate([b[...] for b in left + tangent], axis=0), jnp.concatenate(right, axis=0)
     )
@@ -352,44 +365,60 @@
     members = planes * pairs
     smem = pl.BlockSpec(memory_space=pltpu.SMEM)
     vmem = pl.BlockSpec(memory_space=pltpu.VMEM)
-    group = lax.axis_index("tensor").astype(jnp.int32)
-    task = lax.axis_index("task").astype(jnp.int32)
+    group = lax.axis_index(TENSOR).astype(jnp.int32)
+    task = lax.axis_index(TASK).astype(jnp.int32)
     ids = jnp.stack([group, task // (cores * pairs), (task // cores) % pairs, task % cores])
     places = [((group - s) % n_tensor).astype(jnp.int32).reshape(1) for s in range(n_tensor)]
     inputs, splits, ids, places = lax.optimization_barrier((inputs, splits, ids, places))
 
     def over_tensor(value, shift):
-        return lax.ppermute(value, "tensor", [(i, (i + shift) % n_tensor) for i in range(n_tensor)])
+        return lax.ppermute(value, TENSOR, [(i, (i + shift) % n_tensor) for i in range(n_tensor)])
 
     def from_others(value):
         return [over_tensor(value, shift) for shift in range(1, n_tensor)]
 
     def over_task(value, target):
-        return lax.ppermute(value, "task", [(i, target(i)) for i in range(n_task)])
-
-    def gathered(value):
-        blocks = [value]
-        for turn in range(1, planes):
-            blocks.append(
-                over_task(value, lambda i, turn=turn: (i + turn * cores * pairs) % n_task)
-            )
-        crossed = [over_task(value, lambda i: i ^ cores)]
-        crossed += [over_task(b, lambda i: i ^ cores) for b in blocks[1:]]
+        return lax.ppermute(value, TASK, [(i, target(i)) for i in range(n_task)])
+
+    def turned(value, turn):
+        return over_task(value, lambda i: (i + turn * cores * pairs) % n_task)
+
+    def ring(value, both_ways):
+        blocks, rounds = [value] + [None] * (planes - 1), [0] * planes
+        reach = planes // 2 if both_ways else planes - 1
+        for turn in range(1, reach + 1):
+            rounds[turn] = min(turn, 3)
+            blocks[turn] = turned(blocks[turn - 1], 1)
+        for turn in range(planes - 1, reach, -1):
+            rounds[turn] = min(planes - turn, 3)
+            blocks[turn] = turned(blocks[(turn + 1) % planes], planes - 1)
+        crossed = []
+        for turn in range(planes):
+            crossed.append(over_task(blocks[turn], lambda i: i ^ cores))
         return blocks + crossed
 
-    def spread(value):
-        groups = [[m * cores + c for m in range(members)] for c in range(cores)]
-        moved = lax.all_to_all(value, "task", split_axis=0, concat_axis=0, axis_index_groups=groups, tiled=True)
-        return [moved] + from_others(moved)
+    def dealt_out(blocks):
+        shape = Shape((pairs, blocks.shape[1] // n_tensor, blocks.shape[2]), bf16)
+        sent = call(
+            functools.partial(deal_kernel, n_tensor), [shape] * planes, in_specs=[smem, vmem]
+        )(ids, blocks)
+        return [sent[0]] + [turned(sent[turn], turn) for turn in range(1, planes)]
+
+    def sides(got):
+        shape = Shape((planes,) + got[0].shape[1:], bf16)
+        keep, give = call(sides_kernel, [shape] * 2, in_specs=[smem] + [vmem] * planes)(ids, *got)
+        return keep, over_task(give, lambda i: i ^ cores)
+
+    def stacked(flips):
+        shape = Shape((members,) + flips[0].shape[1:], bf16)
+        kept = call(functools.partial(stack_kernel, planes), shape)(*flips)
+        return [kept] + from_others(kept)
 
     def staged(keep, give):
         taken = over_task(give, lambda i: i ^ cores)
         shape = (pairs,) + keep.shape[1:]
         sent = call(pair_kernel, [Shape(shape, bf16)] * planes)(keep, taken)
-        got = [sent[0]]
-        for turn in range(1, planes):
-            got.append(over_task(sent[turn], lambda i, turn=turn: (i + turn * cores * pairs) % n_task))
-        return got
+        return [sent[0]] + [turned(sent[turn], turn) for turn in range(1, planes)]
 
     x_pieces = [inputs] + from_others(inputs)
     probs, support_weight, query_weight = call(
@@ -452,7 +481,9 @@
         in_specs=[smem] + [vmem] * (1 + n_tensor),
         scratch_shapes=[pltpu.VMEM((members, length, step), bf16)],
     )(ids, scale, *x_pieces)
-    normed_cols = staged(keep, give)
+    got = staged(keep, give)
+    flips = call(flips_kernel, [Shape((planes,) + got[0].shape[1:], bf16)] * pairs)(*got)
+    normed_cols = stacked(flips)
 
     def part_of(c, left, rows, cross=None, pair_of=None, error=None, offset=None):
         begin = starts[c]
@@ -490,9 +521,6 @@
                 if extra is not None:
                     ins.append(stack(extra.shape[1]))
                     args.append(extra)
-            if merged is not None:
-                ins.append(smem)
-                args.append(ids)
             ins += [whole(a) for a in chain]
             args += chain
             aliases = {}
@@ -501,7 +529,7 @@
                 ins.append(pl.BlockSpec(memory_space=pl.ANY))
                 args.append(errors)
             sums = [Shape((rows, width), f32)] + ([Shape((rows, matches.shape[1]), f32)] if matches is not None else [])
-            out_rows = rows if merged is None else length // n_tensor
+            out_rows = rows if merged is None else length
             outs = [Shape((members, out_rows, step), bf16)]
             out_specs = [stack(out_rows)]
             scratch = []
@@ -544,14 +572,10 @@
             Shape((length - low, high), bf16),
         ],
     )
-    dealt = Shape((planes, high // n_tensor, step), bf16)
-    keep, give = call(
-        functools.partial(deal_kernel, n_tensor), [dealt, dealt], in_specs=[smem, vmem]
-    )(ids, error_0)
-    error_0_cols = staged(keep, give)
+    error_0_cols = stacked(sides(dealt_out(error_0)))
 
     parts = [part_of(c, next_q, length - low, dot_nn, cross, error_0, slice(low, length)) for c in range(CHUNKS)]
-    left_all = gathered(left)
+    left_all = ring(left, False)
     error_q, (tangent, grad_rest) = combine(
         parts, slice(low, length), query_weight, error_0, None,
         functools.partial(second_tail, low, high),
@@ -559,20 +583,17 @@
         [Shape((high, width), bf16), Shape((length, width), f32)],
     )
     parts = [part_of(c, tangent, high, dot_tn, cross, error_q) for c in range(CHUNKS)]
-    tangent_all = gathered(tangent)
+    tangent_all = ring(tangent, False)
     merged, (right,) = combine(
         parts, slice(0, high), support_weight, None, error_q,
         functools.partial(third_tail, high),
         [grad_rest, probs],
         [Shape((length, width), bf16)],
     )
-    right_all = gathered(right)
-    merged_cols = spread(merged)
-
-    kept = call(
-        functools.partial(pack_kernel, planes), Shape((members, (length + high) // n_tensor, step), bf16)
-    )(*normed_cols, *error_0_cols)
-    packed = [kept] + from_others(kept)
+    right_all = ring(right, True)
+    merged_cols = []
+    for part in sides(dealt_out(merged)):
+        merged_cols += [part] + from_others(part)
 
     wide_block = wide // n_task
     own_v, sent_v = call(
@@ -580,32 +601,32 @@
         [Shape((wide_block, width), f32), Shape((wide_block, width), bf16)],
         in_specs=[smem] + [vmem] * (n_tensor + members),
         out_specs=[vmem, vmem],
-    )(ids, *packed, *right_all)
+    )(ids, *normed_cols, *right_all)
+    total_value = own_v + over_task(sent_v, lambda i: i ^ 1).astype(f32)
     own_o, sent_o = call(
         functools.partial(output_kernel, n_tensor, planes),
         [Shape((width, wide_block), f32), Shape((width, wide_block), bf16)],
-        in_specs=[smem] + [vmem] * (2 * n_tensor + 2 * members),
+        in_specs=[smem] + [vmem] * ((1 + pairs) * n_tensor + 2 * members),
         out_specs=[vmem, vmem],
-    )(ids, *merged_cols, *packed, *left_all, *tangent_all)
-    total_value = own_v + over_task(sent_v, lambda i: i ^ 1).astype(f32)
+    )(ids, *merged_cols, *error_0_cols, *left_all, *tangent_all)
     total_output = own_o + over_task(sent_o, lambda i: i ^ 1).astype(f32)
     return (total_value, total_output)
 
 
 def solution(mesh):
-    body = functools.partial(program, mesh.shape["task"], mesh.shape["tensor"])
+    body = functools.partial(program, mesh.shape[TASK], mesh.shape[TENSOR])
     return jax.shard_map(
         body,
         mesh=mesh,
         in_specs=(
-            P("task", "tensor"),
-            P("task", "tensor"),
-            P("task", "tensor"),
-            P("task", "tensor"),
-            P(None, "tensor"),
-            P("tensor", None),
-            P("task"),
+            P(TASK, TENSOR),
+            P(TASK, TENSOR),
+            P(TASK, TENSOR),
+            P(TASK, TENSOR),
+            P(None, TENSOR),
+            P(TENSOR, None),
+            P(TASK),
         ),
-        out_specs=(P("task", "tensor"), P("tensor", "task")),
+        out_specs=(P(TASK, TENSOR), P(TENSOR, TASK)),
         check_vma=False,
     )

time: 201 us -> 188 us (0.935)
  waiting for transfers between devices: 54.7 us -> 71.6 us
  starting transfers between devices: 74.2 us -> 58.4 us
  local copies, waits for them, and re-layouts: 18.3 us -> 5.55 us
    ppermute x40 -> x49, waiting for transfers between devices: 54.7 us -> 71.6 us  [the longest x35 55.8 us: over_task(): return lax.ppermute(value, TASK, [(i, target(i)) for i in range(n_task)])]
    unnamed x46 -> x14, local copies, waits for them, and re-layouts: 18.3 us -> 5.55 us
    ppermute x40 -> x49, starting transfers between devices: 70 us -> 58.4 us  [the longest x35 40.9 us: over_task(): return lax.ppermute(value, TASK, [(i, target(i)) for i in range(n_task)])]
    all_to_all x1 -> x0, starting transfers between devices: 4.19 us -> none  [spread(): lax.all_to_all(value, 'task', split_axis=0, concat_axis=0, axis_index_gro...]
    pallas_call x6 -> x9, Pallas kernels: 19.3 us -> 17.2 us  [combine(): call(functools.partial(finish_kernel, row_slice, len(others), matches is...]
    pallas_call x6 -> x9, Pallas kernels: 12.9 us -> 13.9 us  [part_of(): call(functools.partial(part_kernel, cross, offset), Shape((rows, shares[c...]
  transfers between devices with their start and end apart: 41 -> 49, of which waited for: 16 -> 21; matrix products, arithmetic and copies ran while one was open for 1% -> 1% of each run, Pallas kernels for 19% -> 23%
where the time goes in v3:
time: 188 us
  waiting for transfers between devices  71.6 us (38%)
  starting transfers between devices  58.4 us (31%)
  Pallas kernels  48.3 us (26%)
  local copies, waits for them, and re-layouts  5.55 us (3%)
  other arithmetic  2.26 us (1%)
    ppermute x35, waiting for transfers between devices, over_task(): return lax.ppermute(value, TASK, [(i, target(i)) for i in range(n_task)])  55.8 us
    ppermute x35, starting transfers between devices, over_task(): return lax.ppermute(value, TASK, [(i, target(i)) for i in range(n_task)])  40.9 us
    ppermute x14, starting transfers between devices, over_tensor(): lax.ppermute(value, TENSOR, [(i, (i + shift) % n_tensor) for i in range(n...  17.5 us
    pallas_call x9, Pallas kernels, combine(): call(functools.partial(finish_kernel, row_slice, len(others), matches is...  17.2 us
    ppermute x14, waiting for transfers between devices, over_tensor(): lax.ppermute(value, TENSOR, [(i, (i + shift) % n_tensor) for i in range(n...  15.8 us
    pallas_call x9, Pallas kernels, part_of(): call(functools.partial(part_kernel, cross, offset), Shape((rows, shares[c...  13.9 us
    unnamed x14, local copies, waits for them, and re-layouts  5.55 us
  transfers between devices with their start and end apart: 49, of which 21 were waited for; matrix products, arithmetic and copies ran while one was open for 1% of the time, Pallas kernels for 23%

profile of v3, /device:TPU:0, one launch (start us, length us, event | category | flops | bytes accessed | tf_op | source)
XLA Modules:
  0.0 187.9 jit_solution(4242913001551990966)
XLA Ops:
  0.8 3.0 %collective-permute-start = (bf16[128,2048]{1,0:T(8,128)(2,1)}, bf16[128,2048]{1,0:T(8,128)(2,1)S(1)}, u32[]{:S(2)}, u32[]{:S(2)}) collective-permute-start(bf16[128,2048]{1,0:T(8,128)(2,1)} %refs_5_.2), channel_id=1, source_target_pairs={{0,1},{1,0},{2,3},{3,2},{4,5},{5,4},{6,7},{7,6},{8,9},{9,8},{10,11... | collective-permute-start | bytes 1572872 | tf_op jit(solution)/shard_map/ppermute | solution.py:375
  4.4 3.4 %copy-done.1 = bf16[4096,1024]{1,0:T(8,128)(2,1)S(1)} copy-done((bf16[4096,1024]{1,0:T(8,128)(2,1)S(1)}, bf16[4096,1024]{1,0:T(8,128)(2,1)}, u32[]{:S(2)}) %copy-start.1) | copy-done | bytes 8388632
  16.1 2.9 %shard_map.89 = (bf16[128,1024]{1,0:T(8,128)(2,1)S(1)}, bf16[128,1024]{1,0:T(8,128)(2,1)S(1)}, f32[128,1]{1,0:T(8,128)S(1)}) custom-call(s32[1]{0:T(128)} %bitcast.5.place_ref, bf16[128,2048]{1,0:T(8,128)(2,1)S(1)} %collective-permute-done.x_ref.refs_1_, bf16[2048,1024]{1,0:T(8,128)(2,1)S(1)} %shard_map.86.weight_ref, ...), custom_call_target="tpu_custom_call" | custom-call | tf_op jit(solution)/shard_map/pallas_call | solution.py:463
  30.6 2.8 %collective-permute-done.1.take_ref = bf16[4,64,512]{2,1,0:T(8,128)(2,1)S(1)} collective-permute-done((bf16[4,64,512]{2,1,0:T(8,128)(2,1)S(1)}, bf16[4,64,512]{2,1,0:T(8,128)(2,1)S(1)}, u32[]{:S(2)}, u32[]{:S(2)}) %collective-permute-start.1) | collective-permute-done | bytes 262176 | tf_op jit(solution)/shard_map/ppermute | solution.py:381
  35.0 4.9 %collective-permute-done.8.refs_3_ = bf16[96,1024]{1,0:T(8,128)(2,1)S(1)} collective-permute-done((bf16[96,1024]{1,0:T(8,128)(2,1)S(1)}, bf16[96,1024]{1,0:T(8,128)(2,1)S(1)}, u32[]{:S(2)}, u32[]{:S(2)}) %collective-permute-start.8) | collective-permute-done | bytes 196640 | tf_op jit(solution)/shard_map/ppermute | solution.py:375
  43.0 2.7 %shard_map.100 = (bf16[8,96,512]{2,1,0:T(8,128)(2,1)S(1)}, bf16[128,1024]{1,0:T(8,128)(2,1)S(1)}, bf16[96,1024]{1,0:T(8,128)(2,1)S(1)}, bf16[128,1024]{1,0:T(8,128)(2,1)S(1)}, bf16[96,96]{1,0:T(8,128)(2,1)S(1)}) custom-call(bf16[96,1536]{1,0:T(8,128)(2,1)S(1)} %shard_map.95.refs_0_, ...), custom_call_target="tpu_custom_call", output_to_operand_aliasing={{0}: (5, {})} | custom-call | tf_op jit(solution)/shard_map/pallas_call | solution.py:547
  56.3 2.6 %collective-permute-start.30 = (bf16[2,48,512]{2,1,0:T(8,128)(2,1)S(1)}, bf16[2,48,512]{2,1,0:T(8,128)(2,1)S(1)}, u32[]{:S(2)}, u32[]{:S(2)}) collective-permute-start(bf16[2,48,512]{2,1,0:T(8,128)(2,1)S(1)} %get-tuple-element.119), channel_id=1, source_target_pairs={{0,16},{2,18},{4,20},{6,22},{8,24},{10,26},{12,28},{14,30},{16,0},... | collective-permute-start | bytes 294920 | tf_op jit(solution)/shard_map/ppermute | solution.py:381
  63.5 5.0 %collective-permute-done.31.refs_3_ = bf16[2,48,512]{2,1,0:T(8,128)(2,1)S(1)} collective-permute-done((bf16[2,48,512]{2,1,0:T(8,128)(2,1)S(1)}, bf16[2,48,512]{2,1,0:T(8,128)(2,1)S(1)}, u32[]{:S(2)}, u32[]{:S(2)}) %collective-permute-start.31) | collective-permute-done | bytes 98336 | tf_op jit(solution)/shard_map/ppermute | solution.py:381
  69.1 4.3 %collective-permute-start.32 = (bf16[4,48,512]{2,1,0:T(8,128)(2,1)S(1)}, bf16[4,48,512]{2,1,0:T(8,128)(2,1)S(1)}, u32[]{:S(2)}, u32[]{:S(2)}) collective-permute-start(bf16[4,48,512]{2,1,0:T(8,128)(2,1)S(1)} %get-tuple-element.122), channel_id=1, source_target_pairs={{0,4},{2,6},{4,0},{6,2},{8,12},{10,14},{12,8},{14,10},{16,20},{18,... | collective-permute-start | bytes 589832 | tf_op jit(solution)/shard_map/ppermute | solution.py:381
  73.3 3.9 %collective-permute-start.4 = (bf16[2,64,512]{2,1,0:T(8,128)(2,1)S(1)}, bf16[2,64,512]{2,1,0:T(8,128)(2,1)S(1)}, u32[]{:S(2)}, u32[]{:S(2)}) collective-permute-start(bf16[2,64,512]{2,1,0:T(8,128)(2,1)S(1)} %get-tuple-element.78), channel_id=1, source_target_pairs={{0,24},{2,26},{4,28},{6,30},{8,0},{10,2},{12,4},{14,6},{16,8},{18,... | collective-permute-start | bytes 393224 | tf_op jit(solution)/shard_map/ppermute | solution.py:381
  80.5 2.9 %shard_map.106 = (bf16[8,96,512]{2,1,0:T(8,128)(2,1)S(1)}, bf16[96,1024]{1,0:T(8,128)(2,1)S(1)}, f32[128,1024]{1,0:T(8,128)S(1)}) custom-call(bf16[96,1536]{1,0:T(8,128)(2,1)S(1)} %shard_map.101.refs_0_, bf16[1024,4096]{1,0:T(8,128)(2,1)S(1)} %shard_map.94.refs_1_, f32[128,1]{1,0:T(8,128)S(1)} %get-tuple-element.92.refs_2_, ...), custom_call_target="tpu_custom_call", output_to_operand_aliasing={{0}: (7, {})} | custom-call | tf_op jit(solution)/shard_map/pallas_call | solution.py:547
  91.7 5.0 %collective-permute-done.14.refs_3_ = bf16[96,1024]{1,0:T(8,128)(2,1)S(1)} collective-permute-done((bf16[96,1024]{1,0:T(8,128)(2,1)S(1)}, bf16[96,1024]{1,0:T(8,128)(2,1)S(1)}, u32[]{:S(2)}, u32[]{:S(2)}) %collective-permute-start.14) | collective-permute-done | bytes 196640 | tf_op jit(solution)/shard_map/ppermute | solution.py:375
  103.3 2.1 %shard_map.112 = (bf16[8,128,512]{2,1,0:T(8,128)(2,1)S(1)}, bf16[128,1024]{1,0:T(8,128)(2,1)S(1)}) custom-call(bf16[96,1536]{1,0:T(8,128)(2,1)S(1)} %shard_map.107.refs_0_, bf16[1024,4096]{1,0:T(8,128)(2,1)S(1)} %shard_map.94.refs_1_, f32[128,1]{1,0:T(8,128)S(1)} %get-tuple-element.82.refs_2_.refs_10_, ...), custom_call_target="tpu_custom_call", output_to_operand_aliasing={{0}: (6, {})} | custom-call | tf_op jit(solution)/shard_map/pallas_call | solution.py:547
  107.7 2.4 %collective-permute-start.24 = (bf16[2,64,512]{2,1,0:T(8,128)(2,1)S(1)}, bf16[2,64,512]{2,1,0:T(8,128)(2,1)S(1)}, u32[]{:S(2)}, u32[]{:S(2)}) collective-permute-start(bf16[2,64,512]{2,1,0:T(8,128)(2,1)S(1)} %get-tuple-element.113), channel_id=1, source_target_pairs={{0,16},{2,18},{4,20},{6,22},{8,24},{10,26},{12,28},{14,30},{16,0},... | collective-permute-start | bytes 393224 | tf_op jit(solution)/shard_map/ppermute | solution.py:381
  110.1 3.4 %collective-permute-start.25 = (bf16[2,64,512]{2,1,0:T(8,128)(2,1)S(1)}, bf16[2,64,512]{2,1,0:T(8,128)(2,1)S(1)}, u32[]{:S(2)}, u32[]{:S(2)}) collective-permute-start(bf16[2,64,512]{2,1,0:T(8,128)(2,1)S(1)} %get-tuple-element.114), channel_id=1, source_target_pairs={{0,24},{2,26},{4,28},{6,30},{8,0},{10,2},{12,4},{14,6},{16,8},{18,... | collective-permute-start | bytes 393224 | tf_op jit(solution)/shard_map/ppermute | solution.py:381
  116.1 8.2 %collective-permute-done.24.refs_2_ = bf16[2,64,512]{2,1,0:T(8,128)(2,1)S(1)} collective-permute-done((bf16[2,64,512]{2,1,0:T(8,128)(2,1)S(1)}, bf16[2,64,512]{2,1,0:T(8,128)(2,1)S(1)}, u32[]{:S(2)}, u32[]{:S(2)}) %collective-permute-start.24) | collective-permute-done | bytes 131104 | tf_op jit(solution)/shard_map/ppermute | solution.py:381
  137.4 5.8 %collective-permute-done.46.refs_20_ = bf16[96,1024]{1,0:T(8,128)(2,1)S(1)} collective-permute-done((bf16[96,1024]{1,0:T(8,128)(2,1)S(1)}, bf16[96,1024]{1,0:T(8,128)(2,1)S(1)}, u32[]{:S(2)}, u32[]{:S(2)}) %collective-permute-start.46) | collective-permute-done | bytes 196640 | tf_op jit(solution)/shard_map/ppermute | solution.py:381
  143.2 5.5 %collective-permute-done.26.refs_1_ = bf16[4,64,512]{2,1,0:T(8,128)(2,1)S(1)} collective-permute-done((bf16[4,64,512]{2,1,0:T(8,128)(2,1)S(1)}, bf16[4,64,512]{2,1,0:T(8,128)(2,1)S(1)}, u32[]{:S(2)}, u32[]{:S(2)}) %collective-permute-start.26) | collective-permute-done | bytes 262176 | tf_op jit(solution)/shard_map/ppermute | solution.py:375
  149.6 5.1 %collective-permute-done.47.refs_21_ = bf16[96,1024]{1,0:T(8,128)(2,1)S(1)} collective-permute-done((bf16[96,1024]{1,0:T(8,128)(2,1)S(1)}, bf16[96,1024]{1,0:T(8,128)(2,1)S(1)}, u32[]{:S(2)}, u32[]{:S(2)}) %collective-permute-start.47) | collective-permute-done | bytes 196640 | tf_op jit(solution)/shard_map/ppermute | solution.py:381
  154.6 2.7 %shard_map.119 = (f32[1024,256]{1,0:T(8,128)S(1)}, bf16[1024,256]{1,0:T(8,128)(2,1)S(1)}) custom-call(s32[4]{0:T(128)S(1)} %pad_add_fusion.ids_ref.refs_2_.refs_4_, bf16[4,64,512]{2,1,0:T(8,128)(2,1)S(1)} %get-tuple-element.115.refs_0_, bf16[4,64,512]{2,1,0:T(8,128)(2,1)S(1)} %collective-permute-done.26.refs_1_, ...), custom_call_target="tpu_custom_call" | custom-call | tf_op jit(solution)/shard_map/pallas_call | solution.py:606
  161.5 5.1 %collective-permute-done.18.refs_6_ = bf16[128,1024]{1,0:T(8,128)(2,1)S(1)} collective-permute-done((bf16[128,1024]{1,0:T(8,128)(2,1)S(1)}, bf16[128,1024]{1,0:T(8,128)(2,1)S(1)}, u32[]{:S(2)}, u32[]{:S(2)}) %collective-permute-start.18) | collective-permute-done | bytes 262176 | tf_op jit(solution)/shard_map/ppermute | solution.py:381
  166.6 5.6 %collective-permute-done.19.refs_7_ = bf16[128,1024]{1,0:T(8,128)(2,1)S(1)} collective-permute-done((bf16[128,1024]{1,0:T(8,128)(2,1)S(1)}, bf16[128,1024]{1,0:T(8,128)(2,1)S(1)}, u32[]{:S(2)}, u32[]{:S(2)}) %collective-permute-start.19) | collective-permute-done | bytes 262176 | tf_op jit(solution)/shard_map/ppermute | solution.py:381
  172.2 5.6 %collective-permute-done.21.refs_9_ = bf16[128,1024]{1,0:T(8,128)(2,1)S(1)} collective-permute-done((bf16[128,1024]{1,0:T(8,128)(2,1)S(1)}, bf16[128,1024]{1,0:T(8,128)(2,1)S(1)}, u32[]{:S(2)}, u32[]{:S(2)}) %collective-permute-start.21) | collective-permute-done | bytes 262176 | tf_op jit(solution)/shard_map/ppermute | solution.py:381
  177.9 5.1 %collective-permute-done.20.refs_8_ = bf16[128,1024]{1,0:T(8,128)(2,1)S(1)} collective-permute-done((bf16[128,1024]{1,0:T(8,128)(2,1)S(1)}, bf16[128,1024]{1,0:T(8,128)(2,1)S(1)}, u32[]{:S(2)}, u32[]{:S(2)}) %collective-permute-start.20) | collective-permute-done | bytes 262176 | tf_op jit(solution)/shard_map/ppermute | solution.py:381
  (125 shorter events, 86.2 us)
Async XLA Ops:
  0.8 15.3 %collective-permute-start = (bf16[128,2048]{1,0:T(8,128)(2,1)}, bf16[128,2048]{1,0:T(8,128)(2,1)S(1)}, u32[]{:S(2)}, u32[]{:S(2)}) collective-permute-start(bf16[128,2048]{1,0:T(8,128)(2,1)} %refs_5_.2), channel_id=1, source_target_pairs={{0,1},{1,0},{2,3},{3,2},{4,5},{5,4},{6,7},{7,6},{8,9},{9,8},{10,11... | collective-permute-start | bytes 1572872 | tf_op jit(solution)/shard_map/ppermute | solution.py:375
  20.8 20.3 %collective-permute-start.7 = (bf16[96,1536]{1,0:T(8,128)(2,1)S(1)}, bf16[96,1536]{1,0:T(8,128)(2,1)S(1)}, u32[]{:S(2)}, u32[]{:S(2)}) collective-permute-start(bf16[96,1536]{1,0:T(8,128)(2,1)S(1)} %shard_map.96.refs_0_), channel_id=1, source_target_pairs={{0,1},{1,0},{2,3},{3,2},{4,5},{5,4},{6,7},{7,6},{8,9},{9,8},{10,11... | collective-permute-start | bytes 884744 | tf_op jit(solution)/shard_map/ppermute | solution.py:375
  24.2 18.8 %collective-permute-start.6 = (bf16[96,1536]{1,0:T(8,128)(2,1)S(1)}, bf16[96,1536]{1,0:T(8,128)(2,1)S(1)}, u32[]{:S(2)}, u32[]{:S(2)}) collective-permute-start(bf16[96,1536]{1,0:T(8,128)(2,1)S(1)} %shard_map.95.refs_0_), channel_id=1, source_target_pairs={{0,1},{1,0},{2,3},{3,2},{4,5},{5,4},{6,7},{7,6},{8,9},{9,8},{10,11... | collective-permute-start | bytes 884744 | tf_op jit(solution)/shard_map/ppermute | solution.py:375
  33.4 22.9 %collective-permute-start.2 = (bf16[2,64,512]{2,1,0:T(8,128)(2,1)S(1)}, bf16[2,64,512]{2,1,0:T(8,128)(2,1)S(1)}, u32[]{:S(2)}, u32[]{:S(2)}) collective-permute-start(bf16[2,64,512]{2,1,0:T(8,128)(2,1)S(1)} %get-tuple-element.76), channel_id=1, source_target_pairs={{0,8},{2,10},{4,12},{6,14},{8,16},{10,18},{12,20},{14,22},{16,24},... | collective-permute-start | bytes 393224 | tf_op jit(solution)/shard_map/ppermute | solution.py:381
  47.6 25.7 %collective-permute-start.10 = (bf16[96,1536]{1,0:T(8,128)(2,1)S(1)}, bf16[96,1536]{1,0:T(8,128)(2,1)S(1)}, u32[]{:S(2)}, u32[]{:S(2)}) collective-permute-start(bf16[96,1536]{1,0:T(8,128)(2,1)S(1)} %shard_map.102.refs_0_), channel_id=1, source_target_pairs={{0,1},{1,0},{2,3},{3,2},{4,5},{5,4},{6,7},{7,6},{8,9},{9,8},{10,11... | collective-permute-start | bytes 884744 | tf_op jit(solution)/shard_map/ppermute | solution.py:375
  50.5 26.7 %collective-permute-start.9 = (bf16[96,1536]{1,0:T(8,128)(2,1)S(1)}, bf16[96,1536]{1,0:T(8,128)(2,1)S(1)}, u32[]{:S(2)}, u32[]{:S(2)}) collective-permute-start(bf16[96,1536]{1,0:T(8,128)(2,1)S(1)} %shard_map.101.refs_0_), channel_id=1, source_target_pairs={{0,1},{1,0},{2,3},{3,2},{4,5},{5,4},{6,7},{7,6},{8,9},{9,8},{10,11... | collective-permute-start | bytes 884744 | tf_op jit(solution)/shard_map/ppermute | solution.py:375
  63.1 26.4 %collective-permute-start.34 = (bf16[128,1024]{1,0:T(8,128)(2,1)S(1)}, bf16[128,1024]{1,0:T(8,128)(2,1)S(1)}, u32[]{:S(2)}, u32[]{:S(2)}) collective-permute-start(bf16[128,1024]{1,0:T(8,128)(2,1)S(1)} %get-tuple-element.123.refs_6_), channel_id=1, source_target_pairs={{0,8},{2,10},{4,12},{6,14},{8,16},{10,18},{12,20},{14,22},{16,24},... | collective-permute-start | bytes 786440 | tf_op jit(solution)/shard_map/ppermute | solution.py:381
  68.5 16.4 %collective-permute-start.3 = (bf16[2,64,512]{2,1,0:T(8,128)(2,1)S(1)}, bf16[2,64,512]{2,1,0:T(8,128)(2,1)S(1)}, u32[]{:S(2)}, u32[]{:S(2)}) collective-permute-start(bf16[2,64,512]{2,1,0:T(8,128)(2,1)S(1)} %get-tuple-element.77), channel_id=1, source_target_pairs={{0,16},{2,18},{4,20},{6,22},{8,24},{10,26},{12,28},{14,30},{16,0},... | collective-permute-start | bytes 393224 | tf_op jit(solution)/shard_map/ppermute | solution.py:381
  69.1 20.5 %collective-permute-start.32 = (bf16[4,48,512]{2,1,0:T(8,128)(2,1)S(1)}, bf16[4,48,512]{2,1,0:T(8,128)(2,1)S(1)}, u32[]{:S(2)}, u32[]{:S(2)}) collective-permute-start(bf16[4,48,512]{2,1,0:T(8,128)(2,1)S(1)} %get-tuple-element.122), channel_id=1, source_target_pairs={{0,4},{2,6},{4,0},{6,2},{8,12},{10,14},{12,8},{14,10},{16,20},{18,... | collective-permute-start | bytes 589832 | tf_op jit(solution)/shard_map/ppermute | solution.py:381
  84.9 14.1 %collective-permute-start.13 = (bf16[96,1536]{1,0:T(8,128)(2,1)S(1)}, bf16[96,1536]{1,0:T(8,128)(2,1)S(1)}, u32[]{:S(2)}, u32[]{:S(2)}) collective-permute-start(bf16[96,1536]{1,0:T(8,128)(2,1)S(1)} %shard_map.108.refs_0_), channel_id=1, source_target_pairs={{0,1},{1,0},{2,3},{3,2},{4,5},{5,4},{6,7},{7,6},{8,9},{9,8},{10,11... | collective-permute-start | bytes 884744 | tf_op jit(solution)/shard_map/ppermute | solution.py:375
  89.7 23.8 %collective-permute-start.33 = (bf16[8,48,512]{2,1,0:T(8,128)(2,1)S(1)}, bf16[8,48,512]{2,1,0:T(8,128)(2,1)S(1)}, u32[]{:S(2)}, u32[]{:S(2)}) collective-permute-start(bf16[8,48,512]{2,1,0:T(8,128)(2,1)S(1)} %shard_map.118.refs_4_), channel_id=1, source_target_pairs={{0,1},{1,0},{2,3},{3,2},{4,5},{5,4},{6,7},{7,6},{8,9},{9,8},{10,11... | collective-permute-start | bytes 1179656 | tf_op jit(solution)/shard_map/ppermute | solution.py:375
  107.7 16.7 %collective-permute-start.24 = (bf16[2,64,512]{2,1,0:T(8,128)(2,1)S(1)}, bf16[2,64,512]{2,1,0:T(8,128)(2,1)S(1)}, u32[]{:S(2)}, u32[]{:S(2)}) collective-permute-start(bf16[2,64,512]{2,1,0:T(8,128)(2,1)S(1)} %get-tuple-element.113), channel_id=1, source_target_pairs={{0,16},{2,18},{4,20},{6,22},{8,24},{10,26},{12,28},{14,30},{16,0},... | collective-permute-start | bytes 393224 | tf_op jit(solution)/shard_map/ppermute | solution.py:381
  110.1 14.2 %collective-permute-start.25 = (bf16[2,64,512]{2,1,0:T(8,128)(2,1)S(1)}, bf16[2,64,512]{2,1,0:T(8,128)(2,1)S(1)}, u32[]{:S(2)}, u32[]{:S(2)}) collective-permute-start(bf16[2,64,512]{2,1,0:T(8,128)(2,1)S(1)} %get-tuple-element.114), channel_id=1, source_target_pairs={{0,24},{2,26},{4,28},{6,30},{8,0},{10,2},{12,4},{14,6},{16,8},{18,... | collective-permute-start | bytes 393224 | tf_op jit(solution)/shard_map/ppermute | solution.py:381
  113.5 15.0 %collective-permute-start.36 = (bf16[128,1024]{1,0:T(8,128)(2,1)S(1)}, bf16[128,1024]{1,0:T(8,128)(2,1)S(1)}, u32[]{:S(2)}, u32[]{:S(2)}) collective-permute-start(bf16[128,1024]{1,0:T(8,128)(2,1)S(1)} %collective-permute-done.35.refs_8_), channel_id=1, source_target_pairs={{0,8},{2,10},{4,12},{6,14},{8,16},{10,18},{12,20},{14,22},{16,24},... | collective-permute-start | bytes 786440 | tf_op jit(solution)/shard_map/ppermute | solution.py:381
  113.5 16.1 %collective-permute-start.39 = (bf16[128,1024]{1,0:T(8,128)(2,1)S(1)}, bf16[128,1024]{1,0:T(8,128)(2,1)S(1)}, u32[]{:S(2)}, u32[]{:S(2)}) collective-permute-start(bf16[128,1024]{1,0:T(8,128)(2,1)S(1)} %collective-permute-done.35.refs_8_), channel_id=1, source_target_pairs={{0,4},{2,6},{4,0},{6,2},{8,12},{10,14},{12,8},{14,10},{16,20},{18,... | collective-permute-start | bytes 786440 | tf_op jit(solution)/shard_map/ppermute | solution.py:381
  128.5 29.5 %collective-permute-start.5 = (bf16[8,64,512]{2,1,0:T(8,128)(2,1)S(1)}, bf16[8,64,512]{2,1,0:T(8,128)(2,1)S(1)}, u32[]{:S(2)}, u32[]{:S(2)}) collective-permute-start(bf16[8,64,512]{2,1,0:T(8,128)(2,1)S(1)} %shard_map.93.refs_0_), channel_id=1, source_target_pairs={{0,1},{1,0},{2,3},{3,2},{4,5},{5,4},{6,7},{7,6},{8,9},{9,8},{10,11... | collective-permute-start | bytes 1572872 | tf_op jit(solution)/shard_map/ppermute | solution.py:375
  129.6 19.1 %collective-permute-start.26 = (bf16[4,64,512]{2,1,0:T(8,128)(2,1)S(1)}, bf16[4,64,512]{2,1,0:T(8,128)(2,1)S(1)}, u32[]{:S(2)}, u32[]{:S(2)}) collective-permute-start(bf16[4,64,512]{2,1,0:T(8,128)(2,1)S(1)} %get-tuple-element.115.refs_0_), channel_id=1, source_target_pairs={{0,1},{1,0},{2,3},{3,2},{4,5},{5,4},{6,7},{7,6},{8,9},{9,8},{10,11... | collective-permute-start | bytes 786440 | tf_op jit(solution)/shard_map/ppermute | solution.py:375
  132.5 16.4 %collective-permute-start.40 = (bf16[128,1024]{1,0:T(8,128)(2,1)S(1)}, bf16[128,1024]{1,0:T(8,128)(2,1)S(1)}, u32[]{:S(2)}, u32[]{:S(2)}) collective-permute-start(bf16[128,1024]{1,0:T(8,128)(2,1)S(1)} %collective-permute-done.36.refs_9_), channel_id=1, source_target_pairs={{0,4},{2,6},{4,0},{6,2},{8,12},{10,14},{12,8},{14,10},{16,20},{18,... | collective-permute-start | bytes 786440 | tf_op jit(solution)/shard_map/ppermute | solution.py:381
  136.2 18.5 %collective-permute-start.28 = (bf16[4,64,512]{2,1,0:T(8,128)(2,1)S(1)}, bf16[4,64,512]{2,1,0:T(8,128)(2,1)S(1)}, u32[]{:S(2)}, u32[]{:S(2)}) collective-permute-start(bf16[4,64,512]{2,1,0:T(8,128)(2,1)S(1)} %collective-permute-done.27.refs_2_), channel_id=1, source_target_pairs={{0,1},{1,0},{2,3},{3,2},{4,5},{5,4},{6,7},{7,6},{8,9},{9,8},{10,11... | collective-permute-start | bytes 786440 | tf_op jit(solution)/shard_map/ppermute | solution.py:375
  143.2 16.3 %collective-permute-start.17 = (bf16[128,1024]{1,0:T(8,128)(2,1)S(1)}, bf16[128,1024]{1,0:T(8,128)(2,1)S(1)}, u32[]{:S(2)}, u32[]{:S(2)}) collective-permute-start(bf16[128,1024]{1,0:T(8,128)(2,1)S(1)} %get-tuple-element.107.refs_2_), channel_id=1, source_target_pairs={{0,24},{2,26},{4,28},{6,30},{8,0},{10,2},{12,4},{14,6},{16,8},{18,... | collective-permute-start | bytes 786440 | tf_op jit(solution)/shard_map/ppermute | solution.py:381
  157.3 27.6 %collective-permute-start.48 = (bf16[1024,256]{1,0:T(8,128)(2,1)S(1)}, bf16[1024,256]{1,0:T(8,128)(2,1)S(1)}, u32[]{:S(2)}, u32[]{:S(2)}) collective-permute-start(bf16[1024,256]{1,0:T(8,128)(2,1)S(1)} %get-tuple-element.125), channel_id=1, source_target_pairs={{0,2},{2,0},{4,6},{6,4},{8,10},{10,8},{12,14},{14,12},{16,18},{18,... | collective-permute-start | bytes 1572872 | tf_op jit(solution)/shard_map/ppermute | solution.py:381
  158.1 14.2 %collective-permute-start.19 = (bf16[128,1024]{1,0:T(8,128)(2,1)S(1)}, bf16[128,1024]{1,0:T(8,128)(2,1)S(1)}, u32[]{:S(2)}, u32[]{:S(2)}) collective-permute-start(bf16[128,1024]{1,0:T(8,128)(2,1)S(1)} %collective-permute-done.15.refs_3_), channel_id=1, source_target_pairs={{0,4},{2,6},{4,0},{6,2},{8,12},{10,14},{12,8},{14,10},{16,20},{18,... | collective-permute-start | bytes 786440 | tf_op jit(solution)/shard_map/ppermute | solution.py:381
  159.5 18.4 %collective-permute-start.21 = (bf16[128,1024]{1,0:T(8,128)(2,1)S(1)}, bf16[128,1024]{1,0:T(8,128)(2,1)S(1)}, u32[]{:S(2)}, u32[]{:S(2)}) collective-permute-start(bf16[128,1024]{1,0:T(8,128)(2,1)S(1)} %collective-permute-done.17.refs_5_), channel_id=1, source_target_pairs={{0,4},{2,6},{4,0},{6,2},{8,12},{10,14},{12,8},{14,10},{16,20},{18,... | collective-permute-start | bytes 786440 | tf_op jit(solution)/shard_map/ppermute | solution.py:381
  160.1 22.9 %collective-permute-start.20 = (bf16[128,1024]{1,0:T(8,128)(2,1)S(1)}, bf16[128,1024]{1,0:T(8,128)(2,1)S(1)}, u32[]{:S(2)}, u32[]{:S(2)}) collective-permute-start(bf16[128,1024]{1,0:T(8,128)(2,1)S(1)} %collective-permute-done.16.refs_4_), channel_id=1, source_target_pairs={{0,4},{2,6},{4,0},{6,2},{8,12},{10,14},{12,8},{14,10},{16,20},{18,... | collective-permute-start | bytes 786440 | tf_op jit(solution)/shard_map/ppermute | solution.py:381
  (32 other events, 269.3 us)

commit v4 on v3

--- a/solution.py
+++ b/solution.py
@@ -140,7 +140,7 @@
         keep_ref[...] = scale
         scale_ref[...] = scale
 
-    upper = keep_ref[...] * (acc_ref[...] + dot_nn(x_ref[...], weight_ref[...]))
+    upper = keep_ref[...] * (acc_ref[...] + dot_nn(x_ref[...], block_of(weight_ref, 0, upper_ref.shape[1])))
     upper = upper.astype(bf16)
     upper_ref[...] = upper
     mixed_ref[...] = by_head(dot_nn, probs_ref, upper).astype(bf16)
@@ -208,16 +208,21 @@
     deal(ids_ref, pieces, blocks_ref, keep_ref, give_ref)
 
 
-def part_kernel(cross, offset, *refs):
+def block_of(weight_ref, begin, step):
+    start = pl.multiple_of((begin + pl.program_id(0)) * step, step)
+    return weight_ref[:, pl.ds(start, step)]
+
+
+def part_kernel(begin, cross, offset, *refs):
     refs = list(refs)
     take = lambda n: [refs.pop(0) for _ in range(n)]
     left_ref, weight_ref = take(2)
-    part = dot_nn(left_ref[...], weight_ref[...])
+    part = dot_nn(left_ref[...], block_of(weight_ref, begin, refs[-1].shape[1]))
     if cross is not None:
         cross_ref, error_ref = take(2)
         part = part + cross(cross_ref[...], error_ref[0])
     if offset is not None:
-        rows, begin, span = offset
+        rows, span = offset
         piece = (begin + pl.program_id(0)) // span
         group_ref, x_ref, t_ref = take(3)
         gap = x_ref[rows].astype(f32) - t_ref[rows].astype(f32)
@@ -225,7 +230,7 @@
     refs[0][...] = part.astype(bf16)
 
 
-def finish_kernel(rows, others, matched, merged, chained, filled, tail, n_tail, *refs):
+def finish_kernel(begin, rows, others, matched, merged, chained, filled, tail, n_tail, *refs):
     refs = list(refs)
     take = lambda n: [refs.pop(0) for _ in range(n)]
     part_ref, weight_ref, scale_ref = take(3)
@@ -262,7 +267,7 @@
         error_ref[0] = both.astype(bf16)
     else:
         error_ref[0] = error
-    acc = dot_nt(error, weight_ref[...])
+    acc = dot_nt(error, block_of(weight_ref, begin, error.shape[1]))
     match = dot_nt(error, match_in[0][0]) if matched else None
     first = pl.program_id(0) == 0
 
@@ -464,7 +469,7 @@
         functools.partial(upper_kernel, wide),
         [Shape((length, width), bf16), Shape((length, width), bf16), Shape((length, 1), f32)],
         grid_spec=spec(
-            [x_spec, pl.BlockSpec((part_width, block), lambda i, place: (0, i)), cols_spec, one_spec, probs_spec],
+            [x_spec, vmem, cols_spec, one_spec, probs_spec],
             [cols_spec, cols_spec, one_spec],
             [pltpu.VMEM((length, 1), f32)],
         ),
@@ -487,17 +492,17 @@
 
     def part_of(c, left, rows, cross=None, pair_of=None, error=None, offset=None):
         begin = starts[c]
-        ins = [pl.BlockSpec((rows, width), lambda i: (0, 0)), pl.BlockSpec((width, step), lambda i: (0, begin + i))]
+        ins = [pl.BlockSpec((rows, width), lambda i: (0, 0)), vmem]
         args = [left, output_weight]
         if cross is not None:
             ins += [whole(pair_of), pl.BlockSpec((1, error.shape[1], step), lambda i: (begin + i, 0, 0))]
             args += [pair_of, error]
         if offset is not None:
-            offset = (offset, begin, span)
+            offset = (offset, span)
             ins += [smem] + [pl.BlockSpec((length, step), lambda i: (0, (begin + i) % span))] * 2
             args += [ids, inputs, targets]
         part = call(
-            functools.partial(part_kernel, cross, offset),
+            functools.partial(part_kernel, begin, cross, offset),
             Shape((rows, shares[c] * step), bf16),
             grid=(shares[c],),
             in_specs=ins,
@@ -513,7 +518,7 @@
             last = c == CHUNKS - 1
             cols = pl.BlockSpec((rows, step), lambda i: (0, i))
             stack = lambda r, c=c: pl.BlockSpec((1, r, step), lambda i: (starts[c] + i, 0, 0))
-            ins = [cols, pl.BlockSpec((width, step), lambda i, c=c: (0, starts[c] + i)), whole(weight)]
+            ins = [cols, vmem, whole(weight)]
             args = [part, output_weight, weight]
             ins += [cols] * len(others)
             args += others
@@ -546,7 +551,7 @@
                 out_specs += [whole(s) for s in sums]
             results = call(
                 functools.partial(
-                    finish_kernel, row_slice, len(others), matches is not None, merged is not None,
+                    finish_kernel, starts[c], row_slice, len(others), matches is not None, merged is not None,
                     bool(chain), errors is not None, tail if last else None, n_tail,
                 ),
                 outs,

time: 188 us -> 187 us (level)
  waiting for transfers between devices: 71.6 us -> 76.8 us
  Pallas kernels: 48.3 us -> 44.4 us
  starting transfers between devices: 58.4 us -> 55.7 us
    ppermute x35, starting transfers between devices: 40.9 us -> 36.4 us  [over_task(): return lax.ppermute(value, TASK, [(i, target(i)) for i in range(n_task)])]
    ppermute x14, waiting for transfers between devices: 15.8 us -> 20.1 us  [over_tensor(): lax.ppermute(value, TENSOR, [(i, (i + shift) % n_tensor) for i in range(n...]
    pallas_call x18, Pallas kernels: 31 us -> 27.6 us  [the longest x9 15.2 us: combine(): call(functools.partial(finish_kernel, starts[c], row_slice, len(others),...]
  transfers between devices with their start and end apart: 49 -> 49, of which waited for: 21 -> 21; matrix products, arithmetic and copies ran while one was open for 1% -> 1% of each run, Pallas kernels for 23% -> 22%
where the time goes in v4:
time: 187 us
  waiting for transfers between devices  76.8 us (41%)
  starting transfers between devices  55.7 us (30%)
  Pallas kernels  44.4 us (24%)
  local copies, waits for them, and re-layouts  5.55 us (3%)
  other arithmetic  2.26 us (1%)
    ppermute x35, waiting for transfers between devices, over_task(): return lax.ppermute(value, TASK, [(i, target(i)) for i in range(n_task)])  56.7 us
    ppermute x35, starting transfers between devices, over_task(): return lax.ppermute(value, TASK, [(i, target(i)) for i in range(n_task)])  36.4 us
    ppermute x14, waiting for transfers between devices, over_tensor(): lax.ppermute(value, TENSOR, [(i, (i + shift) % n_tensor) for i in range(n...  20.1 us
    ppermute x14, starting transfers between devices, over_tensor(): lax.ppermute(value, TENSOR, [(i, (i + shift) % n_tensor) for i in range(n...  19.3 us
    pallas_call x9, Pallas kernels, combine(): call(functools.partial(finish_kernel, starts[c], row_slice, len(others),...  15.2 us
    pallas_call x9, Pallas kernels, part_of(): call(functools.partial(part_kernel, begin, cross, offset), Shape((rows, s...  12.4 us
    unnamed x14, local copies, waits for them, and re-layouts  5.55 us
  transfers between devices with their start and end apart: 49, of which 21 were waited for; matrix products, arithmetic and copies ran while one was open for 1% of the time, Pallas kernels for 22%

profile of v4, /device:TPU:0, one launch (start us, length us, event | category | flops | bytes accessed | tf_op | source)
XLA Modules:
  0.0 186.6 jit_solution(3122853084873027930)
XLA Ops:
  0.8 3.0 %collective-permute-start = (bf16[128,2048]{1,0:T(8,128)(2,1)}, bf16[128,2048]{1,0:T(8,128)(2,1)S(1)}, u32[]{:S(2)}, u32[]{:S(2)}) collective-permute-start(bf16[128,2048]{1,0:T(8,128)(2,1)} %refs_5_.2), channel_id=1, source_target_pairs={{0,1},{1,0},{2,3},{3,2},{4,5},{5,4},{6,7},{7,6},{8,9},{9,8},{10,11... | collective-permute-start | bytes 1572872 | tf_op jit(solution)/shard_map/ppermute | solution.py:380
  4.4 3.4 %copy-done.1 = bf16[4096,1024]{1,0:T(8,128)(2,1)S(1)} copy-done((bf16[4096,1024]{1,0:T(8,128)(2,1)S(1)}, bf16[4096,1024]{1,0:T(8,128)(2,1)}, u32[]{:S(2)}) %copy-start.1) | copy-done | bytes 8388632
  11.2 2.1 %shard_map.87 = (f32[128,1024]{1,0:T(8,128)S(1)}, f32[128,1]{1,0:T(8,128)S(1)}) custom-call(s32[1]{0:T(128)} %bitcast.4.place_ref, bf16[128,2048]{1,0:T(8,128)(2,1)S(1)} %copy-done, bf16[4096,1024]{1,0:T(8,128)(2,1)S(1)} %copy-done.2), custom_call_target="tpu_custom_call" | custom-call | tf_op jit(solution)/shard_map/pallas_call | solution.py:460
  16.1 2.4 %shard_map.89 = (bf16[128,1024]{1,0:T(8,128)(2,1)S(1)}, bf16[128,1024]{1,0:T(8,128)(2,1)S(1)}, f32[128,1]{1,0:T(8,128)S(1)}) custom-call(s32[1]{0:T(128)} %bitcast.5.place_ref, bf16[128,2048]{1,0:T(8,128)(2,1)S(1)} %collective-permute-done.x_ref.refs_1_, bf16[2048,1024]{1,0:T(8,128)(2,1)S(1)} %shard_map.86.weight_ref, ...), custom_call_target="tpu_custom_call" | custom-call | tf_op jit(solution)/shard_map/pallas_call | solution.py:468
  29.8 2.9 %collective-permute-done.1.take_ref = bf16[4,64,512]{2,1,0:T(8,128)(2,1)S(1)} collective-permute-done((bf16[4,64,512]{2,1,0:T(8,128)(2,1)S(1)}, bf16[4,64,512]{2,1,0:T(8,128)(2,1)S(1)}, u32[]{:S(2)}, u32[]{:S(2)}) %collective-permute-start.1) | collective-permute-done | bytes 262176 | tf_op jit(solution)/shard_map/ppermute | solution.py:386
  34.3 5.0 %collective-permute-done.8.refs_3_ = bf16[96,1024]{1,0:T(8,128)(2,1)S(1)} collective-permute-done((bf16[96,1024]{1,0:T(8,128)(2,1)S(1)}, bf16[96,1024]{1,0:T(8,128)(2,1)S(1)}, u32[]{:S(2)}, u32[]{:S(2)}) %collective-permute-start.8) | collective-permute-done | bytes 196640 | tf_op jit(solution)/shard_map/ppermute | solution.py:380
  42.0 2.5 %shard_map.100 = (bf16[8,96,512]{2,1,0:T(8,128)(2,1)S(1)}, bf16[128,1024]{1,0:T(8,128)(2,1)S(1)}, bf16[96,1024]{1,0:T(8,128)(2,1)S(1)}, bf16[128,1024]{1,0:T(8,128)(2,1)S(1)}, bf16[96,96]{1,0:T(8,128)(2,1)S(1)}) custom-call(bf16[96,1536]{1,0:T(8,128)(2,1)S(1)} %shard_map.95.refs_0_, ...), custom_call_target="tpu_custom_call", output_to_operand_aliasing={{0}: (5, {})} | custom-call | tf_op jit(solution)/shard_map/pallas_call | solution.py:552
  54.6 2.6 %collective-permute-start.30 = (bf16[2,48,512]{2,1,0:T(8,128)(2,1)S(1)}, bf16[2,48,512]{2,1,0:T(8,128)(2,1)S(1)}, u32[]{:S(2)}, u32[]{:S(2)}) collective-permute-start(bf16[2,48,512]{2,1,0:T(8,128)(2,1)S(1)} %get-tuple-element.119), channel_id=1, source_target_pairs={{0,16},{2,18},{4,20},{6,22},{8,24},{10,26},{12,28},{14,30},{16,0},... | collective-permute-start | bytes 294920 | tf_op jit(solution)/shard_map/ppermute | solution.py:386
  59.4 4.3 %collective-permute-done.30.refs_2_ = bf16[2,48,512]{2,1,0:T(8,128)(2,1)S(1)} collective-permute-done((bf16[2,48,512]{2,1,0:T(8,128)(2,1)S(1)}, bf16[2,48,512]{2,1,0:T(8,128)(2,1)S(1)}, u32[]{:S(2)}, u32[]{:S(2)}) %collective-permute-start.30) | collective-permute-done | bytes 98336 | tf_op jit(solution)/shard_map/ppermute | solution.py:386
  69.6 3.4 %collective-permute-start.4 = (bf16[2,64,512]{2,1,0:T(8,128)(2,1)S(1)}, bf16[2,64,512]{2,1,0:T(8,128)(2,1)S(1)}, u32[]{:S(2)}, u32[]{:S(2)}) collective-permute-start(bf16[2,64,512]{2,1,0:T(8,128)(2,1)S(1)} %get-tuple-element.78), channel_id=1, source_target_pairs={{0,24},{2,26},{4,28},{6,30},{8,0},{10,2},{12,4},{14,6},{16,8},{18,... | collective-permute-start | bytes 393224 | tf_op jit(solution)/shard_map/ppermute | solution.py:386
  76.4 2.7 %shard_map.106 = (bf16[8,96,512]{2,1,0:T(8,128)(2,1)S(1)}, bf16[96,1024]{1,0:T(8,128)(2,1)S(1)}, f32[128,1024]{1,0:T(8,128)S(1)}) custom-call(bf16[96,1536]{1,0:T(8,128)(2,1)S(1)} %shard_map.101.refs_0_, bf16[1024,4096]{1,0:T(8,128)(2,1)S(1)} %shard_map.94.refs_1_, f32[128,1]{1,0:T(8,128)S(1)} %get-tuple-element.92.refs_2_, ...), custom_call_target="tpu_custom_call", output_to_operand_aliasing={{0}: (7, {})} | custom-call | tf_op jit(solution)/shard_map/pallas_call | solution.py:552
  86.6 7.7 %collective-permute-done.14.refs_3_ = bf16[96,1024]{1,0:T(8,128)(2,1)S(1)} collective-permute-done((bf16[96,1024]{1,0:T(8,128)(2,1)S(1)}, bf16[96,1024]{1,0:T(8,128)(2,1)S(1)}, u32[]{:S(2)}, u32[]{:S(2)}) %collective-permute-start.14) | collective-permute-done | bytes 196640 | tf_op jit(solution)/shard_map/ppermute | solution.py:380
  103.0 2.2 %collective-permute-done.35.refs_8_ = bf16[128,1024]{1,0:T(8,128)(2,1)S(1)} collective-permute-done((bf16[128,1024]{1,0:T(8,128)(2,1)S(1)}, bf16[128,1024]{1,0:T(8,128)(2,1)S(1)}, u32[]{:S(2)}, u32[]{:S(2)}) %collective-permute-start.35) | collective-permute-done | bytes 262176 | tf_op jit(solution)/shard_map/ppermute | solution.py:386
  113.6 8.9 %collective-permute-done.24.refs_2_ = bf16[2,64,512]{2,1,0:T(8,128)(2,1)S(1)} collective-permute-done((bf16[2,64,512]{2,1,0:T(8,128)(2,1)S(1)}, bf16[2,64,512]{2,1,0:T(8,128)(2,1)S(1)}, u32[]{:S(2)}, u32[]{:S(2)}) %collective-permute-start.24) | collective-permute-done | bytes 131104 | tf_op jit(solution)/shard_map/ppermute | solution.py:386
  126.7 2.6 %collective-permute-start.5 = (bf16[8,64,512]{2,1,0:T(8,128)(2,1)S(1)}, bf16[8,64,512]{2,1,0:T(8,128)(2,1)S(1)}, u32[]{:S(2)}, u32[]{:S(2)}) collective-permute-start(bf16[8,64,512]{2,1,0:T(8,128)(2,1)S(1)} %shard_map.93.refs_0_), channel_id=1, source_target_pairs={{0,1},{1,0},{2,3},{3,2},{4,5},{5,4},{6,7},{7,6},{8,9},{9,8},{10,11... | collective-permute-start | bytes 1572872 | tf_op jit(solution)/shard_map/ppermute | solution.py:380
  134.3 2.5 %collective-permute-start.28 = (bf16[4,64,512]{2,1,0:T(8,128)(2,1)S(1)}, bf16[4,64,512]{2,1,0:T(8,128)(2,1)S(1)}, u32[]{:S(2)}, u32[]{:S(2)}) collective-permute-start(bf16[4,64,512]{2,1,0:T(8,128)(2,1)S(1)} %collective-permute-done.27.refs_2_), channel_id=1, source_target_pairs={{0,1},{1,0},{2,3},{3,2},{4,5},{5,4},{6,7},{7,6},{8,9},{9,8},{10,11... | collective-permute-start | bytes 786440 | tf_op jit(solution)/shard_map/ppermute | solution.py:380
  136.8 4.5 %collective-permute-done.46.refs_20_ = bf16[96,1024]{1,0:T(8,128)(2,1)S(1)} collective-permute-done((bf16[96,1024]{1,0:T(8,128)(2,1)S(1)}, bf16[96,1024]{1,0:T(8,128)(2,1)S(1)}, u32[]{:S(2)}, u32[]{:S(2)}) %collective-permute-start.46) | collective-permute-done | bytes 196640 | tf_op jit(solution)/shard_map/ppermute | solution.py:386
  141.3 6.3 %collective-permute-done.26.refs_1_ = bf16[4,64,512]{2,1,0:T(8,128)(2,1)S(1)} collective-permute-done((bf16[4,64,512]{2,1,0:T(8,128)(2,1)S(1)}, bf16[4,64,512]{2,1,0:T(8,128)(2,1)S(1)}, u32[]{:S(2)}, u32[]{:S(2)}) %collective-permute-start.26) | collective-permute-done | bytes 262176 | tf_op jit(solution)/shard_map/ppermute | solution.py:380
  148.2 5.1 %collective-permute-done.47.refs_21_ = bf16[96,1024]{1,0:T(8,128)(2,1)S(1)} collective-permute-done((bf16[96,1024]{1,0:T(8,128)(2,1)S(1)}, bf16[96,1024]{1,0:T(8,128)(2,1)S(1)}, u32[]{:S(2)}, u32[]{:S(2)}) %collective-permute-start.47) | collective-permute-done | bytes 196640 | tf_op jit(solution)/shard_map/ppermute | solution.py:386
  153.3 2.7 %shard_map.119 = (f32[1024,256]{1,0:T(8,128)S(1)}, bf16[1024,256]{1,0:T(8,128)(2,1)S(1)}) custom-call(s32[4]{0:T(128)S(1)} %pad_add_fusion.ids_ref.refs_2_.refs_4_, bf16[4,64,512]{2,1,0:T(8,128)(2,1)S(1)} %get-tuple-element.115.refs_0_, bf16[4,64,512]{2,1,0:T(8,128)(2,1)S(1)} %collective-permute-done.26.refs_1_, ...), custom_call_target="tpu_custom_call" | custom-call | tf_op jit(solution)/shard_map/pallas_call | solution.py:611
  160.2 5.1 %collective-permute-done.18.refs_6_ = bf16[128,1024]{1,0:T(8,128)(2,1)S(1)} collective-permute-done((bf16[128,1024]{1,0:T(8,128)(2,1)S(1)}, bf16[128,1024]{1,0:T(8,128)(2,1)S(1)}, u32[]{:S(2)}, u32[]{:S(2)}) %collective-permute-start.18) | collective-permute-done | bytes 262176 | tf_op jit(solution)/shard_map/ppermute | solution.py:386
  165.3 5.6 %collective-permute-done.19.refs_7_ = bf16[128,1024]{1,0:T(8,128)(2,1)S(1)} collective-permute-done((bf16[128,1024]{1,0:T(8,128)(2,1)S(1)}, bf16[128,1024]{1,0:T(8,128)(2,1)S(1)}, u32[]{:S(2)}, u32[]{:S(2)}) %collective-permute-start.19) | collective-permute-done | bytes 262176 | tf_op jit(solution)/shard_map/ppermute | solution.py:386
  170.9 5.6 %collective-permute-done.21.refs_9_ = bf16[128,1024]{1,0:T(8,128)(2,1)S(1)} collective-permute-done((bf16[128,1024]{1,0:T(8,128)(2,1)S(1)}, bf16[128,1024]{1,0:T(8,128)(2,1)S(1)}, u32[]{:S(2)}, u32[]{:S(2)}) %collective-permute-start.21) | collective-permute-done | bytes 262176 | tf_op jit(solution)/shard_map/ppermute | solution.py:386
  176.5 5.1 %collective-permute-done.20.refs_8_ = bf16[128,1024]{1,0:T(8,128)(2,1)S(1)} collective-permute-done((bf16[128,1024]{1,0:T(8,128)(2,1)S(1)}, bf16[128,1024]{1,0:T(8,128)(2,1)S(1)}, u32[]{:S(2)}, u32[]{:S(2)}) %collective-permute-start.20) | collective-permute-done | bytes 262176 | tf_op jit(solution)/shard_map/ppermute | solution.py:386
  (125 shorter events, 86.7 us)
Async XLA Ops:
  0.8 15.3 %collective-permute-start = (bf16[128,2048]{1,0:T(8,128)(2,1)}, bf16[128,2048]{1,0:T(8,128)(2,1)S(1)}, u32[]{:S(2)}, u32[]{:S(2)}) collective-permute-start(bf16[128,2048]{1,0:T(8,128)(2,1)} %refs_5_.2), channel_id=1, source_target_pairs={{0,1},{1,0},{2,3},{3,2},{4,5},{5,4},{6,7},{7,6},{8,9},{9,8},{10,11... | collective-permute-start | bytes 1572872 | tf_op jit(solution)/shard_map/ppermute | solution.py:380
  20.2 20.1 %collective-permute-start.7 = (bf16[96,1536]{1,0:T(8,128)(2,1)S(1)}, bf16[96,1536]{1,0:T(8,128)(2,1)S(1)}, u32[]{:S(2)}, u32[]{:S(2)}) collective-permute-start(bf16[96,1536]{1,0:T(8,128)(2,1)S(1)} %shard_map.96.refs_0_), channel_id=1, source_target_pairs={{0,1},{1,0},{2,3},{3,2},{4,5},{5,4},{6,7},{7,6},{8,9},{9,8},{10,11... | collective-permute-start | bytes 884744 | tf_op jit(solution)/shard_map/ppermute | solution.py:380
  23.5 18.5 %collective-permute-start.6 = (bf16[96,1536]{1,0:T(8,128)(2,1)S(1)}, bf16[96,1536]{1,0:T(8,128)(2,1)S(1)}, u32[]{:S(2)}, u32[]{:S(2)}) collective-permute-start(bf16[96,1536]{1,0:T(8,128)(2,1)S(1)} %shard_map.95.refs_0_), channel_id=1, source_target_pairs={{0,1},{1,0},{2,3},{3,2},{4,5},{5,4},{6,7},{7,6},{8,9},{9,8},{10,11... | collective-permute-start | bytes 884744 | tf_op jit(solution)/shard_map/ppermute | solution.py:380
  32.7 21.9 %collective-permute-start.2 = (bf16[2,64,512]{2,1,0:T(8,128)(2,1)S(1)}, bf16[2,64,512]{2,1,0:T(8,128)(2,1)S(1)}, u32[]{:S(2)}, u32[]{:S(2)}) collective-permute-start(bf16[2,64,512]{2,1,0:T(8,128)(2,1)S(1)} %get-tuple-element.76), channel_id=1, source_target_pairs={{0,8},{2,10},{4,12},{6,14},{8,16},{10,18},{12,20},{14,22},{16,24},... | collective-permute-start | bytes 393224 | tf_op jit(solution)/shard_map/ppermute | solution.py:386
  46.2 23.5 %collective-permute-start.10 = (bf16[96,1536]{1,0:T(8,128)(2,1)S(1)}, bf16[96,1536]{1,0:T(8,128)(2,1)S(1)}, u32[]{:S(2)}, u32[]{:S(2)}) collective-permute-start(bf16[96,1536]{1,0:T(8,128)(2,1)S(1)} %shard_map.102.refs_0_), channel_id=1, source_target_pairs={{0,1},{1,0},{2,3},{3,2},{4,5},{5,4},{6,7},{7,6},{8,9},{9,8},{10,11... | collective-permute-start | bytes 884744 | tf_op jit(solution)/shard_map/ppermute | solution.py:380
  48.9 24.1 %collective-permute-start.9 = (bf16[96,1536]{1,0:T(8,128)(2,1)S(1)}, bf16[96,1536]{1,0:T(8,128)(2,1)S(1)}, u32[]{:S(2)}, u32[]{:S(2)}) collective-permute-start(bf16[96,1536]{1,0:T(8,128)(2,1)S(1)} %shard_map.101.refs_0_), channel_id=1, source_target_pairs={{0,1},{1,0},{2,3},{3,2},{4,5},{5,4},{6,7},{7,6},{8,9},{9,8},{10,11... | collective-permute-start | bytes 884744 | tf_op jit(solution)/shard_map/ppermute | solution.py:380
  53.6 14.5 %collective-permute-start.11 = (bf16[96,1024]{1,0:T(8,128)(2,1)S(1)}, bf16[96,1024]{1,0:T(8,128)(2,1)S(1)}, u32[]{:S(2)}, u32[]{:S(2)}) collective-permute-start(bf16[96,1024]{1,0:T(8,128)(2,1)S(1)} %shard_map.103.refs_0_), channel_id=1, source_target_pairs={{0,1},{1,0},{2,3},{3,2},{4,5},{5,4},{6,7},{7,6},{8,9},{9,8},{10,11... | collective-permute-start | bytes 589832 | tf_op jit(solution)/shard_map/ppermute | solution.py:380
  63.7 20.7 %collective-permute-start.34 = (bf16[128,1024]{1,0:T(8,128)(2,1)S(1)}, bf16[128,1024]{1,0:T(8,128)(2,1)S(1)}, u32[]{:S(2)}, u32[]{:S(2)}) collective-permute-start(bf16[128,1024]{1,0:T(8,128)(2,1)S(1)} %get-tuple-element.123.refs_6_), channel_id=1, source_target_pairs={{0,8},{2,10},{4,12},{6,14},{8,16},{10,18},{12,20},{14,22},{16,24},... | collective-permute-start | bytes 786440 | tf_op jit(solution)/shard_map/ppermute | solution.py:386
  65.8 14.5 %collective-permute-start.3 = (bf16[2,64,512]{2,1,0:T(8,128)(2,1)S(1)}, bf16[2,64,512]{2,1,0:T(8,128)(2,1)S(1)}, u32[]{:S(2)}, u32[]{:S(2)}) collective-permute-start(bf16[2,64,512]{2,1,0:T(8,128)(2,1)S(1)} %get-tuple-element.77), channel_id=1, source_target_pairs={{0,16},{2,18},{4,20},{6,22},{8,24},{10,26},{12,28},{14,30},{16,0},... | collective-permute-start | bytes 393224 | tf_op jit(solution)/shard_map/ppermute | solution.py:386
  68.1 16.4 %collective-permute-start.32 = (bf16[4,48,512]{2,1,0:T(8,128)(2,1)S(1)}, bf16[4,48,512]{2,1,0:T(8,128)(2,1)S(1)}, u32[]{:S(2)}, u32[]{:S(2)}) collective-permute-start(bf16[4,48,512]{2,1,0:T(8,128)(2,1)S(1)} %get-tuple-element.122), channel_id=1, source_target_pairs={{0,4},{2,6},{4,0},{6,2},{8,12},{10,14},{12,8},{14,10},{16,20},{18,... | collective-permute-start | bytes 589832 | tf_op jit(solution)/shard_map/ppermute | solution.py:386
  80.2 15.5 %collective-permute-start.13 = (bf16[96,1536]{1,0:T(8,128)(2,1)S(1)}, bf16[96,1536]{1,0:T(8,128)(2,1)S(1)}, u32[]{:S(2)}, u32[]{:S(2)}) collective-permute-start(bf16[96,1536]{1,0:T(8,128)(2,1)S(1)} %shard_map.108.refs_0_), channel_id=1, source_target_pairs={{0,1},{1,0},{2,3},{3,2},{4,5},{5,4},{6,7},{7,6},{8,9},{9,8},{10,11... | collective-permute-start | bytes 884744 | tf_op jit(solution)/shard_map/ppermute | solution.py:380
  84.6 24.4 %collective-permute-start.33 = (bf16[8,48,512]{2,1,0:T(8,128)(2,1)S(1)}, bf16[8,48,512]{2,1,0:T(8,128)(2,1)S(1)}, u32[]{:S(2)}, u32[]{:S(2)}) collective-permute-start(bf16[8,48,512]{2,1,0:T(8,128)(2,1)S(1)} %shard_map.118.refs_4_), channel_id=1, source_target_pairs={{0,1},{1,0},{2,3},{3,2},{4,5},{5,4},{6,7},{7,6},{8,9},{9,8},{10,11... | collective-permute-start | bytes 1179656 | tf_op jit(solution)/shard_map/ppermute | solution.py:380
  105.1 17.4 %collective-permute-start.24 = (bf16[2,64,512]{2,1,0:T(8,128)(2,1)S(1)}, bf16[2,64,512]{2,1,0:T(8,128)(2,1)S(1)}, u32[]{:S(2)}, u32[]{:S(2)}) collective-permute-start(bf16[2,64,512]{2,1,0:T(8,128)(2,1)S(1)} %get-tuple-element.113), channel_id=1, source_target_pairs={{0,16},{2,18},{4,20},{6,22},{8,24},{10,26},{12,28},{14,30},{16,0},... | collective-permute-start | bytes 393224 | tf_op jit(solution)/shard_map/ppermute | solution.py:386
  107.2 15.3 %collective-permute-start.25 = (bf16[2,64,512]{2,1,0:T(8,128)(2,1)S(1)}, bf16[2,64,512]{2,1,0:T(8,128)(2,1)S(1)}, u32[]{:S(2)}, u32[]{:S(2)}) collective-permute-start(bf16[2,64,512]{2,1,0:T(8,128)(2,1)S(1)} %get-tuple-element.114), channel_id=1, source_target_pairs={{0,24},{2,26},{4,28},{6,30},{8,0},{10,2},{12,4},{14,6},{16,8},{18,... | collective-permute-start | bytes 393224 | tf_op jit(solution)/shard_map/ppermute | solution.py:386
  109.0 17.7 %collective-permute-start.36 = (bf16[128,1024]{1,0:T(8,128)(2,1)S(1)}, bf16[128,1024]{1,0:T(8,128)(2,1)S(1)}, u32[]{:S(2)}, u32[]{:S(2)}) collective-permute-start(bf16[128,1024]{1,0:T(8,128)(2,1)S(1)} %collective-permute-done.35.refs_8_), channel_id=1, source_target_pairs={{0,8},{2,10},{4,12},{6,14},{8,16},{10,18},{12,20},{14,22},{16,24},... | collective-permute-start | bytes 786440 | tf_op jit(solution)/shard_map/ppermute | solution.py:386
  109.3 19.9 %collective-permute-start.39 = (bf16[128,1024]{1,0:T(8,128)(2,1)S(1)}, bf16[128,1024]{1,0:T(8,128)(2,1)S(1)}, u32[]{:S(2)}, u32[]{:S(2)}) collective-permute-start(bf16[128,1024]{1,0:T(8,128)(2,1)S(1)} %collective-permute-done.35.refs_8_), channel_id=1, source_target_pairs={{0,4},{2,6},{4,0},{6,2},{8,12},{10,14},{12,8},{14,10},{16,20},{18,... | collective-permute-start | bytes 786440 | tf_op jit(solution)/shard_map/ppermute | solution.py:386
  126.7 30.0 %collective-permute-start.5 = (bf16[8,64,512]{2,1,0:T(8,128)(2,1)S(1)}, bf16[8,64,512]{2,1,0:T(8,128)(2,1)S(1)}, u32[]{:S(2)}, u32[]{:S(2)}) collective-permute-start(bf16[8,64,512]{2,1,0:T(8,128)(2,1)S(1)} %shard_map.93.refs_0_), channel_id=1, source_target_pairs={{0,1},{1,0},{2,3},{3,2},{4,5},{5,4},{6,7},{7,6},{8,9},{9,8},{10,11... | collective-permute-start | bytes 1572872 | tf_op jit(solution)/shard_map/ppermute | solution.py:380
  129.3 18.3 %collective-permute-start.26 = (bf16[4,64,512]{2,1,0:T(8,128)(2,1)S(1)}, bf16[4,64,512]{2,1,0:T(8,128)(2,1)S(1)}, u32[]{:S(2)}, u32[]{:S(2)}) collective-permute-start(bf16[4,64,512]{2,1,0:T(8,128)(2,1)S(1)} %get-tuple-element.115.refs_0_), channel_id=1, source_target_pairs={{0,1},{1,0},{2,3},{3,2},{4,5},{5,4},{6,7},{7,6},{8,9},{9,8},{10,11... | collective-permute-start | bytes 786440 | tf_op jit(solution)/shard_map/ppermute | solution.py:380
  130.7 17.0 %collective-permute-start.40 = (bf16[128,1024]{1,0:T(8,128)(2,1)S(1)}, bf16[128,1024]{1,0:T(8,128)(2,1)S(1)}, u32[]{:S(2)}, u32[]{:S(2)}) collective-permute-start(bf16[128,1024]{1,0:T(8,128)(2,1)S(1)} %collective-permute-done.36.refs_9_), channel_id=1, source_target_pairs={{0,4},{2,6},{4,0},{6,2},{8,12},{10,14},{12,8},{14,10},{16,20},{18,... | collective-permute-start | bytes 786440 | tf_op jit(solution)/shard_map/ppermute | solution.py:386
  134.3 19.1 %collective-permute-start.28 = (bf16[4,64,512]{2,1,0:T(8,128)(2,1)S(1)}, bf16[4,64,512]{2,1,0:T(8,128)(2,1)S(1)}, u32[]{:S(2)}, u32[]{:S(2)}) collective-permute-start(bf16[4,64,512]{2,1,0:T(8,128)(2,1)S(1)} %collective-permute-done.27.refs_2_), channel_id=1, source_target_pairs={{0,1},{1,0},{2,3},{3,2},{4,5},{5,4},{6,7},{7,6},{8,9},{9,8},{10,11... | collective-permute-start | bytes 786440 | tf_op jit(solution)/shard_map/ppermute | solution.py:380
  141.3 16.8 %collective-permute-start.17 = (bf16[128,1024]{1,0:T(8,128)(2,1)S(1)}, bf16[128,1024]{1,0:T(8,128)(2,1)S(1)}, u32[]{:S(2)}, u32[]{:S(2)}) collective-permute-start(bf16[128,1024]{1,0:T(8,128)(2,1)S(1)} %get-tuple-element.107.refs_2_), channel_id=1, source_target_pairs={{0,24},{2,26},{4,28},{6,30},{8,0},{10,2},{12,4},{14,6},{16,8},{18,... | collective-permute-start | bytes 786440 | tf_op jit(solution)/shard_map/ppermute | solution.py:386
  156.0 27.6 %collective-permute-start.48 = (bf16[1024,256]{1,0:T(8,128)(2,1)S(1)}, bf16[1024,256]{1,0:T(8,128)(2,1)S(1)}, u32[]{:S(2)}, u32[]{:S(2)}) collective-permute-start(bf16[1024,256]{1,0:T(8,128)(2,1)S(1)} %get-tuple-element.125), channel_id=1, source_target_pairs={{0,2},{2,0},{4,6},{6,4},{8,10},{10,8},{12,14},{14,12},{16,18},{18,... | collective-permute-start | bytes 1572872 | tf_op jit(solution)/shard_map/ppermute | solution.py:386
  158.2 18.4 %collective-permute-start.21 = (bf16[128,1024]{1,0:T(8,128)(2,1)S(1)}, bf16[128,1024]{1,0:T(8,128)(2,1)S(1)}, u32[]{:S(2)}, u32[]{:S(2)}) collective-permute-start(bf16[128,1024]{1,0:T(8,128)(2,1)S(1)} %collective-permute-done.17.refs_5_), channel_id=1, source_target_pairs={{0,4},{2,6},{4,0},{6,2},{8,12},{10,14},{12,8},{14,10},{16,20},{18,... | collective-permute-start | bytes 786440 | tf_op jit(solution)/shard_map/ppermute | solution.py:386
  158.7 22.9 %collective-permute-start.20 = (bf16[128,1024]{1,0:T(8,128)(2,1)S(1)}, bf16[128,1024]{1,0:T(8,128)(2,1)S(1)}, u32[]{:S(2)}, u32[]{:S(2)}) collective-permute-start(bf16[128,1024]{1,0:T(8,128)(2,1)S(1)} %collective-permute-done.16.refs_4_), channel_id=1, source_target_pairs={{0,4},{2,6},{4,0},{6,2},{8,12},{10,14},{12,8},{14,10},{16,20},{18,... | collective-permute-start | bytes 786440 | tf_op jit(solution)/shard_map/ppermute | solution.py:386
  (32 other events, 275.1 us)
